TPU v7x, 512 devices: a whole 4x4x16 slice. The times are simulated.
512 devices in a mesh: gx: 4 (over x), gy: 8 (over y, core), gz: 16 (over z).
Axes of the slice: x: 4, y: 4, z: 16, core: 2. Of those that a mesh axis runs over, the one named last changes fastest.
Arguments:
- positions: float32 [3, 4, 8, 16, 128], P(None, 'gx', 'gy', 'gz'), may hold values from 0 to 1
- basis: float32 [30, 3, 4, 8, 16, 128], P(None, None, 'gx', 'gy', 'gz'), may hold values from -10 to 10, as said below
- neighbours: int32 [4, 8, 16, 128, 128], P('gx', 'gy', 'gz'), may hold values from 0 to 511
- used_count: int32 [4, 8, 16, 128], P('gx', 'gy', 'gz'), may hold values from 42 to 128
- kinds: int32 [4, 8, 16, 128], P('gx', 'gy', 'gz'), may hold values from 0 to 1
- map_x: int32 [4, 8, 16, 2, 64], P('gx', 'gy', 'gz'), may hold values from 0 to 127
- map_y: int32 [4, 8, 16, 2, 64], P('gx', 'gy', 'gz'), may hold values from 0 to 255
- map_z: int32 [4, 8, 16, 2, 64], P('gx', 'gy', 'gz'), may hold values from 0 to 383
- table: float32 [2, 16, 100], replicated, may hold values from -6 to 6
- fit_w1: float32 [1600, 240], replicated, may hold values from -0.15625 to 0.15625
- fit_b1: float32 [240], replicated, may hold values from -3 to 3
- fit_w2: float32 [240, 240], replicated, may hold values from -0.375 to 0.375
- fit_b2: float32 [240], replicated, may hold values from -3 to 3
- fit_out: float32 [240], replicated, may hold values from -0.375 to 0.375
Outputs:
- next_vector: float32 [3, 4, 8, 16, 128], P(None, 'gx', 'gy', 'gz')
- correlations: float32 [30], replicated
- vector_norm: float32 [], replicated
Inputs may be any that keep to these rules, and one draw needn't show every extreme that they name: `basis`: entries of order one; the stored vectors' magnitude varies from brick to brick.
All inputs are finite; a program needn't handle non-finite values.
Results may differ from a plain program's by a relative error of at most 0.0003.
Values sent between devices are 32-bit elements; how exact they have to be, the bound alone decides.
No kernel may reach another device: no remote copies, remote signals or barrier semaphores. Data moves between devices by JAX's collectives and lax.ppermute only.
A program may use at most 64 MiB of HBM per device.

v0:
```python
import functools

import jax
import jax.numpy as jnp
from jax import lax
from jax.sharding import Mesh
from jax.sharding import PartitionSpec as P

M2 = 16
GY = ("gy_0", "gy_1")
GX_GY_GZ = ("gx", "gy_0", "gy_1", "gz")


def over_pieces(x, axis):
    return lax.all_gather(x, axis).sum(0)


def with_halo(x, sides, width):
    for axis, dim in sides:
        peers, length = (lax.axis_size(axis), x.shape[dim])
        up = [(i, (i + 1) % peers) for i in range(peers)]
        down = [(j, i) for i, j in up]
        last = lax.slice_in_dim(x, length - width, length, axis=dim)
        leading = lax.slice_in_dim(x, 0, width, axis=dim)
        before = lax.ppermute(last, axis, up)
        after = lax.ppermute(leading, axis, down)
        x = jnp.concatenate([before, x, after], axis=dim)
    return x


def by_axis(x, axes):
    return functools.reduce(lax.psum, axes, x)


def site_energy(centre, beside_all, filled, onehot, table, fit_w1, fit_b1, fit_w2, fit_b2, fit_out):
    highest = lax.Precision.HIGHEST
    offsets = beside_all - centre[:, :, None]
    square = jnp.sum(offsets * offsets, axis=0)
    radius = jnp.sqrt(square + 0.01)
    smooth = jnp.exp(-square) / radius * filled
    radial = jnp.concatenate([smooth[None], smooth[None] * offsets / radius[None]], axis=0)
    scaled = smooth / (1.0 + smooth)
    levels = table.shape[1]
    centres = jnp.arange(levels, dtype=jnp.float32) / (levels - 1)
    spread = (scaled[:, None, :] - centres[None, :, None]) * (levels - 1)
    profile = jnp.exp(-spread * spread)
    pooled = jnp.einsum("bkn,abn->bka", profile, radial, precision=highest) / beside_all.shape[2]
    tables = jnp.einsum("bt,tkm->bkm", onehot, table, precision=highest)
    environment = jnp.einsum("bkm,bka->bma", tables, pooled, precision=highest)
    descriptor = jnp.einsum("bma,bna->bmn", environment, environment[:, :M2], precision=highest)
    descriptor = descriptor.reshape(descriptor.shape[0], -1)
    first_layer = jnp.tanh(jnp.dot(descriptor, fit_w1, precision=highest) + fit_b1)
    second_layer = jnp.tanh(jnp.dot(first_layer, fit_w2, precision=highest) + fit_b2) + first_layer
    return jnp.sum(jnp.dot(second_layer, fit_out, precision=highest))


def device_hvp(ext_places, ext_tangent, neighbour_ids, counts, species, weights):
    highest = lax.Precision.HIGHEST
    atom_count, width = neighbour_ids.shape
    extended = ext_places.shape[1]
    block_rows = min(atom_count, 32)
    slots = jnp.arange(width, dtype=jnp.int32)
    columns = jnp.arange(extended, dtype=jnp.int32)
    type_ids = jnp.arange(weights[0].shape[0], dtype=jnp.int32)
    both_fields = jnp.concatenate([ext_places, ext_tangent], axis=0)

    def one_block(counter, summed):
        offset = (counter * block_rows).astype(jnp.int32)
        block_ids = lax.dynamic_slice_in_dim(neighbour_ids, offset, block_rows, 0)
        block_counts = lax.dynamic_slice_in_dim(counts, offset, block_rows, 0)
        block_species = lax.dynamic_slice_in_dim(species, offset, block_rows, 0)
        filled = (slots[None, :] < block_counts[:, None]).astype(jnp.float32)
        onehot = (block_species[:, None] == type_ids[None, :]).astype(jnp.float32)
        selector = (block_ids.reshape(-1)[:, None] == columns[None, :]).astype(jnp.float32)
        picked = jnp.einsum("ce,se->cs", both_fields, selector, precision=highest)
        beside_all = picked[:3].reshape(3, block_rows, width)
        around_tangent = picked[3:].reshape(3, block_rows, width)
        centre = lax.dynamic_slice_in_dim(ext_places, offset, block_rows, 1)
        centre_tangent = lax.dynamic_slice_in_dim(ext_tangent, offset, block_rows, 1)

        def energy(middle, nearby):
            return site_energy(middle, nearby, filled, onehot, *weights)

        def gradient(middle, nearby):
            return jax.grad(energy, argnums=(0, 1))(middle, nearby)

        centre_term, around_term = jax.jvp(
            gradient, (centre, beside_all), (centre_tangent, around_tangent)
        )[1]
        spread_back = jnp.dot(around_term.reshape(3, -1), selector, precision=highest)
        summed = summed + spread_back
        owned = lax.dynamic_slice_in_dim(summed, offset, block_rows, 1) + centre_term
        return lax.dynamic_update_slice_in_dim(summed, owned, offset, 1)

    zeros = jnp.zeros(ext_places.shape, jnp.float32)
    return lax.fori_loop(0, atom_count // block_rows, one_block, zeros)


def outgoing(stacked, maps):
    return jnp.concatenate([stacked[:, :, maps[0]], stacked[:, :, maps[1]]], axis=2)


def attach(stacked, received, ghosts, coord):
    displace = (jnp.arange(3) == coord).astype(jnp.float32)
    displace = jnp.stack([displace, jnp.zeros_like(displace)])[:, :, None]
    return jnp.concatenate(
        [stacked, received[:, :, :ghosts] - displace, received[:, :, -ghosts:] + displace], axis=2
    )


def fold_back(holder, received, maps, ghosts):
    holder = holder.at[:, maps[0]].add(received[:, :ghosts])
    return holder.at[:, maps[1]].add(received[:, -ghosts:])


def on_device(
    positions,
    basis,
    neighbours,
    used_count,
    kinds,
    map_x,
    map_y,
    map_z,
    table,
    fit_w1,
    fit_b1,
    fit_w2,
    fit_b2,
    fit_out,
):
    highest = lax.Precision.HIGHEST
    atom_count = positions.shape[-1]
    places = positions.reshape(3, atom_count)
    vectors = basis.reshape(basis.shape[0], 3, atom_count)
    entries = 3 * atom_count * lax.axis_size("gx") * lax.axis_size(GY) * lax.axis_size("gz")
    gram_local = jnp.einsum("kca,lca->kl", vectors, vectors, precision=highest)
    gram_matrix = over_pieces(gram_local, GX_GY_GZ) / entries
    maps_x = map_x.reshape(2, -1)
    maps_y = map_y.reshape(2, -1)
    maps_z = map_z.reshape(2, -1)
    ghosts = maps_x.shape[1]
    stacked = jnp.stack([places, vectors[-1]])
    received = with_halo(outgoing(stacked, maps_x), (("gx", 2),), ghosts)
    stacked = attach(stacked, received, ghosts, 0)
    received = with_halo(outgoing(stacked, maps_y), ((GY, 2),), ghosts)
    stacked = attach(stacked, received, ghosts, 1)
    received = with_halo(outgoing(stacked, maps_z), (("gz", 2),), ghosts)
    stacked = attach(stacked, received, ghosts, 2)
    weights = (table, fit_w1, fit_b1, fit_w2, fit_b2, fit_out)
    products = device_hvp(
        stacked[0],
        stacked[1],
        neighbours.reshape(atom_count, -1),
        used_count.reshape(atom_count),
        kinds.reshape(atom_count),
        weights,
    )
    current = atom_count + 4 * ghosts
    returned = with_halo(products[:, current:], (("gz", 1),), ghosts)
    products = fold_back(products[:, :current], returned, maps_z, ghosts)
    current = atom_count + 2 * ghosts
    returned = with_halo(products[:, current:], ((GY, 1),), ghosts)
    products = fold_back(products[:, :current], returned, maps_y, ghosts)
    current = atom_count
    returned = with_halo(products[:, current:], (("gx", 1),), ghosts)
    hessian_vec = fold_back(products[:, :current], returned, maps_x, ghosts)
    local_correlation = jnp.einsum("kca,ca->k", vectors, hessian_vec, precision=highest)
    correlations, plain_square = (
        by_axis(local_correlation, GX_GY_GZ),
        by_axis(jnp.sum(hessian_vec * hessian_vec), GX_GY_GZ),
    )
    correlations = correlations / entries
    plain_square = plain_square / entries
    residual = hessian_vec - jnp.einsum("k,kca->ca", correlations, vectors, precision=highest)
    quadratic = jnp.dot(
        correlations, jnp.dot(gram_matrix, correlations, precision=highest), precision=highest
    )
    square_mean = (
        plain_square - 2.0 * jnp.dot(correlations, correlations, precision=highest) + quadratic
    )
    vector_norm = jnp.sqrt(square_mean + 1e-06)
    next_vector = (residual / vector_norm).reshape(positions.shape)
    return (next_vector, correlations, vector_norm)


def solution(mesh):
    torus = Mesh(
        mesh.devices.reshape(mesh.shape["gx"], 4, 2, mesh.shape["gz"]), ("gx", "gy_0", "gy_1", "gz")
    )
    placed = (
        P(None, "gx", GY, "gz", None),
        P(None, None, "gx", GY, "gz", None),
        P("gx", GY, "gz", None, None),
        P("gx", GY, "gz", None),
        P("gx", GY, "gz", None),
        P("gx", GY, "gz", None, None),
        P("gx", GY, "gz", None, None),
        P("gx", GY, "gz", None, None),
        P(),
        P(),
        P(),
        P(),
        P(),
        P(),
    )
    return jax.shard_map(
        on_device,
        mesh=torus,
        in_specs=placed,
        out_specs=(P(None, "gx", GY, "gz", None), P(), P()),
        check_vma=False,
    )
```

profile of v0, /device:TPU:8, one launch (start us, length us, event | category | flops | bytes accessed | tf_op | source)
XLA Modules:
  0.0 330.9 jit_solution(17714793216860241665)
XLA Ops:
  7.3 1.7 convolution_bitcast_fusion
  12.1 3.4 %collective-permute-start = (f32[2,3,64]{1,0,2:T(2,128)S(1)}, f32[2,3,64]{1,0,2:T(2,128)S(1)}, u32[]{:S(2)}, u32[]{:S(2)}) collective-permute-start(f32[2,3,64]{1,0,2:T(2,128)S(1)} %bitcast.521), channel_id=1, source_target_pairs={{0,128},{128,256},{256,384},{384,0},{1,129},{129,257},{257,385},{3... | collective-permute-start | bytes 4616 | tf_op jit(solution)/shard_map/ppermute | solution.py:25
  16.2 3.7 %collective-permute-start.1 = (f32[2,3,64]{1,0,2:T(2,128)S(1)}, f32[2,3,64]{1,0,2:T(2,128)S(1)}, u32[]{:S(2)}, u32[]{:S(2)}) collective-permute-start(f32[2,3,64]{1,0,2:T(2,128)S(1)} %bitcast.520), channel_id=1, source_target_pairs={{128,0},{256,128},{384,256},{0,384},{129,1},{257,129},{385,257},{1... | collective-permute-start | bytes 4616 | tf_op jit(solution)/shard_map/ppermute | solution.py:26
  23.9 1.7 collective-permute-start.3
  25.6 1.3 collective-permute-done.2
  28.9 11.4 %collective-permute-start.5 = (f32[2,3,64]{1,0,2:T(2,128)S(1)}, f32[2,3,64]{1,0,2:T(2,128)S(1)}, u32[]{:S(2)}, u32[]{:S(2)}) collective-permute-start(f32[2,3,64]{1,0,2:T(2,128)S(1)} %bitcast.523), channel_id=1, source_target_pairs={{1,0},{2,1},{3,2},{4,3},{5,4},{6,5},{7,6},{8,7},{9,8},{10,9},{11,1... | collective-permute-start | bytes 4616 | tf_op jit(solution)/shard_map/ppermute | solution.py:26
  40.3 1.9 collective-permute-start.4
  42.6 5.3 %collective-permute-done.4 = f32[2,3,64]{1,0,2:T(2,128)S(1)} collective-permute-done((f32[2,3,64]{1,0,2:T(2,128)S(1)}, f32[2,3,64]{1,0,2:T(2,128)S(1)}, u32[]{:S(2)}, u32[]{:S(2)}) %collective-permute-start.4) | collective-permute-done | bytes 1568 | tf_op jit(solution)/shard_map/ppermute | solution.py:25
  49.5 180.2 %while.15 = (s32[]{:T(128)}, f32[3,512]{1,0:T(4,128)}, s32[128]{0:T(128)S(1)}, s32[128,128]{1,0:T(8,128)}, f32[6,512]{1,0:T(8,128)}, /*index=5*/f32[3,512]{1,0:T...) while((s32[]{:T(128)}, f32[3,512]{1,0:T(4,128)}, ...), condition=%wide.region_10.11_spmd.clone.clone, body=%wide.region_0.10_spmd.clone.clone.sunk | while | flops 976472256 | bytes 24909864 | solution.py:96
  50.6 4.5 %fusion.396 = f32[6,4096]{1,0:T(8,128)S(1)} fusion(f32[6,512]{1,0:T(8,128)} %get-tuple-element.738, s32[4096]{0:T(1024)S(1)} %dynamic-slice_bitcast_fusion.2), kind=kOutput, calls=%fused_computation.18.clone.1 | convolution fusion | flops 153092096 | bytes 126976 | tf_op jit(solution)/shard_map/while/body/eval_jaxpr/ce,se->cs/dot_general | solution.py:75
  62.7 2.3 fusion.402
  66.0 1.6 convolution_multiply_fusion.12
  68.2 2.9 fusion.404
  73.2 1.1 fusion.407
  76.1 2.0 fusion.420
  78.1 2.8 fusion.414
  82.5 1.4 convolution_add_fusion.16
  83.8 1.2 fusion.417
  88.3 4.0 %fusion.425 = f32[3,512]{1,0:T(4,128)} fusion(f32[3,512]{1,0:T(4,128)} %get-tuple-element.716, s32[4096]{0:T(1024)S(1)} %copy-done.39, f32[1,3,32,128]{3,2,1,0:T(8,128)S(1)} %bitcast.505), kind=kOutput, calls=%fused_computation.45.clone.1 | convolution fusion | flops 77596160 | bytes 77824 | tf_op jit(solution)/shard_map/while/body/eval_jaxpr/dot_general | solution.py:90
  93.1 1.3 dynamic_update_slice.10
  95.6 4.5 %fusion.396 = f32[6,4096]{1,0:T(8,128)S(1)} fusion(f32[6,512]{1,0:T(8,128)} %get-tuple-element.738, s32[4096]{0:T(1024)S(1)} %dynamic-slice_bitcast_fusion.2), kind=kOutput, calls=%fused_computation.18.clone.1 | convolution fusion | flops 153092096 | bytes 126976 | tf_op jit(solution)/shard_map/while/body/eval_jaxpr/ce,se->cs/dot_general | solution.py:75
  107.6 2.3 fusion.402
  111.0 1.6 convolution_multiply_fusion.12
  113.1 2.9 fusion.404
  118.1 1.1 fusion.407
  121.0 2.0 fusion.420
  123.0 2.8 fusion.414
  127.4 1.4 convolution_add_fusion.16
  128.8 1.2 fusion.417
  133.3 4.0 %fusion.425 = f32[3,512]{1,0:T(4,128)} fusion(f32[3,512]{1,0:T(4,128)} %get-tuple-element.716, s32[4096]{0:T(1024)S(1)} %copy-done.39, f32[1,3,32,128]{3,2,1,0:T(8,128)S(1)} %bitcast.505), kind=kOutput, calls=%fused_computation.45.clone.1 | convolution fusion | flops 77596160 | bytes 77824 | tf_op jit(solution)/shard_map/while/body/eval_jaxpr/dot_general | solution.py:90
  138.0 1.4 dynamic_update_slice.10
  140.6 4.5 %fusion.396 = f32[6,4096]{1,0:T(8,128)S(1)} fusion(f32[6,512]{1,0:T(8,128)} %get-tuple-element.738, s32[4096]{0:T(1024)S(1)} %dynamic-slice_bitcast_fusion.2), kind=kOutput, calls=%fused_computation.18.clone.1 | convolution fusion | flops 153092096 | bytes 126976 | tf_op jit(solution)/shard_map/while/body/eval_jaxpr/ce,se->cs/dot_general | solution.py:75
  152.7 2.3 fusion.402
  156.0 1.6 convolution_multiply_fusion.12
  158.2 2.9 fusion.404
  163.1 1.1 fusion.407
  166.1 2.0 fusion.420
  168.1 2.8 fusion.414
  172.4 1.4 convolution_add_fusion.16
  173.8 1.2 fusion.417
  178.3 4.0 %fusion.425 = f32[3,512]{1,0:T(4,128)} fusion(f32[3,512]{1,0:T(4,128)} %get-tuple-element.716, s32[4096]{0:T(1024)S(1)} %copy-done.39, f32[1,3,32,128]{3,2,1,0:T(8,128)S(1)} %bitcast.505), kind=kOutput, calls=%fused_computation.45.clone.1 | convolution fusion | flops 77596160 | bytes 77824 | tf_op jit(solution)/shard_map/while/body/eval_jaxpr/dot_general | solution.py:90
  183.1 1.4 dynamic_update_slice.10
  185.7 4.5 %fusion.396 = f32[6,4096]{1,0:T(8,128)S(1)} fusion(f32[6,512]{1,0:T(8,128)} %get-tuple-element.738, s32[4096]{0:T(1024)S(1)} %dynamic-slice_bitcast_fusion.2), kind=kOutput, calls=%fused_computation.18.clone.1 | convolution fusion | flops 153092096 | bytes 126976 | tf_op jit(solution)/shard_map/while/body/eval_jaxpr/ce,se->cs/dot_general | solution.py:75
  197.7 2.3 fusion.402
  201.1 1.6 convolution_multiply_fusion.12
  203.2 2.9 fusion.404
  208.2 1.1 fusion.407
  211.1 2.0 fusion.420
  213.1 2.8 fusion.414
  217.5 1.4 convolution_add_fusion.16
  218.9 1.2 fusion.417
  223.4 4.0 %fusion.425 = f32[3,512]{1,0:T(4,128)} fusion(f32[3,512]{1,0:T(4,128)} %get-tuple-element.716, s32[4096]{0:T(1024)S(1)} %copy-done.39, f32[1,3,32,128]{3,2,1,0:T(8,128)S(1)} %bitcast.505), kind=kOutput, calls=%fused_computation.45.clone.1 | convolution fusion | flops 77596160 | bytes 77824 | tf_op jit(solution)/shard_map/while/body/eval_jaxpr/dot_general | solution.py:90
  228.1 1.4 dynamic_update_slice.10
  230.6 1.9 collective-permute-start.6
  232.5 5.1 %collective-permute-start.7 = (f32[3,64]{1,0:T(4,128)S(1)}, f32[3,64]{1,0:T(4,128)S(1)}, u32[]{:S(2)}, u32[]{:S(2)}) collective-permute-start(f32[3,64]{1,0:T(4,128)S(1)} %get-tuple-element.537), channel_id=1, source_target_pairs={{1,0},{2,1},{3,2},{4,3},{5,4},{6,5},{7,6},{8,7},{9,8},{10,9},{11,1... | collective-permute-start | bytes 2312 | tf_op jit(solution)/shard_map/ppermute | solution.py:26
  241.3 1.7 collective-permute-start.9
  243.1 1.6 collective-permute-done.8
  246.9 3.4 %collective-permute-start.10 = (f32[3,64]{0,1:T(8,128)S(1)}, f32[3,64]{0,1:T(8,128)S(1)}, u32[]{:S(2)}, u32[]{:S(2)}) collective-permute-start(f32[3,64]{0,1:T(8,128)S(1)} %get-tuple-element.534), channel_id=1, source_target_pairs={{0,128},{128,256},{256,384},{384,0},{1,129},{129,257},{257,385},{3... | collective-permute-start | bytes 2312 | tf_op jit(solution)/shard_map/ppermute | solution.py:25
  250.3 3.6 %collective-permute-start.11 = (f32[3,64]{0,1:T(8,128)S(1)}, f32[3,64]{0,1:T(8,128)S(1)}, u32[]{:S(2)}, u32[]{:S(2)}) collective-permute-start(f32[3,64]{0,1:T(8,128)S(1)} %get-tuple-element.533), channel_id=1, source_target_pairs={{128,0},{256,128},{384,256},{0,384},{129,1},{257,129},{385,257},{1... | collective-permute-start | bytes 2312 | tf_op jit(solution)/shard_map/ppermute | solution.py:26
  258.1 11.3 %all-reduce.7 = (f32[30]{0:T(128)S(1)}, f32[]{:T(128)}) all-reduce(f32[30]{0:T(128)S(1)} %convolution_bitcast_fusion.2, f32[]{:T(128)} %multiply_reduce_fusion.3), channel_id=1, replica_groups=mesh['gx'=4,'gy_0'=4,'gy_1'=2,'gz'=16] {'gx'}, use_global_device_ids=true, to_apply=%region_17.18 | all-reduce | flops 31 | bytes 248 | tf_op jit(solution)/shard_map/psum | solution.py:32
  269.3 11.0 %all-reduce.6 = (f32[30]{0:T(128)S(1)}, f32[]{:T(128)}) all-reduce(f32[30]{0:T(128)S(1)} %get-tuple-element.491, f32[]{:T(128)} %get-tuple-element.492), channel_id=1, replica_groups=mesh['gx'=4,'gy_0'=4,'gy_1'=2,'gz'=16] {'gy_0'}, use_global_device_ids=true, to_apply=%region_18.19 | all-reduce | flops 31 | bytes 248 | tf_op jit(solution)/shard_map/psum | solution.py:32
  280.3 3.1 all-reduce.8
  283.4 31.1 %all-reduce.5 = (f32[30]{0:T(128)S(1)}, f32[]{:T(128)}) all-reduce(f32[30]{0:T(128)S(1)} %get-tuple-element.493, f32[]{:T(128)} %get-tuple-element.494), channel_id=1, replica_groups=mesh['gx'=4,'gy_0'=4,'gy_1'=2,'gz'=16] {'gz'}, use_global_device_ids=true, to_apply=%region_20.0 | all-reduce | flops 31 | bytes 248 | tf_op jit(solution)/shard_map/psum | solution.py:32
  316.7 4.1 %reduce_sum.194 = f32[30,30]{1,0:T(8,128)S(1)} reduce(f32[512,30,30]{2,1,0:T(8,128)} %all-gather.4.cloned.1.call-done, f32[]{:T(128)} %constant.129.clone.1), dimensions={0}, to_apply=%region_26.0 | reduce | flops 459900 | bytes 1846804 | tf_op jit(solution)/shard_map/reduce_sum | solution.py:15
  (727 shorter events, 100.0 us)
Async XLA Ops:
  7.2 35.1 %copy-start.49 = (f32[2,16,100]{2,1,0:T(8,128)S(1)}, f32[2,16,100]{2,1,0:T(8,128)}, u32[]{:S(2)}) copy-start(f32[2,16,100]{2,1,0:T(8,128)} %param.24) | copy-start | bytes 38404
  7.2 42.3 %copy-start.1 = (f32[240,240]{1,0:T(8,128)S(1)}, f32[240,240]{1,0:T(8,128)}, u32[]{:S(2)}) copy-start(f32[240,240]{1,0:T(8,128)} %param.27) | copy-start | bytes 691204
  7.2 42.3 %copy-start = (f32[1600,240]{0,1:T(8,128)S(1)}, f32[1600,240]{0,1:T(8,128)}, u32[]{:S(2)}) copy-start(f32[1600,240]{0,1:T(8,128)} %param.25) | copy-start | bytes 4608004
  7.2 42.3 %copy-start.59 = (s32[1,1,1,128]{3,2,1,0:T(1,128)S(1)}, s32[1,1,1,128]{3,2,1,0:T(1,128)}, u32[]{:S(2)}) copy-start(s32[1,1,1,128]{3,2,1,0:T(1,128)} %param.20) | copy-start | bytes 1540
  7.2 42.3 %copy-start.57 = (s32[1,1,1,128]{3,2,1,0:T(1,128)S(1)}, s32[1,1,1,128]{3,2,1,0:T(1,128)}, u32[]{:S(2)}) copy-start(s32[1,1,1,128]{3,2,1,0:T(1,128)} %param.19) | copy-start | bytes 1540
  7.2 309.5 %all-gather.4.cloned.1.call-start = ((), (), s32[]{:S(2)}) async-start(), calls=%async_computation | async-start | bytes 8404992 | tf_op jit(solution)/shard_map/all_gather | solution.py:15
  10.6 10.9 %copy-start.53 = (s32[64]{0:T(128)}, s32[64]{0:T(128)S(1)}, u32[]{:S(2)}) copy-start(s32[64]{0:T(128)S(1)} %get-tuple-element.546) | copy-start | bytes 772
  10.6 10.9 %copy-start.54 = (s32[64]{0:T(128)}, s32[64]{0:T(128)S(1)}, u32[]{:S(2)}) copy-start(s32[64]{0:T(128)S(1)} %get-tuple-element.545) | copy-start | bytes 772
  12.1 9.8 %collective-permute-start = (f32[2,3,64]{1,0,2:T(2,128)S(1)}, f32[2,3,64]{1,0,2:T(2,128)S(1)}, u32[]{:S(2)}, u32[]{:S(2)}) collective-permute-start(f32[2,3,64]{1,0,2:T(2,128)S(1)} %bitcast.521), channel_id=1, source_target_pairs={{0,128},{128,256},{256,384},{384,0},{1,129},{129,257},{257,385},{3... | collective-permute-start | bytes 4616 | tf_op jit(solution)/shard_map/ppermute | solution.py:25
  16.2 6.2 %collective-permute-start.1 = (f32[2,3,64]{1,0,2:T(2,128)S(1)}, f32[2,3,64]{1,0,2:T(2,128)S(1)}, u32[]{:S(2)}, u32[]{:S(2)}) collective-permute-start(f32[2,3,64]{1,0,2:T(2,128)S(1)} %bitcast.520), channel_id=1, source_target_pairs={{128,0},{256,128},{384,256},{0,384},{129,1},{257,129},{385,257},{1... | collective-permute-start | bytes 4616 | tf_op jit(solution)/shard_map/ppermute | solution.py:26
  23.2 3.7 %collective-permute-start.2 = (f32[2,3,64]{1,0,2:T(2,128)S(1)}, f32[2,3,64]{1,0,2:T(2,128)S(1)}, u32[]{:S(2)}, u32[]{:S(2)}) collective-permute-start(f32[2,3,64]{1,0,2:T(2,128)S(1)} %bitcast.525), channel_id=1, source_target_pairs={{0,16},{16,32},{32,48},{48,64},{64,80},{80,96},{96,112},{112,0},{1... | collective-permute-start | bytes 4616 | tf_op jit(solution)/shard_map/ppermute | solution.py:25
  23.9 3.6 %collective-permute-start.3 = (f32[2,3,64]{1,0,2:T(2,128)S(1)}, f32[2,3,64]{1,0,2:T(2,128)S(1)}, u32[]{:S(2)}, u32[]{:S(2)}) collective-permute-start(f32[2,3,64]{1,0,2:T(2,128)S(1)} %bitcast.524), channel_id=1, source_target_pairs={{16,0},{32,16},{48,32},{64,48},{80,64},{96,80},{112,96},{0,112},{1... | collective-permute-start | bytes 4616 | tf_op jit(solution)/shard_map/ppermute | solution.py:26
  28.9 13.7 %collective-permute-start.5 = (f32[2,3,64]{1,0,2:T(2,128)S(1)}, f32[2,3,64]{1,0,2:T(2,128)S(1)}, u32[]{:S(2)}, u32[]{:S(2)}) collective-permute-start(f32[2,3,64]{1,0,2:T(2,128)S(1)} %bitcast.523), channel_id=1, source_target_pairs={{1,0},{2,1},{3,2},{4,3},{5,4},{6,5},{7,6},{8,7},{9,8},{10,9},{11,1... | collective-permute-start | bytes 4616 | tf_op jit(solution)/shard_map/ppermute | solution.py:26
  40.3 7.6 %collective-permute-start.4 = (f32[2,3,64]{1,0,2:T(2,128)S(1)}, f32[2,3,64]{1,0,2:T(2,128)S(1)}, u32[]{:S(2)}, u32[]{:S(2)}) collective-permute-start(f32[2,3,64]{1,0,2:T(2,128)S(1)} %bitcast.522), channel_id=1, source_target_pairs={{0,1},{1,2},{2,3},{3,4},{4,5},{5,6},{6,7},{7,8},{8,9},{9,10},{10,1... | collective-permute-start | bytes 4616 | tf_op jit(solution)/shard_map/ppermute | solution.py:25
  49.5 6.6 %copy-start.44 = (f32[3,512]{1,0:T(4,128)}, f32[3,512]{1,0:T(4,128)S(1)}, u32[]{:S(2)}) copy-start(f32[3,512]{1,0:T(4,128)S(1)} %get-tuple-element.740) | copy-start | bytes 18436 | tf_op jit(solution)/shard_map/while
  49.5 6.6 %copy-start.46 = (f32[3,512]{1,0:T(4,128)}, f32[3,512]{1,0:T(4,128)S(1)}, u32[]{:S(2)}) copy-start(f32[3,512]{1,0:T(4,128)S(1)} %get-tuple-element.739) | copy-start | bytes 18436 | tf_op jit(solution)/shard_map/while
  49.5 9.3 %copy-start.31 = (f32[2,16,100]{2,0,1:T(2,128)}, f32[2,16,100]{2,0,1:T(2,128)S(1)}, u32[]{:S(2)}) copy-start(f32[2,16,100]{2,0,1:T(2,128)S(1)} %get-tuple-element.742) | copy-start | bytes 38404 | tf_op jit(solution)/shard_map/while
  49.5 8.6 %copy-start.61 = (f32[16]{0:T(128)}, f32[16]{0:T(128)S(1)}, u32[]{:S(2)}) copy-start(f32[16]{0:T(128)S(1)} %iota_multiply_fusion.2) | copy-start | bytes 196 | tf_op jit(solution)/shard_map/while
  73.2 7.8 %copy-start.28 = (f32[32,16,4]{1,2,0:T(4,128)}, f32[32,16,4]{1,2,0:T(4,128)S(1)}, u32[]{:S(2)}) copy-start(f32[32,16,4]{1,2,0:T(4,128)S(1)} %convolution_multiply_fusion.11) | copy-start | bytes 24580 | tf_op jit(solution)/shard_map/while
  82.0 5.1 %copy-start.25 = (f32[32,128]{1,0:T(8,128)S(1)}, f32[32,128]{1,0:T(8,128)}, u32[]{:S(2)}) copy-start(f32[32,128]{1,0:T(8,128)} %copy-done.23) | copy-start | bytes 49156 | tf_op jit(solution)/shard_map/while
  82.0 5.1 %copy-start.27 = (f32[4,32,128]{2,1,0:T(8,128)S(1)}, f32[4,32,128]{2,1,0:T(8,128)}, u32[]{:S(2)}) copy-start(f32[4,32,128]{2,1,0:T(8,128)} %copy-done.26) | copy-start | bytes 196612 | tf_op jit(solution)/shard_map/while
  88.0 6.4 %copy-start.32 = (f32[2,16,100]{2,0,1:T(2,128)S(1)}, f32[2,16,100]{2,0,1:T(2,128)}, u32[]{:S(2)}) copy-start(f32[2,16,100]{2,0,1:T(2,128)} %copy-done.31) | copy-start | bytes 38404 | tf_op jit(solution)/shard_map/while
  88.0 6.4 %copy-start.45 = (f32[3,512]{1,0:T(4,128)S(1)}, f32[3,512]{1,0:T(4,128)}, u32[]{:S(2)}) copy-start(f32[3,512]{1,0:T(4,128)} %copy-done.44) | copy-start | bytes 18436 | tf_op jit(solution)/shard_map/while
  88.0 6.4 %copy-start.47 = (f32[3,512]{1,0:T(4,128)S(1)}, f32[3,512]{1,0:T(4,128)}, u32[]{:S(2)}) copy-start(f32[3,512]{1,0:T(4,128)} %copy-done.46) | copy-start | bytes 18436 | tf_op jit(solution)/shard_map/while
  88.0 6.4 %copy-start.58 = (s32[1,1,1,128]{3,2,1,0:T(1,128)S(1)}, s32[1,1,1,128]{3,2,1,0:T(1,128)}, u32[]{:S(2)}) copy-start(s32[1,1,1,128]{3,2,1,0:T(1,128)} %get-tuple-element.800) | copy-start | bytes 1540 | tf_op jit(solution)/shard_map/while
  88.0 6.4 %copy-start.60 = (s32[1,1,1,128]{3,2,1,0:T(1,128)S(1)}, s32[1,1,1,128]{3,2,1,0:T(1,128)}, u32[]{:S(2)}) copy-start(s32[1,1,1,128]{3,2,1,0:T(1,128)} %get-tuple-element.821) | copy-start | bytes 1540 | tf_op jit(solution)/shard_map/while
  94.4 6.6 %copy-start.44 = (f32[3,512]{1,0:T(4,128)}, f32[3,512]{1,0:T(4,128)S(1)}, u32[]{:S(2)}) copy-start(f32[3,512]{1,0:T(4,128)S(1)} %get-tuple-element.740) | copy-start | bytes 18436 | tf_op jit(solution)/shard_map/while
  94.4 6.6 %copy-start.46 = (f32[3,512]{1,0:T(4,128)}, f32[3,512]{1,0:T(4,128)S(1)}, u32[]{:S(2)}) copy-start(f32[3,512]{1,0:T(4,128)S(1)} %get-tuple-element.739) | copy-start | bytes 18436 | tf_op jit(solution)/shard_map/while
  94.4 9.3 %copy-start.31 = (f32[2,16,100]{2,0,1:T(2,128)}, f32[2,16,100]{2,0,1:T(2,128)S(1)}, u32[]{:S(2)}) copy-start(f32[2,16,100]{2,0,1:T(2,128)S(1)} %get-tuple-element.742) | copy-start | bytes 38404 | tf_op jit(solution)/shard_map/while
  94.5 8.6 %copy-start.61 = (f32[16]{0:T(128)}, f32[16]{0:T(128)S(1)}, u32[]{:S(2)}) copy-start(f32[16]{0:T(128)S(1)} %iota_multiply_fusion.2) | copy-start | bytes 196 | tf_op jit(solution)/shard_map/while
  118.1 7.8 %copy-start.28 = (f32[32,16,4]{1,2,0:T(4,128)}, f32[32,16,4]{1,2,0:T(4,128)S(1)}, u32[]{:S(2)}) copy-start(f32[32,16,4]{1,2,0:T(4,128)S(1)} %convolution_multiply_fusion.11) | copy-start | bytes 24580 | tf_op jit(solution)/shard_map/while
  132.9 6.5 %copy-start.32 = (f32[2,16,100]{2,0,1:T(2,128)S(1)}, f32[2,16,100]{2,0,1:T(2,128)}, u32[]{:S(2)}) copy-start(f32[2,16,100]{2,0,1:T(2,128)} %copy-done.31) | copy-start | bytes 38404 | tf_op jit(solution)/shard_map/while
  132.9 6.5 %copy-start.45 = (f32[3,512]{1,0:T(4,128)S(1)}, f32[3,512]{1,0:T(4,128)}, u32[]{:S(2)}) copy-start(f32[3,512]{1,0:T(4,128)} %copy-done.44) | copy-start | bytes 18436 | tf_op jit(solution)/shard_map/while
  132.9 6.5 %copy-start.47 = (f32[3,512]{1,0:T(4,128)S(1)}, f32[3,512]{1,0:T(4,128)}, u32[]{:S(2)}) copy-start(f32[3,512]{1,0:T(4,128)} %copy-done.46) | copy-start | bytes 18436 | tf_op jit(solution)/shard_map/while
  132.9 6.5 %copy-start.58 = (s32[1,1,1,128]{3,2,1,0:T(1,128)S(1)}, s32[1,1,1,128]{3,2,1,0:T(1,128)}, u32[]{:S(2)}) copy-start(s32[1,1,1,128]{3,2,1,0:T(1,128)} %get-tuple-element.800) | copy-start | bytes 1540 | tf_op jit(solution)/shard_map/while
  133.0 6.5 %copy-start.60 = (s32[1,1,1,128]{3,2,1,0:T(1,128)S(1)}, s32[1,1,1,128]{3,2,1,0:T(1,128)}, u32[]{:S(2)}) copy-start(s32[1,1,1,128]{3,2,1,0:T(1,128)} %get-tuple-element.821) | copy-start | bytes 1540 | tf_op jit(solution)/shard_map/while
  139.5 6.6 %copy-start.44 = (f32[3,512]{1,0:T(4,128)}, f32[3,512]{1,0:T(4,128)S(1)}, u32[]{:S(2)}) copy-start(f32[3,512]{1,0:T(4,128)S(1)} %get-tuple-element.740) | copy-start | bytes 18436 | tf_op jit(solution)/shard_map/while
  139.5 6.6 %copy-start.46 = (f32[3,512]{1,0:T(4,128)}, f32[3,512]{1,0:T(4,128)S(1)}, u32[]{:S(2)}) copy-start(f32[3,512]{1,0:T(4,128)S(1)} %get-tuple-element.739) | copy-start | bytes 18436 | tf_op jit(solution)/shard_map/while
  139.5 9.3 %copy-start.31 = (f32[2,16,100]{2,0,1:T(2,128)}, f32[2,16,100]{2,0,1:T(2,128)S(1)}, u32[]{:S(2)}) copy-start(f32[2,16,100]{2,0,1:T(2,128)S(1)} %get-tuple-element.742) | copy-start | bytes 38404 | tf_op jit(solution)/shard_map/while
  139.5 8.6 %copy-start.61 = (f32[16]{0:T(128)}, f32[16]{0:T(128)S(1)}, u32[]{:S(2)}) copy-start(f32[16]{0:T(128)S(1)} %iota_multiply_fusion.2) | copy-start | bytes 196 | tf_op jit(solution)/shard_map/while
  163.1 7.8 %copy-start.28 = (f32[32,16,4]{1,2,0:T(4,128)}, f32[32,16,4]{1,2,0:T(4,128)S(1)}, u32[]{:S(2)}) copy-start(f32[32,16,4]{1,2,0:T(4,128)S(1)} %convolution_multiply_fusion.11) | copy-start | bytes 24580 | tf_op jit(solution)/shard_map/while
  178.0 6.5 %copy-start.32 = (f32[2,16,100]{2,0,1:T(2,128)S(1)}, f32[2,16,100]{2,0,1:T(2,128)}, u32[]{:S(2)}) copy-start(f32[2,16,100]{2,0,1:T(2,128)} %copy-done.31) | copy-start | bytes 38404 | tf_op jit(solution)/shard_map/while
  178.0 6.5 %copy-start.45 = (f32[3,512]{1,0:T(4,128)S(1)}, f32[3,512]{1,0:T(4,128)}, u32[]{:S(2)}) copy-start(f32[3,512]{1,0:T(4,128)} %copy-done.44) | copy-start | bytes 18436 | tf_op jit(solution)/shard_map/while
  178.0 6.5 %copy-start.47 = (f32[3,512]{1,0:T(4,128)S(1)}, f32[3,512]{1,0:T(4,128)}, u32[]{:S(2)}) copy-start(f32[3,512]{1,0:T(4,128)} %copy-done.46) | copy-start | bytes 18436 | tf_op jit(solution)/shard_map/while
  178.0 6.5 %copy-start.58 = (s32[1,1,1,128]{3,2,1,0:T(1,128)S(1)}, s32[1,1,1,128]{3,2,1,0:T(1,128)}, u32[]{:S(2)}) copy-start(s32[1,1,1,128]{3,2,1,0:T(1,128)} %get-tuple-element.800) | copy-start | bytes 1540 | tf_op jit(solution)/shard_map/while
  178.0 6.5 %copy-start.60 = (s32[1,1,1,128]{3,2,1,0:T(1,128)S(1)}, s32[1,1,1,128]{3,2,1,0:T(1,128)}, u32[]{:S(2)}) copy-start(s32[1,1,1,128]{3,2,1,0:T(1,128)} %get-tuple-element.821) | copy-start | bytes 1540 | tf_op jit(solution)/shard_map/while
  184.5 6.6 %copy-start.44 = (f32[3,512]{1,0:T(4,128)}, f32[3,512]{1,0:T(4,128)S(1)}, u32[]{:S(2)}) copy-start(f32[3,512]{1,0:T(4,128)S(1)} %get-tuple-element.740) | copy-start | bytes 18436 | tf_op jit(solution)/shard_map/while
  184.5 6.6 %copy-start.46 = (f32[3,512]{1,0:T(4,128)}, f32[3,512]{1,0:T(4,128)S(1)}, u32[]{:S(2)}) copy-start(f32[3,512]{1,0:T(4,128)S(1)} %get-tuple-element.739) | copy-start | bytes 18436 | tf_op jit(solution)/shard_map/while
  184.5 9.3 %copy-start.31 = (f32[2,16,100]{2,0,1:T(2,128)}, f32[2,16,100]{2,0,1:T(2,128)S(1)}, u32[]{:S(2)}) copy-start(f32[2,16,100]{2,0,1:T(2,128)S(1)} %get-tuple-element.742) | copy-start | bytes 38404 | tf_op jit(solution)/shard_map/while
  184.6 8.6 %copy-start.61 = (f32[16]{0:T(128)}, f32[16]{0:T(128)S(1)}, u32[]{:S(2)}) copy-start(f32[16]{0:T(128)S(1)} %iota_multiply_fusion.2) | copy-start | bytes 196 | tf_op jit(solution)/shard_map/while
  208.2 7.8 %copy-start.28 = (f32[32,16,4]{1,2,0:T(4,128)}, f32[32,16,4]{1,2,0:T(4,128)S(1)}, u32[]{:S(2)}) copy-start(f32[32,16,4]{1,2,0:T(4,128)S(1)} %convolution_multiply_fusion.11) | copy-start | bytes 24580 | tf_op jit(solution)/shard_map/while
  223.0 6.5 %copy-start.32 = (f32[2,16,100]{2,0,1:T(2,128)S(1)}, f32[2,16,100]{2,0,1:T(2,128)}, u32[]{:S(2)}) copy-start(f32[2,16,100]{2,0,1:T(2,128)} %copy-done.31) | copy-start | bytes 38404 | tf_op jit(solution)/shard_map/while
  223.0 6.5 %copy-start.45 = (f32[3,512]{1,0:T(4,128)S(1)}, f32[3,512]{1,0:T(4,128)}, u32[]{:S(2)}) copy-start(f32[3,512]{1,0:T(4,128)} %copy-done.44) | copy-start | bytes 18436 | tf_op jit(solution)/shard_map/while
  223.0 6.5 %copy-start.47 = (f32[3,512]{1,0:T(4,128)S(1)}, f32[3,512]{1,0:T(4,128)}, u32[]{:S(2)}) copy-start(f32[3,512]{1,0:T(4,128)} %copy-done.46) | copy-start | bytes 18436 | tf_op jit(solution)/shard_map/while
  223.0 6.5 %copy-start.58 = (s32[1,1,1,128]{3,2,1,0:T(1,128)S(1)}, s32[1,1,1,128]{3,2,1,0:T(1,128)}, u32[]{:S(2)}) copy-start(s32[1,1,1,128]{3,2,1,0:T(1,128)} %get-tuple-element.800) | copy-start | bytes 1540 | tf_op jit(solution)/shard_map/while
  223.1 6.5 %copy-start.60 = (s32[1,1,1,128]{3,2,1,0:T(1,128)S(1)}, s32[1,1,1,128]{3,2,1,0:T(1,128)}, u32[]{:S(2)}) copy-start(s32[1,1,1,128]{3,2,1,0:T(1,128)} %get-tuple-element.821) | copy-start | bytes 1540 | tf_op jit(solution)/shard_map/while
  229.7 27.5 %copy-start.30 = (f32[30,3,1,1,1,128]{5,4,3,2,1,0:T(1,128)S(1)}, f32[30,3,1,1,1,128]{5,4,3,2,1,0:T(1,128)}, u32[]{:S(2)}) copy-start(f32[30,3,1,1,1,128]{5,4,3,2,1,0:T(1,128)} %param.17) | copy-start | bytes 138244
  230.6 7.9 %collective-permute-start.6 = (f32[3,64]{1,0:T(4,128)S(1)}, f32[3,64]{1,0:T(4,128)S(1)}, u32[]{:S(2)}, u32[]{:S(2)}) collective-permute-start(f32[3,64]{1,0:T(4,128)S(1)} %get-tuple-element.538), channel_id=1, source_target_pairs={{0,1},{1,2},{2,3},{3,4},{4,5},{5,6},{6,7},{7,8},{8,9},{9,10},{10,1... | collective-permute-start | bytes 2312 | tf_op jit(solution)/shard_map/ppermute | solution.py:25
  232.5 6.4 %collective-permute-start.7 = (f32[3,64]{1,0:T(4,128)S(1)}, f32[3,64]{1,0:T(4,128)S(1)}, u32[]{:S(2)}, u32[]{:S(2)}) collective-permute-start(f32[3,64]{1,0:T(4,128)S(1)} %get-tuple-element.537), channel_id=1, source_target_pairs={{1,0},{2,1},{3,2},{4,3},{5,4},{6,5},{7,6},{8,7},{9,8},{10,9},{11,1... | collective-permute-start | bytes 2312 | tf_op jit(solution)/shard_map/ppermute | solution.py:26
  241.3 3.4 %collective-permute-start.8 = (f32[3,64]{0,1:T(8,128)S(1)}, f32[3,64]{0,1:T(8,128)S(1)}, u32[]{:S(2)}, u32[]{:S(2)}) collective-permute-start(f32[3,64]{0,1:T(8,128)S(1)} %get-tuple-element.532), channel_id=1, source_target_pairs={{0,16},{16,32},{32,48},{48,64},{64,80},{80,96},{96,112},{112,0},{1... | collective-permute-start | bytes 2312 | tf_op jit(solution)/shard_map/ppermute | solution.py:25
  241.3 4.4 %collective-permute-start.9 = (f32[3,64]{0,1:T(8,128)S(1)}, f32[3,64]{0,1:T(8,128)S(1)}, u32[]{:S(2)}, u32[]{:S(2)}) collective-permute-start(f32[3,64]{0,1:T(8,128)S(1)} %get-tuple-element.531), channel_id=1, source_target_pairs={{16,0},{32,16},{48,32},{64,48},{80,64},{96,80},{112,96},{0,112},{1... | collective-permute-start | bytes 2312 | tf_op jit(solution)/shard_map/ppermute | solution.py:26
  246.9 7.3 %collective-permute-start.10 = (f32[3,64]{0,1:T(8,128)S(1)}, f32[3,64]{0,1:T(8,128)S(1)}, u32[]{:S(2)}, u32[]{:S(2)}) collective-permute-start(f32[3,64]{0,1:T(8,128)S(1)} %get-tuple-element.534), channel_id=1, source_target_pairs={{0,128},{128,256},{256,384},{384,0},{1,129},{129,257},{257,385},{3... | collective-permute-start | bytes 2312 | tf_op jit(solution)/shard_map/ppermute | solution.py:25
  250.3 5.8 %collective-permute-start.11 = (f32[3,64]{0,1:T(8,128)S(1)}, f32[3,64]{0,1:T(8,128)S(1)}, u32[]{:S(2)}, u32[]{:S(2)}) collective-permute-start(f32[3,64]{0,1:T(8,128)S(1)} %get-tuple-element.533), channel_id=1, source_target_pairs={{128,0},{256,128},{384,256},{0,384},{129,1},{257,129},{385,257},{1... | collective-permute-start | bytes 2312 | tf_op jit(solution)/shard_map/ppermute | solution.py:26
  315.1 5.7 %copy-start.52 = (f32[30]{0:T(128)}, f32[30]{0:T(128)S(1)}, u32[]{:S(2)}) copy-start(f32[30]{0:T(128)S(1)} %get-tuple-element.504) | copy-start | bytes 364
  (174 other events, 601.1 us)
Sparse Core Ops, SparseCore 0:
  12.6 217.5 all-gather.3
where the time goes:
time: 333 us; the launch traced here: 331 us
  matrix products  148 us (44%)
  blocking collectives  56.4 us (17%)
  starting transfers between devices  38 us (11%)
  local copies, waits for them, and re-layouts  31.5 us (9%)
  other arithmetic  24.6 us (7%)
  between operations  17.6 us (5%)
  waiting for transfers between devices  10.5 us (3%)
  loops' own time  4.36 us (1%)
    psum x4, blocking collectives, by_axis(): return functools.reduce(lax.psum, axes, x)  56.4 us
    dot_general x16, matrix products, site_energy(): jnp.dot(descriptor, fit_w1, precision=highest) + fit_b1  38.2 us
    dot_general x36, matrix products, site_energy(): jnp.einsum('bkn,abn->bka', profile, radial, precision=highest)  32.5 us
    ppermute x6, starting transfers between devices, with_halo(): after = lax.ppermute(leading, axis, down)  27.3 us
    dot_general x36, matrix products, site_energy(): jnp.einsum('bma,bna->bmn', environment, environment[:, :M2], precision=hi...  25.1 us
    dot_general x4, matrix products, one_block(): picked = jnp.einsum('ce,se->cs', both_fields, selector, precision=highest)  17.9 us
    dot_general x4, matrix products, one_block(): jnp.dot(around_term.reshape(3, -1), selector, precision=highest)  16.1 us
    ppermute x6, starting transfers between devices, with_halo(): before = lax.ppermute(last, axis, up)  10.7 us
  transfers between devices with their start and end apart: 13, of which 8 were waited for; matrix products, arithmetic and copies ran while one was open for 59% of the time, Pallas kernels for 0%

commit v1 on v0

v1 whole, which is shorter than its diff:
```python
import functools

import jax
import jax.numpy as jnp
from jax import lax
from jax.experimental import pallas as pl
from jax.experimental.pallas import tpu as pltpu
from jax.sharding import PartitionSpec as P

F32 = jnp.float32
BF16 = jnp.bfloat16
LOG2E = 1.4426950408889634
NT = (((1,), (1,)), ((), ()))


def split(x):
    hi = x.astype(BF16)
    return hi, (x - hi.astype(F32)).astype(BF16)


def mm(a, b):
    return jnp.dot(a, b, preferred_element_type=F32)


def dot3(a, b):
    ah, al = a if isinstance(a, tuple) else split(a)
    bh, bl = b if isinstance(b, tuple) else split(b)
    return mm(ah, bh) + (mm(ah, bl) + mm(al, bh))


def lane_pick(table, index):
    return jnp.take_along_axis(table, index, axis=1, mode="promise_in_bounds")


def rows_of(shape, dim=0):
    return lax.broadcasted_iota(jnp.int32, shape, dim)


def prepare_kernel(table, w1, w2, b1, b2, wo, ids, u_hi, u_lo, ut_hi, ut_lo, w2_hi, w2_lo, w2t_hi, w2t_lo, cols, ids_t, ws, ys, us, pad):
    types, levels, width = table.shape
    hidden = w1.shape[1]
    inner = levels * levels
    m2 = w1.shape[0] // width
    rest = hidden - 128
    tall = split(table[...].reshape(types * levels, width))
    ws[0] = w1[:, 0:128]
    ws[1] = jnp.zeros_like(ws[1])
    ws[1, :, 0:rest] = w1[:, 128:hidden]
    for j in range(m2):
        column = jnp.concatenate([ws[0, pl.ds(j, width, stride=m2), :], ws[1, pl.ds(j, width, stride=m2), :]], axis=1)
        part = dot3(tall, column)
        for t in range(types):
            for half in range(2):
                ys[t, half, pl.ds(j, levels, stride=m2), :] = part[t * levels : (t + 1) * levels, half * 128 : (half + 1) * 128]
    r = rows_of((inner, levels))
    spread = (r % levels == rows_of((inner, levels), 1)).astype(BF16)
    r = rows_of((m2, levels * m2), 1)
    tile = (r % m2 == rows_of((m2, levels * m2))).astype(BF16)
    same = rows_of((inner, levels * m2)) // levels == rows_of((inner, levels * m2), 1) // m2
    for t in range(types):
        th, tl = split(table[t][:, 0:m2])
        kh = mm(mm(spread, th).astype(BF16), tile)
        kl = mm(mm(spread, tl).astype(BF16), tile)
        kron = (jnp.where(same, kh, 0.0).astype(BF16), jnp.where(same, kl, 0.0).astype(BF16))
        for half in range(2):
            us[half, t * inner : (t + 1) * inner, :] = dot3(kron, ys[t, half])
    for t in range(types):
        for k in range(levels):
            at = t * inner + k * levels
            for half in range(2):
                block = us[half, at : at + levels, :]
                other = us[half, pl.ds(t * inner + k, levels, stride=levels), :]
                hi, lo = split(0.5 * (block + other))
                u_hi[at : at + levels, half * 128 : (half + 1) * 128] = hi
                u_lo[at : at + levels, half * 128 : (half + 1) * 128] = lo
    full = u_hi[...].astype(F32) + u_lo[...].astype(F32)
    hi, lo = split(full.T)
    ut_hi[...] = hi
    ut_lo[...] = lo
    pad[...] = jnp.zeros_like(pad)
    pad[0:hidden, 0:hidden] = w2[...]
    hi, lo = split(pad[...])
    w2_hi[...] = hi
    w2_lo[...] = lo
    hi, lo = split(pad[...].T)
    w2t_hi[...] = hi
    w2t_lo[...] = lo
    pad[...] = jnp.zeros_like(pad)
    pad[0:1, 0:hidden] = b1[...]
    pad[1:2, 0:hidden] = b2[...]
    pad[2:3, 0:hidden] = wo[...]
    cols[...] = pad[0:128, :].T
    ids_t[...] = ids[0, 0, 0].astype(F32).T.astype(jnp.int32)


def vmem(n):
    return [pl.BlockSpec(memory_space=pltpu.VMEM)] * n


def prepare(table, w1, w2, b1, b2, wo, ids):
    n = ids.shape[-1]
    hp = 256
    inner = table.shape[0] * table.shape[1] ** 2
    shapes = [((inner, hp), BF16)] * 2 + [((hp, inner), BF16)] * 2 + [((hp, hp), BF16)] * 4 + [((hp, 128), F32), ((n, 128), jnp.int32)]
    return pl.pallas_call(
        prepare_kernel,
        out_shape=[jax.ShapeDtypeStruct(s, d) for s, d in shapes],
        in_specs=vmem(7),
        out_specs=vmem(len(shapes)),
        scratch_shapes=[
            pltpu.VMEM((2, w1.shape[0], 128), F32),
            pltpu.VMEM((table.shape[0], 2, inner // table.shape[0], 128), F32),
            pltpu.VMEM((2, inner, 128), F32),
            pltpu.VMEM((hp, hp), F32),
        ],
        name="prepare",
    )(table, w1, w2, b1[None], b2[None], wo[None], ids)


def shifted_ghosts(below, above, coord, rows):
    lower = rows_of((rows, 128), 1) < 64
    step = jnp.where(rows_of((rows, 128)) == coord, 1.0, 0.0)
    return jnp.where(lower, below - step, above + step)


def product_kernel(tiles, below, above, ids_t, counts, kinds, u_hi, u_lo, ut_hi, ut_lo, w2_hi, w2_lo, w2t_hi, w2t_lo, cols, out, xv, edge, phis, acc, pairs, grads, force, lows):
    n_slots = ids_t.shape[0]
    levels = 16
    gap = levels - 1
    blocks = n_slots // 8
    xv[0:3] = tiles[...]
    xv[3] = shifted_ghosts(pltpu.roll(below[...], 64, 1), pltpu.roll(above[...], 64, 1), 2, 8)
    count_row = jnp.broadcast_to(counts[0, 0], (8, 128))

    def geometry(nb, carry):
        rows = pl.ds(pl.multiple_of(nb * 8, 8), 8)
        index = ids_t[rows, :]
        low = index & 127
        high = index >> 7
        lows[rows, :] = low.astype(F32)
        near = []
        for f in range(6):
            picks = [lane_pick(jnp.broadcast_to(xv[q, f : f + 1, :], (8, 128)), low) for q in range(4)]
            value = jnp.where(high < 2, jnp.where(high == 0, picks[0], picks[1]), jnp.where(high == 2, picks[2], picks[3]))
            near.append(value - jnp.broadcast_to(xv[0, f : f + 1, :], (8, 128)))
        d, dd = near[:3], near[3:]
        square = d[0] * d[0] + d[1] * d[1] + d[2] * d[2]
        rate = 2.0 * (d[0] * dd[0] + d[1] * dd[1] + d[2] * dd[2])
        wide = square + 0.01
        inverse = lax.rsqrt(wide)
        half = 0.5 / wide
        live = (rows_of((8, 128)) + nb * 8) < count_row
        s = jnp.where(live, jnp.exp(-square) * inverse, 0.0)
        tau = s * inverse
        sq = -s * (1.0 + half)
        tq = -tau * (1.0 + 2.0 * half)
        share = 1.0 / (1.0 + s)
        us = gap * share * share
        for c in range(3):
            edge[c, rows, :] = d[c]
            edge[3 + c, rows, :] = dd[c]
            edge[9 + c, rows, :] = tau * d[c]
            edge[13 + c, rows, :] = tq * rate * d[c] + tau * dd[c]
        edge[6, rows, :] = gap * s * share
        edge[7, rows, :] = us * sq * rate
        edge[8, rows, :] = s
        edge[12, rows, :] = sq * rate
        edge[16, rows, :] = tau
        edge[17, rows, :] = half
        edge[18, rows, :] = rate
        return carry

    lax.fori_loop(0, blocks, geometry, 0)

    def pooling(kk, carry):
        sums = [[jnp.zeros((8, 128), F32) for _ in range(8)] for _ in range(2)]
        for nb in range(blocks):
            rows = pl.ds(nb * 8, 8)
            u = edge[6, rows, :]
            w = -2.0 * edge[7, rows, :]
            radial = [edge[8 + a, rows, :] for a in range(4)]
            moved = [edge[12 + a, rows, :] for a in range(4)]
            for side in range(2):
                z = u - (2 * kk + side).astype(F32)
                phi = jnp.exp2(z * (z * (-LOG2E)))
                phis[2 * kk + side, rows, :] = phi
                dphi = phi * (z * w)
                for a in range(4):
                    sums[side][a] = sums[side][a] + phi * radial[a]
                    sums[side][4 + a] = sums[side][4 + a] + (dphi * radial[a] + phi * moved[a])
        for side in range(2):
            for a in range(8):
                acc[pl.ds(pl.multiple_of((a * levels + 2 * kk + side) * 8, 8), 8), :] = sums[side][a]
        return carry

    lax.fori_loop(0, levels // 2, pooling, 0)
    pooled = acc[pl.ds(0, 128, stride=8), :]
    for s in range(1, 8):
        pooled = pooled + acc[pl.ds(s, 128, stride=8), :]
    pooled = pooled * (1.0 / n_slots)
    grads[...] = pooled
    second = jnp.broadcast_to(kinds[0, 0], (16, 128)) == 1
    p = [pooled[a * 16 : (a + 1) * 16] for a in range(4)]
    dp = [pooled[64 + a * 16 : 64 + (a + 1) * 16] for a in range(4)]
    for k in range(levels):
        value = jnp.zeros((16, 128), F32)
        moved = jnp.zeros((16, 128), F32)
        for a in range(4):
            value = value + p[a] * jnp.broadcast_to(grads[a * 16 + k : a * 16 + k + 1, :], (16, 128))
            moved = moved + p[a] * jnp.broadcast_to(grads[64 + a * 16 + k : 64 + a * 16 + k + 1, :], (16, 128))
        moved = 2.0 * moved
        pairs[k * 16 : (k + 1) * 16, 0:128] = jnp.where(second, 0.0, value)
        pairs[k * 16 : (k + 1) * 16, 128:256] = jnp.where(second, 0.0, moved)
        pairs[256 + k * 16 : 256 + (k + 1) * 16, 0:128] = jnp.where(second, value, 0.0)
        pairs[256 + k * 16 : 256 + (k + 1) * 16, 128:256] = jnp.where(second, moved, 0.0)
    z1 = dot3((ut_hi[...], ut_lo[...]), pairs[...])
    h1 = jnp.tanh(z1[:, 0:128] + cols[:, 0:1])
    slope1 = 1.0 - h1 * h1
    dh1 = slope1 * z1[:, 128:256]
    z2 = dot3((w2t_hi[...], w2t_lo[...]), jnp.concatenate([h1, dh1], axis=1))
    t2 = jnp.tanh(z2[:, 0:128] + cols[:, 1:2])
    slope2 = 1.0 - t2 * t2
    read = cols[:, 2:3]
    delta2 = slope2 * read
    ddelta2 = -2.0 * t2 * (slope2 * z2[:, 128:256]) * read
    back = dot3((w2_hi[...], w2_lo[...]), jnp.concatenate([delta2, ddelta2], axis=1))
    e1 = back[:, 0:128] + read
    delta1 = slope1 * e1
    ddelta1 = slope1 * back[:, 128:256] - 2.0 * h1 * dh1 * e1
    pairs[...] = dot3((u_hi[...], u_lo[...]), jnp.concatenate([delta1, ddelta1], axis=1))
    g = [jnp.zeros((16, 128), F32) for _ in range(4)]
    dg = [jnp.zeros((16, 128), F32) for _ in range(4)]
    for k in range(levels):
        low, top = pl.ds(k * 16, 16), pl.ds(256 + k * 16, 16)
        m = jnp.where(second, pairs[top, 0:128], pairs[low, 0:128])
        dm = jnp.where(second, pairs[top, 128:256], pairs[low, 128:256])
        for a in range(4):
            row = jnp.broadcast_to(grads[a * 16 + k : a * 16 + k + 1, :], (16, 128))
            drow = jnp.broadcast_to(grads[64 + a * 16 + k : 64 + a * 16 + k + 1, :], (16, 128))
            g[a] = g[a] + m * row
            dg[a] = dg[a] + (dm * row + m * drow)
    scale = 2.0 / n_slots
    for a in range(4):
        grads[a * 16 : (a + 1) * 16, :] = g[a] * scale
        grads[64 + a * 16 : 64 + (a + 1) * 16, :] = dg[a] * scale

    def backward(nb, centre):
        rows = pl.ds(pl.multiple_of(nb * 8, 8), 8)
        u = edge[6, rows, :]
        zero = jnp.zeros((8, 128), F32)
        s0, s1, s2, r0, r1 = ([zero] * 4 for _ in range(5))
        for k in range(levels):
            z = u - float(k)
            phi = phis[k, rows, :]
            phi1 = z * phi
            phi2 = z * phi1
            for a in range(4):
                row = jnp.broadcast_to(grads[a * 16 + k : a * 16 + k + 1, :], (8, 128))
                drow = jnp.broadcast_to(grads[64 + a * 16 + k : 64 + a * 16 + k + 1, :], (8, 128))
                s0[a] = s0[a] + row * phi
                s1[a] = s1[a] + row * phi1
                s2[a] = s2[a] + row * phi2
                r0[a] = r0[a] + drow * phi
                r1[a] = r1[a] + drow * phi1
        d = [edge[c, rows, :] for c in range(3)]
        dd = [edge[3 + c, rows, :] for c in range(3)]
        du = edge[7, rows, :]
        radial = [edge[8 + a, rows, :] for a in range(4)]
        moved = [edge[12 + a, rows, :] for a in range(4)]
        s = radial[0]
        tau = edge[16, rows, :]
        half = edge[17, rows, :]
        rate = edge[18, rows, :]
        one = 1.0 + half
        two = one + half
        sq = -s * one
        sqq = s * (one * one + 2.0 * half * half)
        tq = -tau * two
        tqq = tau * (two * two + 4.0 * half * half)
        share = 1.0 / (1.0 + s)
        us = gap * share * share
        uq = us * sq
        uqq = us * (sqq - 2.0 * share * sq * sq)
        a1 = [-2.0 * v for v in s1]
        da = [r0[a] + a1[a] * du for a in range(4)]
        da1 = [-2.0 * r1[a] + (4.0 * s2[a] - 2.0 * s0[a]) * du for a in range(4)]
        a1r = a1[0] * radial[0] + a1[1] * radial[1] + (a1[2] * radial[2] + a1[3] * radial[3])
        ad = s0[1] * d[0] + s0[2] * d[1] + s0[3] * d[2]
        turned = da1[0] * radial[0] + a1[0] * moved[0]
        for a in range(1, 4):
            turned = turned + (da1[a] * radial[a] + a1[a] * moved[a])
        dad = da[1] * d[0] + s0[1] * dd[0]
        for c in range(1, 3):
            dad = dad + (da[c + 1] * d[c] + s0[c + 1] * dd[c])
        eq = uq * a1r + sq * s0[0] + tq * ad
        deq = rate * (uqq * a1r + sqq * s0[0] + tqq * ad) + uq * turned + sq * da[0] + tq * dad
        dtau = tq * rate
        result = []
        for c in range(3):
            value = 2.0 * (dd[c] * eq + d[c] * deq) + (dtau * s0[c + 1] + tau * da[c + 1])
            hi = value.astype(BF16).astype(F32)
            force[c, rows, :] = hi
            force[3 + c, rows, :] = value - hi
            result.append(centre[c] + value)
        return tuple(result)

    zero = jnp.zeros((8, 128), F32)
    centre = lax.fori_loop(0, blocks, backward, (zero, zero, zero))
    row8 = rows_of((8, 128))
    quarter = row8 & 3
    upper = row8 < 4
    rows16 = [(rows_of((16, 128)) + 16 * rg).astype(F32).astype(BF16) for rg in range(8)]
    chunk = 8

    def scatter(step, total):
        lefts, hots = [], []
        for i in range(chunk):
            n = step * chunk + i
            high = jnp.broadcast_to(ids_t[pl.ds(n, 1), :], (8, 128)) >> 7
            here = high == quarter
            stack = [
                jnp.where(here, jnp.where(upper, jnp.broadcast_to(force[c, pl.ds(n, 1), :], (8, 128)), jnp.broadcast_to(force[3 + c, pl.ds(n, 1), :], (8, 128))), 0.0)
                for c in range(3)
            ]
            lefts.append(jnp.concatenate(stack, axis=0).astype(BF16))
            low = jnp.broadcast_to(lows[pl.ds(n, 1), :], (16, 128)).astype(BF16)
            hots.append(jnp.concatenate([jnp.where(low == r, 1.0, 0.0).astype(BF16) for r in rows16], axis=0))
        return total + lax.dot_general(jnp.concatenate(lefts, axis=1), jnp.concatenate(hots, axis=1), NT, preferred_element_type=F32)

    total = lax.fori_loop(0, n_slots // chunk, scatter, jnp.zeros((24, 128), F32))
    out[...] = jnp.zeros_like(out)
    for c in range(3):
        both = total[c * 8 : c * 8 + 4] + total[c * 8 + 4 : c * 8 + 8]
        for q in range(4):
            row = both[q : q + 1]
            if q == 0:
                row = row - jnp.sum(centre[c], axis=0, keepdims=True)
            out[q, c : c + 1, :] = row


def product(tiles, below, above, prepared, counts, kinds):
    *weights, ids_t = prepared
    n = ids_t.shape[0]
    return pl.pallas_call(
        product_kernel,
        out_shape=jax.ShapeDtypeStruct((4, 8, 128), F32),
        in_specs=vmem(15),
        out_specs=vmem(1)[0],
        scratch_shapes=[
            pltpu.VMEM((4, 8, 128), F32),
            pltpu.VMEM((19, n, 128), F32),
            pltpu.VMEM((16, n, 128), F32),
            pltpu.VMEM((1024, 128), F32),
            pltpu.VMEM((512, 256), F32),
            pltpu.VMEM((128, 128), F32),
            pltpu.VMEM((6, n, 128), F32),
            pltpu.VMEM((n, 128), F32),
        ],
        name="product",
    )(tiles, below, above, ids_t, counts, kinds, *weights)


def halves(ref):
    return jnp.concatenate([ref[0, 0, 0, 0:1, :], ref[0, 0, 0, 1:2, :]], axis=1)


def pack_kernel(places, tangent, map_x, map_y, out):
    rows = [places[c, 0, 0] for c in range(3)] + [tangent[0, c, 0, 0] for c in range(3)]
    rows += [halves(map_x).astype(F32), halves(map_y).astype(F32)]
    out[...] = jnp.broadcast_to(jnp.concatenate(rows, axis=0)[None], out.shape)


def pack(positions, basis, map_x, map_y, bricks):
    last = basis.shape[0] - 1
    whole = lambda a: pl.BlockSpec(a.shape, lambda i: (0,) * a.ndim)
    return pl.pallas_call(
        pack_kernel,
        grid=(1,),
        out_shape=jax.ShapeDtypeStruct((bricks, 8, 128), F32),
        in_specs=[
            whole(positions),
            pl.BlockSpec((1,) + basis.shape[1:], lambda i: (last,) + (0,) * (basis.ndim - 1)),
            whole(map_x),
            whole(map_y),
        ],
        out_specs=pl.BlockSpec((bricks, 8, 128), lambda i: (0, 0, 0)),
        name="pack",
    )(positions, basis, map_x, map_y)


def brick_reader(where, grid):
    nx, ny = grid

    def at(ref, dx, dy):
        x = lax.rem(where[0] + (dx + nx), nx)
        y = lax.rem(where[1] + (dy + ny), ny)
        return ref[x * ny + y]

    return at


def as_index(row):
    return jnp.broadcast_to(row, (8, 128)).astype(jnp.int32)


def turn(x):
    return pltpu.roll(x, 64, 1)


def assemble_kernel(grid, where, got, map_z, tiles, message):
    at = brick_reader(where, grid)
    lower = rows_of((8, 128), 1) < 64
    row = rows_of((8, 128))
    step_x = jnp.where(row == 0, 1.0, 0.0)
    step_y = jnp.where(row == 1, 1.0, 0.0)
    middle, ghosts, index = {}, {}, {}
    for dy in (-1, 0, 1):
        own, low, high = at(got, 0, dy), at(got, -1, dy), at(got, 1, dy)
        from_low = lane_pick(low, turn(as_index(low[6:7])))
        from_high = lane_pick(high, turn(as_index(high[6:7])))
        middle[dy] = own
        ghosts[dy] = jnp.where(lower, from_low - step_x, from_high + step_x)
        index[dy] = turn(as_index(own[7:8]))

    def second(dy):
        low = index[dy] & 127
        return jnp.where(index[dy] < 128, lane_pick(middle[dy], low), lane_pick(ghosts[dy], low))

    third = jnp.where(lower, second(-1) - step_y, second(1) + step_y)
    tiles[0] = middle[0]
    tiles[1] = ghosts[0]
    tiles[2] = third
    chosen = jnp.broadcast_to(halves(map_z), (8, 128))
    low = chosen & 127
    message[...] = jnp.where(
        chosen < 128, lane_pick(middle[0], low), jnp.where(chosen < 256, lane_pick(ghosts[0], low), lane_pick(third, low))
    )


def smem():
    return [pl.BlockSpec(memory_space=pltpu.SMEM)]


def assemble(where, got, map_z, grid):
    return pl.pallas_call(
        functools.partial(assemble_kernel, grid),
        out_shape=[jax.ShapeDtypeStruct((3, 8, 128), F32), jax.ShapeDtypeStruct((8, 128), F32)],
        in_specs=smem() + vmem(2),
        out_specs=vmem(2),
        name="assemble",
    )(where, got, map_z)


def thirds(x):
    hi, rest = x.astype(BF16), x
    rest = x - hi.astype(F32)
    mid = rest.astype(BF16)
    low = (rest - mid.astype(F32)).astype(BF16)
    return jnp.concatenate([hi.astype(F32), mid.astype(F32), low.astype(F32)], axis=0).astype(BF16)


def spread_columns(values, index, columns, first):
    target = rows_of((columns, 128)) + first
    hot = jnp.where(jnp.broadcast_to(index, (columns, 128)) == target, 1.0, 0.0).astype(BF16)
    both = lax.dot_general(thirds(values), hot, NT, preferred_element_type=F32)
    return both[0:8] + (both[8:16] + both[16:24])


def fold_z_kernel(products, below, above, map_z, own, out):
    lower = rows_of((8, 128), 1) < 64
    value = jnp.where(lower, turn(below[...]), turn(above[...]))
    added = spread_columns(value, halves(map_z), 384, 0)
    own[...] = products[0] + added[:, 0:128]
    first = products[1] + added[:, 128:256]
    second = products[2] + added[:, 256:384]
    tile = jnp.concatenate([first[0:3], second[0:3], jnp.zeros((2, 128), F32)], axis=0)
    out[...] = jnp.broadcast_to(tile[None], out.shape)


def fold_z(products, below, above, map_z, bricks):
    return pl.pallas_call(
        fold_z_kernel,
        out_shape=[jax.ShapeDtypeStruct((8, 128), F32), jax.ShapeDtypeStruct((bricks, 8, 128), F32)],
        in_specs=vmem(4),
        out_specs=vmem(2),
        name="fold_z",
    )(products, below, above, map_z)


def gram_kernel(basis, stored, gram):
    count = basis.shape[0]
    stored[...] = jnp.zeros_like(stored)
    total = jnp.zeros((32, 32), F32)
    for c in range(3):
        for k in range(count):
            stored[c, k : k + 1, :] = basis[k, c, 0, 0]
        total = total + lax.dot_general(stored[c], stored[c], NT, precision=lax.Precision.HIGHEST, preferred_element_type=F32)
    gram[...] = jnp.zeros_like(gram)
    gram[:, 0:32] = total


def local_gram(basis):
    return pl.pallas_call(
        gram_kernel,
        out_shape=[jax.ShapeDtypeStruct((3, 32, 128), F32), jax.ShapeDtypeStruct((32, 128), F32)],
        in_specs=vmem(1),
        out_specs=vmem(2),
        name="gram",
    )(basis)


def fold_kernel(grid, where, own, got, maps, stored, gram, product, out):
    at = brick_reader(where, grid)
    lower = rows_of((8, 128), 1) < 64

    def from_y(dx):
        return jnp.where(lower, turn(at(got, dx, -1)), turn(at(got, dx, 1)))

    def second(value):
        return jnp.concatenate([value[3:6], jnp.zeros((5, 128), F32)], axis=0)

    def ghost(dx):
        index = at(maps, dx, 0)[7:8].astype(jnp.int32)
        return at(got, dx, 0) + spread_columns(second(from_y(dx)), index, 128, 128)

    mine = at(maps, 0, 0)
    total = own[...] + spread_columns(second(from_y(0)), mine[7:8].astype(jnp.int32), 128, 0)
    from_x = jnp.where(lower, turn(ghost(-1)), turn(ghost(1)))
    total = total + spread_columns(from_x, mine[6:7].astype(jnp.int32), 128, 0)
    product[...] = total
    last = rows_of((32, 128)) == 30
    column = jnp.zeros((32, 128), F32)
    line = jnp.zeros((8, 32), F32)
    for c in range(3):
        row = total[c : c + 1]
        rows = jnp.where(last, row, stored[c])
        column = column + rows * row
        line = line + lax.dot_general(
            jnp.broadcast_to(row, (8, 128)), rows, NT, precision=lax.Precision.HIGHEST, preferred_element_type=F32
        )
    column = jnp.sum(column, axis=1, keepdims=True)
    line = jnp.concatenate([line[0:1], jnp.zeros((1, 96), F32)], axis=1)
    lane = rows_of((32, 128), 1)
    full = jnp.where(lane == 30, column, jnp.where(last, line, gram[...]))
    tile = full[0:8]
    for b in range(1, 4):
        tile = tile + pltpu.roll(full[8 * b : 8 * b + 8], 32 * b, 1)
    out[...] = jnp.broadcast_to(tile[None], out.shape)


def fold(where, own, got, maps, stored, gram, grid):
    return pl.pallas_call(
        functools.partial(fold_kernel, grid),
        out_shape=[jax.ShapeDtypeStruct((8, 128), F32), jax.ShapeDtypeStruct(got.shape, F32)],
        in_specs=smem() + vmem(5),
        out_specs=vmem(2),
        name="fold",
    )(where, own, got, maps, stored, gram)


def total_kernel(got, out):
    out[...] = jnp.broadcast_to(jnp.sum(got[...], axis=0)[None], out.shape)


def total_of(got, copies):
    return pl.pallas_call(
        total_kernel,
        out_shape=jax.ShapeDtypeStruct((copies,) + got.shape[1:], F32),
        in_specs=vmem(1),
        out_specs=vmem(1)[0],
        name="total",
    )(got)


def finish_kernel(entries, got, product, stored, result, correlations, norm):
    count = correlations.shape[1] - 98
    packed = jnp.sum(got[...], axis=0) * (1.0 / entries)
    full = jnp.concatenate([packed] + [pltpu.roll(packed, 128 - 32 * b, 1) for b in range(1, 4)], axis=0)
    column = full[:, count : count + 1]
    line = full[count : count + 1, :]
    row = rows_of((32, 1))
    lane = rows_of((1, 128), 1)
    down = jnp.where(row < count, column, jnp.where(row == count, -1.0, 0.0))
    across = jnp.where(lane < count, line, jnp.where(lane == count, -1.0, 0.0))
    square = jnp.sum(jnp.where(rows_of((32, 128), 1) <= count, full * across * down, 0.0), axis=1, keepdims=True)
    length = jnp.sqrt(jnp.maximum(jnp.sum(square, axis=0, keepdims=True), 0.0) + 1e-06)
    norm[...] = length
    correlations[...] = line
    share = jnp.where(row < count, column, 0.0)
    for c in range(3):
        taken = jnp.sum(stored[c] * share, axis=0, keepdims=True)
        result[c, 0, 0] = (product[c : c + 1, :] - taken) / length


def finish(got, product, stored, shape, entries):
    return pl.pallas_call(
        functools.partial(finish_kernel, entries),
        out_shape=[
            jax.ShapeDtypeStruct(shape, F32),
            jax.ShapeDtypeStruct((1, 128), F32),
            jax.ShapeDtypeStruct((1, 1), F32),
        ],
        in_specs=vmem(3),
        out_specs=vmem(3),
        name="finish",
    )(got, product, stored)


def on_device(positions, basis, neighbours, used_count, kinds, map_x, map_y, map_z, table, fit_w1, fit_b1, fit_w2, fit_b2, fit_out):
    nx, ny, nz = (lax.axis_size(a) for a in ("gx", "gy", "gz"))
    plane = ("gx", "gy")
    where = jnp.stack([lax.axis_index("gx"), lax.axis_index("gy")]).astype(jnp.int32)
    up = [(i, (i + 1) % nz) for i in range(nz)]
    down = [(j, i) for i, j in up]

    def exchange(x):
        return lax.all_to_all(x, plane, 0, 0)

    raw = exchange(pack(positions, basis, map_x, map_y, nx * ny))
    tiles, message = assemble(where, raw, map_z, (nx, ny))
    below, above = lax.ppermute(message, "gz", up), lax.ppermute(message, "gz", down)
    prepared = prepare(table, fit_w1, fit_w2, fit_b1, fit_b2, fit_out, neighbours)
    stored, gram = local_gram(basis)
    products = product(tiles, below, above, prepared, used_count, kinds)
    outgoing = products[3]
    below, above = lax.ppermute(outgoing, "gz", up), lax.ppermute(outgoing, "gz", down)
    own, shared = fold_z(products, below, above, map_z, nx * ny)
    hessian_vec, summary = fold(where, own, exchange(shared), raw, stored, gram, (nx, ny))
    summary = total_of(exchange(summary), nz)
    summary = lax.all_to_all(summary, "gz", 0, 0)
    entries = 3 * positions.shape[-1] * nx * ny * nz
    next_vector, correlations, vector_norm = finish(summary, hessian_vec, stored, positions.shape, entries)
    return next_vector, correlations[0, : basis.shape[0]], vector_norm[0, 0]


def solution(mesh):
    bricks = P("gx", "gy", "gz", None)
    lists = P("gx", "gy", "gz", None, None)
    vector = P(None, "gx", "gy", "gz", None)
    return jax.shard_map(
        on_device,
        mesh=mesh,
        in_specs=(vector, P(None, None, "gx", "gy", "gz", None), lists, bricks, bricks, lists, lists, lists) + (P(),) * 6,
        out_specs=(vector, P(), P()),
        check_vma=False,
    )
```

time: 333 us -> 119 us (0.36)
  the two profiles are of different devices: /device:TPU:8 before, /device:TPU:1 now
where the time goes in v1:
time: 119 us
  blocking collectives  33.5 us (28%)
  starting transfers between devices  33.3 us (28%)
  Pallas kernels  29.5 us (25%)
  waiting for transfers between devices  14.1 us (12%)
  local copies, waits for them, and re-layouts  6.92 us (6%)
    all_to_all x1, blocking collectives, on_device(): summary = lax.all_to_all(summary, 'gz', 0, 0)  21.2 us
    all_to_all x2, starting transfers between devices, exchange(): return lax.all_to_all(x, plane, 0, 0)  15.6 us
    all_to_all x2, waiting for transfers between devices, exchange(): return lax.all_to_all(x, plane, 0, 0)  13.4 us
    pallas_call x1, Pallas kernels, product(): pl.pallas_call(product_kernel, out_shape=jax.ShapeDtypeStruct((4, 8, 128)...  12.4 us
    all_to_all x1, blocking collectives, exchange(): return lax.all_to_all(x, plane, 0, 0)  12.4 us
    ppermute x1, starting transfers between devices, on_device(): lax.ppermute(message, 'gz', down)  9.25 us
    unnamed x13, local copies, waits for them, and re-layouts  5.13 us
    pallas_call x1, Pallas kernels, prepare(): pl.pallas_call(prepare_kernel, out_shape=[jax.ShapeDtypeStruct(s, d) for...  4.9 us
  transfers between devices with their start and end apart: 6, of which 3 were waited for; matrix products, arithmetic and copies ran while one was open for 3% of the time, Pallas kernels for 5%

profile of v1, /device:TPU:1, one launch (start us, length us, event | category | flops | bytes accessed | tf_op | source)
XLA Modules:
  0.0 118.7 jit_solution(11655210450049153910)
XLA Ops:
  0.6 1.5 %pack.1 = f32[32,8,128]{2,1,0:T(8,128)} custom-call(f32[3,1,1,1,128]{4,3,2,1,0:T(1,128)} %places.1, f32[30,3,1,1,1,128]{5,4,3,2,1,0:T(1,128)} %basis.1, s32[1,1,1,2,64]{4,3,2,1,0:T(2,128)} %map_x.1, s32[1,1,1,2,64]{4,3,2,1,0:T(2,128)} %map_y.1), custom_call_target="tpu_custom_call" | custom-call | tf_op jit(solution)/shard_map/pack/pallas_call | solution.py:376
  2.1 10.3 %all-to-all-start = ((f32[32,8,128]{2,1,0:T(8,128)}), f32[32,8,128]{2,1,0:T(8,128)S(1)}, u32[]{:S(2)}, u32[]{:S(2)}) async-start(f32[32,8,128]{2,1,0:T(8,128)} %pack.1), calls=%async_computation | async-start | bytes 262144 | tf_op jit(solution)/shard_map/all_to_all | solution.py:617
  12.4 0.6 pad_add_fusion.where
  13.0 7.2 %all-to-all-done.got.maps = f32[32,8,128]{2,1,0:T(8,128)S(1)} async-done(((f32[32,8,128]{2,1,0:T(8,128)}), f32[32,8,128]{2,1,0:T(8,128)S(1)}, u32[]{:S(2)}, u32[]{:S(2)}) %all-to-all-start) | async-done | bytes 131104 | tf_op jit(solution)/shard_map/all_to_all | solution.py:617
  20.2 0.0 copy-start
  20.2 0.7 copy-done
  20.9 1.8 %assemble.1 = (f32[3,8,128]{2,1,0:T(8,128)}, f32[8,128]{1,0:T(8,128)}) custom-call(s32[2]{0:T(128)} %pad_add_fusion.where, f32[32,8,128]{2,1,0:T(8,128)} %copy-done, s32[1,1,1,2,64]{4,3,2,1,0:T(2,128)} %map_z.3), custom_call_target="tpu_custom_call" | custom-call | tf_op jit(solution)/shard_map/assemble/pallas_call | solution.py:445
  22.7 1.9 %collective-permute-start = (f32[8,128]{1,0:T(8,128)}, f32[8,128]{1,0:T(8,128)S(1)}, u32[]{:S(2)}, u32[]{:S(2)}) collective-permute-start(f32[8,128]{1,0:T(8,128)} %get-tuple-element.25), channel_id=1, source_target_pairs={{0,1},{1,2},{2,3},{3,4},{4,5},{5,6},{6,7},{7,8},{8,9},{9,10},{10,1... | collective-permute-start | bytes 12296 | tf_op jit(solution)/shard_map/ppermute | solution.py:621
  24.6 9.2 %collective-permute-start.1 = (f32[8,128]{1,0:T(8,128)}, f32[8,128]{1,0:T(8,128)S(1)}, u32[]{:S(2)}, u32[]{:S(2)}) collective-permute-start(f32[8,128]{1,0:T(8,128)} %get-tuple-element.25), channel_id=1, source_target_pairs={{1,0},{2,1},{3,2},{4,3},{5,4},{6,5},{7,6},{8,7},{9,8},{10,9},{11,1... | collective-permute-start | bytes 12296 | tf_op jit(solution)/shard_map/ppermute | solution.py:621
  33.9 2.6 %copy.17.w1 = f32[1600,240]{1,0:T(8,128)} copy(f32[1600,240]{0,1:T(8,128)} %param.23) | data formatting | bytes 3072000 | tf_op args[9]
  36.5 4.9 %prepare.1 = (bf16[512,256]{1,0:T(8,128)(2,1)}, bf16[512,256]{1,0:T(8,128)(2,1)}, bf16[256,512]{1,0:T(8,128)(2,1)}, bf16[256,512]{1,0:T(8,128)(2,1)}, bf16[256,2...) custom-call(f32[2,16,100]{2,1,0:T(8,128)} %table.1, ...), custom_call_target="tpu_custom_call" | custom-call | tf_op jit(solution)/shard_map/prepare/pallas_call | solution.py:105
  41.4 0.0 collective-permute-done.below
  41.4 0.0 copy-start.2
  41.4 0.0 collective-permute-done.1.above
  41.4 0.0 copy-start.3
  41.4 0.6 copy-done.2
  42.0 0.0 copy-done.3
  42.0 12.4 %product.1.products = f32[4,8,128]{2,1,0:T(8,128)} custom-call(f32[3,8,128]{2,1,0:T(8,128)} %get-tuple-element.24.tiles, f32[8,128]{1,0:T(8,128)} %copy-done.2, f32[8,128]{1,0:T(8,128)} %copy-done.3, s32[128,128]{1,0:T(8,128)} %get-tuple-element.26.ids_t, s32[1,1,1,128]{3,2,1,0:T(1,128)} %counts.1, s32[1,1,1,128]{3,2,1,0:T(1,128)} %kinds.1, ...), custom_call_target="tpu_custom_call" | custom-call | tf_op jit(solution)/shard_map/product/pallas_call | solution.py:344
  54.4 0.7 slice_bitcast_fusion
  55.1 1.9 %collective-permute-start.2 = (f32[8,128]{1,0:T(8,128)S(1)}, f32[8,128]{1,0:T(8,128)S(1)}, u32[]{:S(2)}, u32[]{:S(2)}) collective-permute-start(f32[8,128]{1,0:T(8,128)S(1)} %slice_bitcast_fusion), channel_id=1, source_target_pairs={{0,1},{1,2},{2,3},{3,4},{4,5},{5,6},{6,7},{7,8},{8,9},{9,10},{10,1... | collective-permute-start | bytes 12296 | tf_op jit(solution)/shard_map/ppermute | solution.py:626
  57.0 4.6 %collective-permute-start.3 = (f32[8,128]{1,0:T(8,128)S(1)}, f32[8,128]{1,0:T(8,128)S(1)}, u32[]{:S(2)}, u32[]{:S(2)}) collective-permute-start(f32[8,128]{1,0:T(8,128)S(1)} %slice_bitcast_fusion), channel_id=1, source_target_pairs={{1,0},{2,1},{3,2},{4,3},{5,4},{6,5},{7,6},{8,7},{9,8},{10,9},{11,1... | collective-permute-start | bytes 12296 | tf_op jit(solution)/shard_map/ppermute | solution.py:626
  61.6 0.0 collective-permute-done.2.below
  61.6 0.0 copy-start.4
  61.6 0.7 collective-permute-done.3.above
  62.4 0.0 copy-done.4
  62.4 0.0 copy-start.5
  62.4 0.6 copy-done.5
  63.0 1.6 %fold_z.1 = (f32[8,128]{1,0:T(8,128)}, f32[32,8,128]{2,1,0:T(8,128)}) custom-call(f32[4,8,128]{2,1,0:T(8,128)} %product.1.products, f32[8,128]{1,0:T(8,128)} %copy-done.4, f32[8,128]{1,0:T(8,128)} %copy-done.5, s32[1,1,1,2,64]{4,3,2,1,0:T(2,128)} %map_z.3), custom_call_target="tpu_custom_call" | custom-call | tf_op jit(solution)/shard_map/fold_z/pallas_call | solution.py:481
  64.6 5.3 %all-to-all-start.1 = ((f32[32,8,128]{2,1,0:T(8,128)}), f32[32,8,128]{2,1,0:T(8,128)S(1)}, u32[]{:S(2)}, u32[]{:S(2)}) async-start(f32[32,8,128]{2,1,0:T(8,128)} %get-tuple-element.37), calls=%async_computation.1 | async-start | bytes 262144 | tf_op jit(solution)/shard_map/all_to_all | solution.py:617
  69.9 1.6 %gram.1 = (f32[3,32,128]{2,1,0:T(8,128)}, f32[32,128]{1,0:T(8,128)}) custom-call(f32[30,3,1,1,1,128]{5,4,3,2,1,0:T(1,128)} %basis.1), custom_call_target="tpu_custom_call" | custom-call | tf_op jit(solution)/shard_map/gram/pallas_call | solution.py:503
  71.5 6.2 %all-to-all-done.1.got = f32[32,8,128]{2,1,0:T(8,128)S(1)} async-done(((f32[32,8,128]{2,1,0:T(8,128)}), f32[32,8,128]{2,1,0:T(8,128)S(1)}, u32[]{:S(2)}, u32[]{:S(2)}) %all-to-all-start.1) | async-done | bytes 131104 | tf_op jit(solution)/shard_map/all_to_all | solution.py:617
  77.7 0.0 copy-start.1
  77.7 0.6 copy-done.1
  78.3 2.5 %fold.1 = (f32[8,128]{1,0:T(8,128)}, f32[32,8,128]{2,1,0:T(8,128)}) custom-call(s32[2]{0:T(128)} %pad_add_fusion.where, f32[8,128]{1,0:T(8,128)} %get-tuple-element.36.own, f32[32,8,128]{2,1,0:T(8,128)} %copy-done.1, f32[32,8,128]{2,1,0:T(8,128)} %copy-done, f32[3,32,128]{2,1,0:T(8,128)} %get-tuple-element.38.stored, f32[32,128]{1,0:T(8,128)} %get-tuple-element.39.gram), custom_call_target="tpu_custom_call" | custom-call | tf_op jit(solution)/shard_map/fold/pallas_call | solution.py:552
  80.8 12.4 %all_to_all.20.got = f32[32,8,128]{2,1,0:T(8,128)} all-to-all(f32[32,8,128]{2,1,0:T(8,128)} %get-tuple-element.40), channel_id=1, replica_groups=mesh['gx'=4,'gy'=8,'gz'=16] {'gx','gy'}, dimensions={0} | all-to-all | bytes 262144 | tf_op jit(solution)/shard_map/all_to_all | solution.py:617
  93.2 1.6 %total.1 = f32[16,8,128]{2,1,0:T(8,128)} custom-call(f32[32,8,128]{2,1,0:T(8,128)} %all_to_all.20.got), custom_call_target="tpu_custom_call" | custom-call | tf_op jit(solution)/shard_map/total/pallas_call | solution.py:566
  94.7 21.2 %all_to_all.21.got = f32[16,8,128]{2,1,0:T(8,128)} all-to-all(f32[16,8,128]{2,1,0:T(8,128)} %total.1), channel_id=1, replica_groups=mesh['gx'=4,'gy'=8,'gz'=16] {'gz'}, dimensions={0} | all-to-all | bytes 131072 | tf_op jit(solution)/shard_map/all_to_all | solution.py:630
  115.9 1.7 %finish.1 = (f32[3,1,1,1,128]{4,3,2,1,0:T(1,128)}, f32[1,128]{1,0:T(1,128)}, f32[1,1]{1,0:T(1,128)}) custom-call(f32[16,8,128]{2,1,0:T(8,128)} %all_to_all.21.got, f32[8,128]{1,0:T(8,128)} %get-tuple-element.41.product, f32[3,32,128]{2,1,0:T(8,128)} %get-tuple-element.38.stored), custom_call_target="tpu_custom_call" | custom-call | tf_op jit(solution)/shard_map/finish/pallas_call | solution.py:596
  117.5 1.1 slice_bitcast_fusion.1
Async XLA Ops:
  2.1 18.1 %all-to-all-start = ((f32[32,8,128]{2,1,0:T(8,128)}), f32[32,8,128]{2,1,0:T(8,128)S(1)}, u32[]{:S(2)}, u32[]{:S(2)}) async-start(f32[32,8,128]{2,1,0:T(8,128)} %pack.1), calls=%async_computation | async-start | bytes 262144 | tf_op jit(solution)/shard_map/all_to_all | solution.py:617
  20.2 0.7 copy-start
  22.7 18.7 %collective-permute-start = (f32[8,128]{1,0:T(8,128)}, f32[8,128]{1,0:T(8,128)S(1)}, u32[]{:S(2)}, u32[]{:S(2)}) collective-permute-start(f32[8,128]{1,0:T(8,128)} %get-tuple-element.25), channel_id=1, source_target_pairs={{0,1},{1,2},{2,3},{3,4},{4,5},{5,6},{6,7},{7,8},{8,9},{9,10},{10,1... | collective-permute-start | bytes 12296 | tf_op jit(solution)/shard_map/ppermute | solution.py:621
  24.6 16.8 %collective-permute-start.1 = (f32[8,128]{1,0:T(8,128)}, f32[8,128]{1,0:T(8,128)S(1)}, u32[]{:S(2)}, u32[]{:S(2)}) collective-permute-start(f32[8,128]{1,0:T(8,128)} %get-tuple-element.25), channel_id=1, source_target_pairs={{1,0},{2,1},{3,2},{4,3},{5,4},{6,5},{7,6},{8,7},{9,8},{10,9},{11,1... | collective-permute-start | bytes 12296 | tf_op jit(solution)/shard_map/ppermute | solution.py:621
  41.4 0.6 copy-start.2
  41.4 0.6 copy-start.3
  55.1 6.5 %collective-permute-start.2 = (f32[8,128]{1,0:T(8,128)S(1)}, f32[8,128]{1,0:T(8,128)S(1)}, u32[]{:S(2)}, u32[]{:S(2)}) collective-permute-start(f32[8,128]{1,0:T(8,128)S(1)} %slice_bitcast_fusion), channel_id=1, source_target_pairs={{0,1},{1,2},{2,3},{3,4},{4,5},{5,6},{6,7},{7,8},{8,9},{9,10},{10,1... | collective-permute-start | bytes 12296 | tf_op jit(solution)/shard_map/ppermute | solution.py:626
  57.0 5.3 %collective-permute-start.3 = (f32[8,128]{1,0:T(8,128)S(1)}, f32[8,128]{1,0:T(8,128)S(1)}, u32[]{:S(2)}, u32[]{:S(2)}) collective-permute-start(f32[8,128]{1,0:T(8,128)S(1)} %slice_bitcast_fusion), channel_id=1, source_target_pairs={{1,0},{2,1},{3,2},{4,3},{5,4},{6,5},{7,6},{8,7},{9,8},{10,9},{11,1... | collective-permute-start | bytes 12296 | tf_op jit(solution)/shard_map/ppermute | solution.py:626
  61.6 0.7 copy-start.4
  62.4 0.6 copy-start.5
  64.6 13.1 %all-to-all-start.1 = ((f32[32,8,128]{2,1,0:T(8,128)}), f32[32,8,128]{2,1,0:T(8,128)S(1)}, u32[]{:S(2)}, u32[]{:S(2)}) async-start(f32[32,8,128]{2,1,0:T(8,128)} %get-tuple-element.37), calls=%async_computation.1 | async-start | bytes 262144 | tf_op jit(solution)/shard_map/all_to_all | solution.py:617
  77.7 0.6 copy-start.1

commit v2 on v1

--- a/solution.py
+++ b/solution.py
@@ -36,48 +36,71 @@
     return lax.broadcasted_iota(jnp.int32, shape, dim)
 
 
-def prepare_kernel(table, w1, w2, b1, b2, wo, ids, u_hi, u_lo, ut_hi, ut_lo, w2_hi, w2_lo, w2t_hi, w2t_lo, cols, ids_t, ws, ys, us, pad):
+def halves(ref):
+    return jnp.concatenate([ref[0, 0, 0, 0:1, :], ref[0, 0, 0, 1:2, :]], axis=1)
+
+
+def fetch(sources, places, semaphores):
+    copies = [pltpu.make_async_copy(x, y, semaphores.at[i]) for i, (x, y) in enumerate(zip(sources, places))]
+    for copy in copies:
+        copy.start()
+    return copies
+
+
+EXACT = dict(precision=lax.Precision.HIGHEST, preferred_element_type=F32)
+
+
+def mixing_kernel(table_at, w1_at, map_at, u_hi, u_lo, ut_hi, ut_lo, map_row, table, w1t, map_z, outer, inner, k_hi, k_lo, semaphores):
+    copies = fetch((table_at, map_at, w1_at), (table, map_z, w1t), semaphores)
     types, levels, width = table.shape
-    hidden = w1.shape[1]
-    inner = levels * levels
-    m2 = w1.shape[0] // width
-    rest = hidden - 128
-    tall = split(table[...].reshape(types * levels, width))
-    ws[0] = w1[:, 0:128]
-    ws[1] = jnp.zeros_like(ws[1])
-    ws[1, :, 0:rest] = w1[:, 128:hidden]
-    for j in range(m2):
-        column = jnp.concatenate([ws[0, pl.ds(j, width, stride=m2), :], ws[1, pl.ds(j, width, stride=m2), :]], axis=1)
-        part = dot3(tall, column)
-        for t in range(types):
-            for half in range(2):
-                ys[t, half, pl.ds(j, levels, stride=m2), :] = part[t * levels : (t + 1) * levels, half * 128 : (half + 1) * 128]
-    r = rows_of((inner, levels))
-    spread = (r % levels == rows_of((inner, levels), 1)).astype(BF16)
-    r = rows_of((m2, levels * m2), 1)
-    tile = (r % m2 == rows_of((m2, levels * m2))).astype(BF16)
-    same = rows_of((inner, levels * m2)) // levels == rows_of((inner, levels * m2), 1) // m2
-    for t in range(types):
-        th, tl = split(table[t][:, 0:m2])
-        kh = mm(mm(spread, th).astype(BF16), tile)
-        kl = mm(mm(spread, tl).astype(BF16), tile)
-        kron = (jnp.where(same, kh, 0.0).astype(BF16), jnp.where(same, kl, 0.0).astype(BF16))
-        for half in range(2):
-            us[half, t * inner : (t + 1) * inner, :] = dot3(kron, ys[t, half])
-    for t in range(types):
-        for k in range(levels):
-            at = t * inner + k * levels
-            for half in range(2):
-                block = us[half, at : at + levels, :]
-                other = us[half, pl.ds(t * inner + k, levels, stride=levels), :]
-                hi, lo = split(0.5 * (block + other))
-                u_hi[at : at + levels, half * 128 : (half + 1) * 128] = hi
-                u_lo[at : at + levels, half * 128 : (half + 1) * 128] = lo
-    full = u_hi[...].astype(F32) + u_lo[...].astype(F32)
-    hi, lo = split(full.T)
+    hidden = w1t.shape[0]
+    m2 = w1t.shape[1] // width
+    count = types * levels * levels
+    copies[0].wait()
+    tall = table[...].reshape(types * levels, width)
+    tall = jnp.concatenate([tall, jnp.zeros((types * levels, 128 - width), F32)], axis=1)
+    tall = jnp.concatenate([tall, jnp.zeros((128 - types * levels, 128), F32)], axis=0).T
+    column = rows_of((128, count), 1)
+    row = rows_of((128, count))
+    kind = column // (levels * levels)
+    first = jnp.where(row == kind * levels + (column // levels) % levels, 1.0, 0.0)
+    second = jnp.where(row == kind * levels + column % levels, 1.0, 0.0)
+    outer[...] = jnp.dot(tall, first, **EXACT) * 0.5
+    inner[...] = jnp.dot(tall, second, **EXACT) * 0.5
+    near = inner[0:m2, :] * 2.0
+    far = outer[0:m2, :] * 2.0
+
+    def kron(m, carry):
+        value = jnp.broadcast_to(outer[pl.ds(m, 1), :], (m2, count)) * near + jnp.broadcast_to(inner[pl.ds(m, 1), :], (m2, count)) * far
+        hi, lo = split(value)
+        at = pl.ds(pl.multiple_of(m * m2, m2), m2)
+        k_hi[at, :] = hi
+        k_lo[at, :] = lo
+        return carry
+
+    lax.fori_loop(0, width, kron, 0, unroll=4)
+    copies[1].wait()
+    map_row[...] = halves(map_z)
+    copies[2].wait()
+    full = dot3(w1t[...], (k_hi[...], k_lo[...]))
+    full = jnp.concatenate([full, jnp.zeros((256 - hidden, count), F32)], axis=0)
+    hi, lo = split(full)
     ut_hi[...] = hi
     ut_lo[...] = lo
+    hi, lo = split(full.T)
+    u_hi[...] = hi
+    u_lo[...] = lo
+
+
+def lists_kernel(w2_at, b1_at, b2_at, wo_at, ids_at, counts_at, kinds_at, basis_at, w2_hi, w2_lo, w2t_hi, w2t_lo, cols, ids_t, count_row, kind_row, stored, gram, w2, b1, b2, wo, ids, counts, kinds, basis, pad, semaphores):
+    places = (w2, b1, b2, wo, ids, counts, kinds, basis)
+    copies = fetch((w2_at, b1_at, b2_at, wo_at, ids_at, counts_at, kinds_at, basis_at), places, semaphores)
+    hidden = w2.shape[0]
     pad[...] = jnp.zeros_like(pad)
+    stored[...] = jnp.zeros_like(stored)
+    gram[...] = jnp.zeros_like(gram)
+    for copy in copies:
+        copy.wait()
     pad[0:hidden, 0:hidden] = w2[...]
     hi, lo = split(pad[...])
     w2_hi[...] = hi
@@ -85,36 +108,57 @@
     hi, lo = split(pad[...].T)
     w2t_hi[...] = hi
     w2t_lo[...] = lo
-    pad[...] = jnp.zeros_like(pad)
+    pad[0:128, :] = jnp.zeros((128, pad.shape[1]), F32)
     pad[0:1, 0:hidden] = b1[...]
     pad[1:2, 0:hidden] = b2[...]
     pad[2:3, 0:hidden] = wo[...]
     cols[...] = pad[0:128, :].T
     ids_t[...] = ids[0, 0, 0].astype(F32).T.astype(jnp.int32)
+    count_row[...] = counts[0, 0]
+    kind_row[...] = kinds[0, 0]
+    total = jnp.zeros((32, 32), F32)
+    for c in range(3):
+        for k in range(basis.shape[0]):
+            stored[c, k : k + 1, :] = basis[k, c, 0, 0]
+        total = total + lax.dot_general(stored[c], stored[c], NT, **EXACT)
+    gram[:, 0:32] = total
 
 
 def vmem(n):
     return [pl.BlockSpec(memory_space=pltpu.VMEM)] * n
 
 
-def prepare(table, w1, w2, b1, b2, wo, ids):
-    n = ids.shape[-1]
+def here(*arrays):
+    return [pltpu.with_memory_space_constraint(a, pltpu.VMEM) for a in arrays]
+
+
+def from_hbm(kernel, name, shapes, scratch, *arrays):
+    return pl.pallas_call(
+        kernel,
+        out_shape=[pltpu.VMEM(s, d) for s, d in shapes],
+        in_specs=[pl.BlockSpec(memory_space=pltpu.HBM)] * len(arrays),
+        out_specs=vmem(len(shapes)),
+        scratch_shapes=[pltpu.VMEM(a.shape, a.dtype) for a in arrays] + scratch + [pltpu.SemaphoreType.DMA((len(arrays),))],
+        name=name,
+    )(*(pltpu.with_memory_space_constraint(a, pltpu.HBM) for a in arrays))
+
+
+def mixing(table, w1, map_z):
     hp = 256
-    inner = table.shape[0] * table.shape[1] ** 2
-    shapes = [((inner, hp), BF16)] * 2 + [((hp, inner), BF16)] * 2 + [((hp, hp), BF16)] * 4 + [((hp, 128), F32), ((n, 128), jnp.int32)]
-    return pl.pallas_call(
-        prepare_kernel,
-        out_shape=[jax.ShapeDtypeStruct(s, d) for s, d in shapes],
-        in_specs=vmem(7),
-        out_specs=vmem(len(shapes)),
-        scratch_shapes=[
-            pltpu.VMEM((2, w1.shape[0], 128), F32),
-            pltpu.VMEM((table.shape[0], 2, inner // table.shape[0], 128), F32),
-            pltpu.VMEM((2, inner, 128), F32),
-            pltpu.VMEM((hp, hp), F32),
-        ],
-        name="prepare",
-    )(table, w1, w2, b1[None], b2[None], wo[None], ids)
+    count = table.shape[0] * table.shape[1] ** 2
+    shapes = [((count, hp), BF16)] * 2 + [((hp, count), BF16)] * 2 + [((1, 128), jnp.int32)]
+    scratch = [pltpu.VMEM((128, count), F32)] * 2 + [pltpu.VMEM((w1.shape[0], count), BF16)] * 2
+    *weights, map_row = from_hbm(mixing_kernel, "mixing", shapes, scratch, table, w1.T, map_z)
+    return weights, map_row
+
+
+def lists_of(w2, b1, b2, wo, ids, counts, kinds, basis):
+    hp = 256
+    row = ((1, 128), jnp.int32)
+    shapes = [((hp, hp), BF16)] * 4 + [((hp, 128), F32), ((ids.shape[-1], 128), jnp.int32), row, row, ((3, 32, 128), F32), ((32, 128), F32)]
+    scratch = [pltpu.VMEM((hp, hp), F32)]
+    done = from_hbm(lists_kernel, "lists", shapes, scratch, w2, b1[None], b2[None], wo[None], ids, counts, kinds, basis)
+    return done[:5], done[5:8], done[8], done[9]
 
 
 def shifted_ghosts(below, above, coord, rows):
@@ -123,21 +167,21 @@
     return jnp.where(lower, below - step, above + step)
 
 
-def product_kernel(tiles, below, above, ids_t, counts, kinds, u_hi, u_lo, ut_hi, ut_lo, w2_hi, w2_lo, w2t_hi, w2t_lo, cols, out, xv, edge, phis, acc, pairs, grads, force, lows):
+def product_kernel(tiles, below, above, ids_t, counts, kinds, u_hi, u_lo, ut_hi, ut_lo, w2_hi, w2_lo, w2t_hi, w2t_lo, cols, out, sent, xv, edge, phis, acc, pairs, grads, force, lows):
     n_slots = ids_t.shape[0]
     levels = 16
     gap = levels - 1
     blocks = n_slots // 8
     xv[0:3] = tiles[...]
     xv[3] = shifted_ghosts(pltpu.roll(below[...], 64, 1), pltpu.roll(above[...], 64, 1), 2, 8)
-    count_row = jnp.broadcast_to(counts[0, 0], (8, 128))
+    count_row = jnp.broadcast_to(counts[...], (8, 128))
 
     def geometry(nb, carry):
         rows = pl.ds(pl.multiple_of(nb * 8, 8), 8)
         index = ids_t[rows, :]
         low = index & 127
         high = index >> 7
-        lows[rows, :] = low.astype(F32)
+        lows[rows, :] = (index & 63).astype(F32)
         near = []
         for f in range(6):
             picks = [lane_pick(jnp.broadcast_to(xv[q, f : f + 1, :], (8, 128)), low) for q in range(4)]
@@ -170,7 +214,7 @@
         edge[18, rows, :] = rate
         return carry
 
-    lax.fori_loop(0, blocks, geometry, 0)
+    lax.fori_loop(0, blocks, geometry, 0, unroll=2)
 
     def pooling(kk, carry):
         sums = [[jnp.zeros((8, 128), F32) for _ in range(8)] for _ in range(2)]
@@ -199,7 +243,7 @@
         pooled = pooled + acc[pl.ds(s, 128, stride=8), :]
     pooled = pooled * (1.0 / n_slots)
     grads[...] = pooled
-    second = jnp.broadcast_to(kinds[0, 0], (16, 128)) == 1
+    second = jnp.broadcast_to(kinds[...], (16, 128)) == 1
     p = [pooled[a * 16 : (a + 1) * 16] for a in range(4)]
     dp = [pooled[64 + a * 16 : 64 + (a + 1) * 16] for a in range(4)]
     for k in range(levels):
@@ -305,47 +349,46 @@
         return tuple(result)
 
     zero = jnp.zeros((8, 128), F32)
-    centre = lax.fori_loop(0, blocks, backward, (zero, zero, zero))
+    centre = lax.fori_loop(0, blocks, backward, (zero, zero, zero), unroll=2)
     row8 = rows_of((8, 128))
-    quarter = row8 & 3
-    upper = row8 < 4
-    rows16 = [(rows_of((16, 128)) + 16 * rg).astype(F32).astype(BF16) for rg in range(8)]
+    rows16 = [(rows_of((16, 128)) + 16 * rg).astype(F32).astype(BF16) for rg in range(4)]
+    on = jnp.ones((16, 128), BF16)
+    off = jnp.zeros((16, 128), BF16)
     chunk = 8
 
     def scatter(step, total):
         lefts, hots = [], []
         for i in range(chunk):
             n = step * chunk + i
-            high = jnp.broadcast_to(ids_t[pl.ds(n, 1), :], (8, 128)) >> 7
-            here = high == quarter
-            stack = [
-                jnp.where(here, jnp.where(upper, jnp.broadcast_to(force[c, pl.ds(n, 1), :], (8, 128)), jnp.broadcast_to(force[3 + c, pl.ds(n, 1), :], (8, 128))), 0.0)
-                for c in range(3)
-            ]
+            hit = (jnp.broadcast_to(ids_t[pl.ds(n, 1), :], (8, 128)) >> 6) == row8
+            stack = [jnp.where(hit, jnp.broadcast_to(force[c, pl.ds(n, 1), :], (8, 128)), 0.0) for c in range(6)]
             lefts.append(jnp.concatenate(stack, axis=0).astype(BF16))
             low = jnp.broadcast_to(lows[pl.ds(n, 1), :], (16, 128)).astype(BF16)
-            hots.append(jnp.concatenate([jnp.where(low == r, 1.0, 0.0).astype(BF16) for r in rows16], axis=0))
+            hots.append(jnp.concatenate([jnp.where(low == r, on, off) for r in rows16], axis=0))
         return total + lax.dot_general(jnp.concatenate(lefts, axis=1), jnp.concatenate(hots, axis=1), NT, preferred_element_type=F32)
 
-    total = lax.fori_loop(0, n_slots // chunk, scatter, jnp.zeros((24, 128), F32))
+    total = lax.fori_loop(0, n_slots // chunk, scatter, jnp.zeros((48, 64), F32), unroll=2)
     out[...] = jnp.zeros_like(out)
+    sent[...] = jnp.zeros_like(sent)
     for c in range(3):
-        both = total[c * 8 : c * 8 + 4] + total[c * 8 + 4 : c * 8 + 8]
+        both = total[c * 8 : c * 8 + 8] + total[24 + c * 8 : 32 + c * 8]
         for q in range(4):
-            row = both[q : q + 1]
+            row = jnp.concatenate([both[2 * q : 2 * q + 1], both[2 * q + 1 : 2 * q + 2]], axis=1)
             if q == 0:
                 row = row - jnp.sum(centre[c], axis=0, keepdims=True)
-            out[q, c : c + 1, :] = row
-
-
-def product(tiles, below, above, prepared, counts, kinds):
-    *weights, ids_t = prepared
-    n = ids_t.shape[0]
+            if q < 3:
+                out[q, c : c + 1, :] = row
+            else:
+                sent[c : c + 1, :] = row
+
+
+def product(tiles, below, above, lists, weights):
+    n = lists[0].shape[0]
     return pl.pallas_call(
         product_kernel,
-        out_shape=jax.ShapeDtypeStruct((4, 8, 128), F32),
+        out_shape=[pltpu.VMEM((3, 8, 128), F32), pltpu.VMEM((8, 128), F32)],
         in_specs=vmem(15),
-        out_specs=vmem(1)[0],
+        out_specs=vmem(2),
         scratch_shapes=[
             pltpu.VMEM((4, 8, 128), F32),
             pltpu.VMEM((19, n, 128), F32),
@@ -357,11 +400,7 @@
             pltpu.VMEM((n, 128), F32),
         ],
         name="product",
-    )(tiles, below, above, ids_t, counts, kinds, *weights)
-
-
-def halves(ref):
-    return jnp.concatenate([ref[0, 0, 0, 0:1, :], ref[0, 0, 0, 1:2, :]], axis=1)
+    )(*here(tiles, below, above, *lists, *weights))
 
 
 def pack_kernel(places, tangent, map_x, map_y, out):
@@ -376,24 +415,25 @@
     return pl.pallas_call(
         pack_kernel,
         grid=(1,),
-        out_shape=jax.ShapeDtypeStruct((bricks, 8, 128), F32),
+        out_shape=pltpu.VMEM((bricks, 8, 128), F32),
         in_specs=[
             whole(positions),
             pl.BlockSpec((1,) + basis.shape[1:], lambda i: (last,) + (0,) * (basis.ndim - 1)),
             whole(map_x),
             whole(map_y),
         ],
-        out_specs=pl.BlockSpec((bricks, 8, 128), lambda i: (0, 0, 0)),
+        out_specs=vmem(1)[0],
         name="pack",
     )(positions, basis, map_x, map_y)
 
 
-def brick_reader(where, grid):
+def brick_reader(grid):
     nx, ny = grid
+    px, py = lax.axis_index("gx"), lax.axis_index("gy")
 
     def at(ref, dx, dy):
-        x = lax.rem(where[0] + (dx + nx), nx)
-        y = lax.rem(where[1] + (dy + ny), ny)
+        x = lax.rem(px + (dx + nx), nx)
+        y = lax.rem(py + (dy + ny), ny)
         return ref[x * ny + y]
 
     return at
@@ -407,8 +447,8 @@
     return pltpu.roll(x, 64, 1)
 
 
-def assemble_kernel(grid, where, got, map_z, tiles, message):
-    at = brick_reader(where, grid)
+def assemble_kernel(grid, got, map_z, tiles, message):
+    at = brick_reader(grid)
     lower = rows_of((8, 128), 1) < 64
     row = rows_of((8, 128))
     step_x = jnp.where(row == 0, 1.0, 0.0)
@@ -430,25 +470,21 @@
     tiles[0] = middle[0]
     tiles[1] = ghosts[0]
     tiles[2] = third
-    chosen = jnp.broadcast_to(halves(map_z), (8, 128))
+    chosen = jnp.broadcast_to(map_z[...], (8, 128))
     low = chosen & 127
     message[...] = jnp.where(
         chosen < 128, lane_pick(middle[0], low), jnp.where(chosen < 256, lane_pick(ghosts[0], low), lane_pick(third, low))
     )
 
 
-def smem():
-    return [pl.BlockSpec(memory_space=pltpu.SMEM)]
-
-
-def assemble(where, got, map_z, grid):
+def assemble(got, map_z, grid):
     return pl.pallas_call(
         functools.partial(assemble_kernel, grid),
-        out_shape=[jax.ShapeDtypeStruct((3, 8, 128), F32), jax.ShapeDtypeStruct((8, 128), F32)],
-        in_specs=smem() + vmem(2),
+        out_shape=[pltpu.VMEM((3, 8, 128), F32), pltpu.VMEM((8, 128), F32)],
+        in_specs=vmem(2),
         out_specs=vmem(2),
         name="assemble",
-    )(where, got, map_z)
+    )(*here(got, map_z))
 
 
 def thirds(x):
@@ -469,7 +505,7 @@
 def fold_z_kernel(products, below, above, map_z, own, out):
     lower = rows_of((8, 128), 1) < 64
     value = jnp.where(lower, turn(below[...]), turn(above[...]))
-    added = spread_columns(value, halves(map_z), 384, 0)
+    added = spread_columns(value, map_z[...], 384, 0)
     own[...] = products[0] + added[:, 0:128]
     first = products[1] + added[:, 128:256]
     second = products[2] + added[:, 256:384]
@@ -480,37 +516,15 @@
 def fold_z(products, below, above, map_z, bricks):
     return pl.pallas_call(
         fold_z_kernel,
-        out_shape=[jax.ShapeDtypeStruct((8, 128), F32), jax.ShapeDtypeStruct((bricks, 8, 128), F32)],
+        out_shape=[pltpu.VMEM((8, 128), F32), pltpu.VMEM((bricks, 8, 128), F32)],
         in_specs=vmem(4),
         out_specs=vmem(2),
         name="fold_z",
-    )(products, below, above, map_z)
-
-
-def gram_kernel(basis, stored, gram):
-    count = basis.shape[0]
-    stored[...] = jnp.zeros_like(stored)
-    total = jnp.zeros((32, 32), F32)
-    for c in range(3):
-        for k in range(count):
-            stored[c, k : k + 1, :] = basis[k, c, 0, 0]
-        total = total + lax.dot_general(stored[c], stored[c], NT, precision=lax.Precision.HIGHEST, preferred_element_type=F32)
-    gram[...] = jnp.zeros_like(gram)
-    gram[:, 0:32] = total
-
-
-def local_gram(basis):
-    return pl.pallas_call(
-        gram_kernel,
-        out_shape=[jax.ShapeDtypeStruct((3, 32, 128), F32), jax.ShapeDtypeStruct((32, 128), F32)],
-        in_specs=vmem(1),
-        out_specs=vmem(2),
-        name="gram",
-    )(basis)
-
-
-def fold_kernel(grid, where, own, got, maps, stored, gram, product, out):
-    at = brick_reader(where, grid)
+    )(*here(products, below, above, map_z))
+
+
+def fold_kernel(grid, own, got, maps, stored, gram, product, out):
+    at = brick_reader(grid)
     lower = rows_of((8, 128), 1) < 64
 
     def from_y(dx):
@@ -548,14 +562,14 @@
     out[...] = jnp.broadcast_to(tile[None], out.shape)
 
 
-def fold(where, own, got, maps, stored, gram, grid):
+def fold(own, got, maps, stored, gram, grid):
     return pl.pallas_call(
         functools.partial(fold_kernel, grid),
-        out_shape=[jax.ShapeDtypeStruct((8, 128), F32), jax.ShapeDtypeStruct(got.shape, F32)],
-        in_specs=smem() + vmem(5),
+        out_shape=[pltpu.VMEM((8, 128), F32), pltpu.VMEM(got.shape, F32)],
+        in_specs=vmem(5),
         out_specs=vmem(2),
         name="fold",
-    )(where, own, got, maps, stored, gram)
+    )(*here(own, got, maps, stored, gram))
 
 
 def total_kernel(got, out):
@@ -565,15 +579,15 @@
 def total_of(got, copies):
     return pl.pallas_call(
         total_kernel,
-        out_shape=jax.ShapeDtypeStruct((copies,) + got.shape[1:], F32),
+        out_shape=pltpu.VMEM((copies,) + got.shape[1:], F32),
         in_specs=vmem(1),
         out_specs=vmem(1)[0],
         name="total",
-    )(got)
+    )(*here(got))
 
 
 def finish_kernel(entries, got, product, stored, result, correlations, norm):
-    count = correlations.shape[1] - 98
+    count = correlations.shape[1]
     packed = jnp.sum(got[...], axis=0) * (1.0 / entries)
     full = jnp.concatenate([packed] + [pltpu.roll(packed, 128 - 32 * b, 1) for b in range(1, 4)], axis=0)
     column = full[:, count : count + 1]
@@ -585,52 +599,53 @@
     square = jnp.sum(jnp.where(rows_of((32, 128), 1) <= count, full * across * down, 0.0), axis=1, keepdims=True)
     length = jnp.sqrt(jnp.maximum(jnp.sum(square, axis=0, keepdims=True), 0.0) + 1e-06)
     norm[...] = length
-    correlations[...] = line
+    correlations[...] = line[:, 0:count]
     share = jnp.where(row < count, column, 0.0)
     for c in range(3):
         taken = jnp.sum(stored[c] * share, axis=0, keepdims=True)
         result[c, 0, 0] = (product[c : c + 1, :] - taken) / length
 
 
-def finish(got, product, stored, shape, entries):
+def finish(got, product, stored, shape, count, entries):
     return pl.pallas_call(
         functools.partial(finish_kernel, entries),
         out_shape=[
             jax.ShapeDtypeStruct(shape, F32),
-            jax.ShapeDtypeStruct((1, 128), F32),
+            jax.ShapeDtypeStruct((1, count), F32),
             jax.ShapeDtypeStruct((1, 1), F32),
         ],
         in_specs=vmem(3),
         out_specs=vmem(3),
         name="finish",
-    )(got, product, stored)
+    )(*here(got, product, stored))
 
 
 def on_device(positions, basis, neighbours, used_count, kinds, map_x, map_y, map_z, table, fit_w1, fit_b1, fit_w2, fit_b2, fit_out):
     nx, ny, nz = (lax.axis_size(a) for a in ("gx", "gy", "gz"))
     plane = ("gx", "gy")
-    where = jnp.stack([lax.axis_index("gx"), lax.axis_index("gy")]).astype(jnp.int32)
     up = [(i, (i + 1) % nz) for i in range(nz)]
     down = [(j, i) for i, j in up]
 
     def exchange(x):
         return lax.all_to_all(x, plane, 0, 0)
 
-    raw = exchange(pack(positions, basis, map_x, map_y, nx * ny))
-    tiles, message = assemble(where, raw, map_z, (nx, ny))
+    packed = pack(positions, basis, map_x, map_y, nx * ny)
+    raw = exchange(packed)
+    table, _ = lax.optimization_barrier((table, packed))
+    mixed, map_row = mixing(table, fit_w1, map_z)
+    layers, lists, stored, gram = lists_of(fit_w2, fit_b1, fit_b2, fit_out, neighbours, used_count, kinds, basis)
+    raw, map_row = lax.optimization_barrier((raw, map_row))
+    tiles, message = assemble(raw, map_row, (nx, ny))
     below, above = lax.ppermute(message, "gz", up), lax.ppermute(message, "gz", down)
-    prepared = prepare(table, fit_w1, fit_w2, fit_b1, fit_b2, fit_out, neighbours)
-    stored, gram = local_gram(basis)
-    products = product(tiles, below, above, prepared, used_count, kinds)
-    outgoing = products[3]
+    products, outgoing = product(tiles, below, above, lists, (*mixed, *layers))
     below, above = lax.ppermute(outgoing, "gz", up), lax.ppermute(outgoing, "gz", down)
-    own, shared = fold_z(products, below, above, map_z, nx * ny)
-    hessian_vec, summary = fold(where, own, exchange(shared), raw, stored, gram, (nx, ny))
+    own, shared = fold_z(products, below, above, map_row, nx * ny)
+    hessian_vec, summary = fold(own, exchange(shared), raw, stored, gram, (nx, ny))
     summary = total_of(exchange(summary), nz)
     summary = lax.all_to_all(summary, "gz", 0, 0)
     entries = 3 * positions.shape[-1] * nx * ny * nz
-    next_vector, correlations, vector_norm = finish(summary, hessian_vec, stored, positions.shape, entries)
-    return next_vector, correlations[0, : basis.shape[0]], vector_norm[0, 0]
+    next_vector, correlations, vector_norm = finish(summary, hessian_vec, stored, positions.shape, basis.shape[0], entries)
+    return next_vector, correlations.reshape(-1), vector_norm.reshape(())
 
 
 def solution(mesh):

time: 119 us -> 94.9 us (0.80)
  Pallas kernels: 29.5 us -> 16.6 us
  blocking collectives: 33.5 us -> 41.6 us
  local copies, waits for them, and re-layouts: 6.92 us -> 0 us
  starting transfers between devices: 33.3 us -> 26.8 us
  waiting for transfers between devices: 14.1 us -> 8.59 us
    all_to_all x1 -> x2, blocking collectives: 12.4 us -> 24.7 us  [exchange(): return lax.all_to_all(x, plane, 0, 0)]
    pallas_call x8, Pallas kernels: 27.8 us -> 15.8 us  [the longest x1 7.65 us: product(): pl.pallas_call(product_kernel, out_shape=[pltpu.VMEM((3, 8, 128), F32), p...]
    all_to_all x2 -> x1, waiting for transfers between devices: 13.4 us -> 3.76 us  [exchange(): return lax.all_to_all(x, plane, 0, 0)]
    all_to_all x2 -> x1, starting transfers between devices: 15.6 us -> 10.3 us  [exchange(): return lax.all_to_all(x, plane, 0, 0)]
    unnamed x13 -> x0, local copies, waits for them, and re-layouts: 5.13 us -> none
    all_to_all x1, blocking collectives: 21.2 us -> 16.9 us  [on_device(): summary = lax.all_to_all(summary, 'gz', 0, 0)]
    ppermute x1, waiting for transfers between devices: 0.01 us -> 2.55 us  [on_device(): lax.ppermute(outgoing, 'gz', up)]
    ppermute x1, starting transfers between devices: 4.57 us -> 2.28 us  [on_device(): lax.ppermute(outgoing, 'gz', down)]
  transfers between devices with their start and end apart: 6 -> 5, of which waited for: 3 -> 3; matrix products, arithmetic and copies ran while one was open for 3% -> 0% of each run, Pallas kernels for 5% -> 6%
where the time goes in v2:
time: 94.9 us; the launch traced here: 94.3 us
  blocking collectives  41.6 us (44%)
  starting transfers between devices  26.8 us (28%)
  Pallas kernels  16.6 us (17%)
  waiting for transfers between devices  8.59 us (9%)
    all_to_all x2, blocking collectives, exchange(): return lax.all_to_all(x, plane, 0, 0)  24.7 us
    all_to_all x1, blocking collectives, on_device(): summary = lax.all_to_all(summary, 'gz', 0, 0)  16.9 us
    all_to_all x1, starting transfers between devices, exchange(): return lax.all_to_all(x, plane, 0, 0)  10.3 us
    ppermute x1, starting transfers between devices, on_device(): lax.ppermute(message, 'gz', down)  9.26 us
    pallas_call x1, Pallas kernels, product(): pl.pallas_call(product_kernel, out_shape=[pltpu.VMEM((3, 8, 128), F32), p...  7.65 us
    pallas_call x2, Pallas kernels, from_hbm(): pl.pallas_call(kernel, out_shape=[pltpu.VMEM(s, d) for s, d in shapes], i...  5.36 us
    all_to_all x1, waiting for transfers between devices, exchange(): return lax.all_to_all(x, plane, 0, 0)  3.76 us
    ppermute x1, starting transfers between devices, on_device(): lax.ppermute(outgoing, 'gz', up)  2.99 us
  transfers between devices with their start and end apart: 5, of which 3 were waited for; matrix products, arithmetic and copies ran while one was open for 0% of the time, Pallas kernels for 6%

profile of v2, /device:TPU:1, one launch (start us, length us, event | category | flops | bytes accessed | tf_op | source)
XLA Modules:
  0.0 94.3 jit_solution(6002032388039927202)
XLA Ops:
  0.6 1.5 %pack.1 = f32[32,8,128]{2,1,0:T(8,128)} custom-call(f32[3,1,1,1,128]{4,3,2,1,0:T(1,128)} %places.1, f32[30,3,1,1,1,128]{5,4,3,2,1,0:T(1,128)} %basis_at.1, s32[1,1,1,2,64]{4,3,2,1,0:T(2,128)} %map_x.1, s32[1,1,1,2,64]{4,3,2,1,0:T(2,128)} %map_y.1), custom_call_target="tpu_custom_call" | custom-call | tf_op jit(solution)/shard_map/pack/pallas_call | solution.py:415
  2.1 10.3 %all-to-all-start = ((f32[32,8,128]{2,1,0:T(8,128)}), f32[32,8,128]{2,1,0:T(8,128)S(1)}, u32[]{:S(2)}, u32[]{:S(2)}) async-start(f32[32,8,128]{2,1,0:T(8,128)} %pack.1), calls=%async_computation | async-start | bytes 262144 | tf_op jit(solution)/shard_map/all_to_all | solution.py:630
  12.4 4.0 %mixing.1 = (bf16[512,256]{1,0:T(8,128)(2,1)S(1)}, bf16[512,256]{1,0:T(8,128)(2,1)S(1)}, bf16[256,512]{1,0:T(8,128)(2,1)S(1)}, bf16[256,512]{1,0:T(8,128)(2,1)S(1)}, s32[1,128]{1,0:T(1,128)S(1)}) custom-call(f32[2,16,100]{2,1,0:T(8,128)} %table_at, f32[240,1600]{1,0:T(8,128)} %bitcast.6, s32[1,1,1,2,64]{4,3,2,1,0:T(2,128)} %map_at.1), custom_call_target="tpu_custom_call" | custom-call | tf_op jit(solution)/shard_map/mixing/pallas_call | solution.py:136
  16.5 3.8 %all-to-all-done.got.maps = f32[32,8,128]{2,1,0:T(8,128)S(1)} async-done(((f32[32,8,128]{2,1,0:T(8,128)}), f32[32,8,128]{2,1,0:T(8,128)S(1)}, u32[]{:S(2)}, u32[]{:S(2)}) %all-to-all-start) | async-done | bytes 131104 | tf_op jit(solution)/shard_map/all_to_all | solution.py:630
  20.2 0.3 assemble.1
  20.5 9.3 %collective-permute-start.1 = (f32[8,128]{1,0:T(8,128)S(1)}, f32[8,128]{1,0:T(8,128)S(1)}, u32[]{:S(2)}, u32[]{:S(2)}) collective-permute-start(f32[8,128]{1,0:T(8,128)S(1)} %get-tuple-element.37), channel_id=1, source_target_pairs={{1,0},{2,1},{3,2},{4,3},{5,4},{6,5},{7,6},{8,7},{9,8},{10,9},{11,1... | collective-permute-start | bytes 12296 | tf_op jit(solution)/shard_map/ppermute | solution.py:639
  29.8 1.9 %collective-permute-start = (f32[8,128]{1,0:T(8,128)S(1)}, f32[8,128]{1,0:T(8,128)S(1)}, u32[]{:S(2)}, u32[]{:S(2)}) collective-permute-start(f32[8,128]{1,0:T(8,128)S(1)} %get-tuple-element.37), channel_id=1, source_target_pairs={{0,1},{1,2},{2,3},{3,4},{4,5},{5,6},{6,7},{7,8},{8,9},{9,10},{10,1... | collective-permute-start | bytes 12296 | tf_op jit(solution)/shard_map/ppermute | solution.py:639
  31.7 1.3 %lists.1 = (bf16[256,256]{1,0:T(8,128)(2,1)S(1)}, bf16[256,256]{1,0:T(8,128)(2,1)S(1)}, bf16[256,256]{1,0:T(8,128)(2,1)S(1)}, bf16[256,256]{1,0:T(8,128)(2,1)S(1...) custom-call(f32[240,240]{1,0:T(8,128)} %w2_at.1, ...), custom_call_target="tpu_custom_call" | custom-call | tf_op jit(solution)/shard_map/lists/pallas_call | solution.py:136
  33.1 0.0 collective-permute-done.1.above
  33.1 2.3 %collective-permute-done.below = f32[8,128]{1,0:T(8,128)S(1)} collective-permute-done((f32[8,128]{1,0:T(8,128)S(1)}, f32[8,128]{1,0:T(8,128)S(1)}, u32[]{:S(2)}, u32[]{:S(2)}) %collective-permute-start) | collective-permute-done | bytes 4128 | tf_op jit(solution)/shard_map/ppermute | solution.py:639
  35.3 7.7 %product.1 = (f32[3,8,128]{2,1,0:T(8,128)S(1)}, f32[8,128]{1,0:T(8,128)S(1)}) custom-call(f32[3,8,128]{2,1,0:T(8,128)S(1)} %get-tuple-element.36.tiles, f32[8,128]{1,0:T(8,128)S(1)} %collective-permute-done.below, f32[8,128]{1,0:T(8,128)S(1)} %collective-permute-done.1.above, s32[128,128]{1,0:T(8,128)S(1)} %get-tuple-element.38.ids_t, ...), custom_call_target="tpu_custom_call" | custom-call | tf_op jit(solution)/shard_map/product/pallas_call | solution.py:387
  43.0 2.3 %collective-permute-start.3 = (f32[8,128]{1,0:T(8,128)S(1)}, f32[8,128]{1,0:T(8,128)S(1)}, u32[]{:S(2)}, u32[]{:S(2)}) collective-permute-start(f32[8,128]{1,0:T(8,128)S(1)} %get-tuple-element.51), channel_id=1, source_target_pairs={{1,0},{2,1},{3,2},{4,3},{5,4},{6,5},{7,6},{8,7},{9,8},{10,9},{11,1... | collective-permute-start | bytes 12296 | tf_op jit(solution)/shard_map/ppermute | solution.py:641
  45.3 3.0 %collective-permute-start.2 = (f32[8,128]{1,0:T(8,128)S(1)}, f32[8,128]{1,0:T(8,128)S(1)}, u32[]{:S(2)}, u32[]{:S(2)}) collective-permute-start(f32[8,128]{1,0:T(8,128)S(1)} %get-tuple-element.51), channel_id=1, source_target_pairs={{0,1},{1,2},{2,3},{3,4},{4,5},{5,6},{6,7},{7,8},{8,9},{9,10},{10,1... | collective-permute-start | bytes 12296 | tf_op jit(solution)/shard_map/ppermute | solution.py:641
  48.3 0.0 collective-permute-done.3.above
  48.3 2.5 %collective-permute-done.2.below = f32[8,128]{1,0:T(8,128)S(1)} collective-permute-done((f32[8,128]{1,0:T(8,128)S(1)}, f32[8,128]{1,0:T(8,128)S(1)}, u32[]{:S(2)}, u32[]{:S(2)}) %collective-permute-start.2) | collective-permute-done | bytes 4128 | tf_op jit(solution)/shard_map/ppermute | solution.py:641
  50.8 0.2 fold_z.1
  51.0 13.5 %all_to_all.20.got = f32[32,8,128]{2,1,0:T(8,128)S(1)} all-to-all(f32[32,8,128]{2,1,0:T(8,128)S(1)} %get-tuple-element.53), channel_id=1, replica_groups=mesh['gx'=4,'gy'=8,'gz'=16] {'gx','gy'}, dimensions={0} | all-to-all | bytes 262144 | tf_op jit(solution)/shard_map/all_to_all | solution.py:630
  64.5 0.8 fold.1
  65.3 11.2 %all_to_all.21.got = f32[32,8,128]{2,1,0:T(8,128)S(1)} all-to-all(f32[32,8,128]{2,1,0:T(8,128)S(1)} %get-tuple-element.56), channel_id=1, replica_groups=mesh['gx'=4,'gy'=8,'gz'=16] {'gx','gy'}, dimensions={0} | all-to-all | bytes 262144 | tf_op jit(solution)/shard_map/all_to_all | solution.py:630
  76.6 16.9 %all_to_all.22.got = f32[16,8,128]{2,1,0:T(8,128)S(1)} all-to-all(f32[16,8,128]{2,1,0:T(8,128)S(1)} %total.1), channel_id=1, replica_groups=mesh['gx'=4,'gy'=8,'gz'=16] {'gz'}, dimensions={0} | all-to-all | bytes 131072 | tf_op jit(solution)/shard_map/all_to_all | solution.py:645
  93.5 0.8 finish.1
  (1 shorter events, 0.0 us)
Async XLA Ops:
  2.1 18.1 %all-to-all-start = ((f32[32,8,128]{2,1,0:T(8,128)}), f32[32,8,128]{2,1,0:T(8,128)S(1)}, u32[]{:S(2)}, u32[]{:S(2)}) async-start(f32[32,8,128]{2,1,0:T(8,128)} %pack.1), calls=%async_computation | async-start | bytes 262144 | tf_op jit(solution)/shard_map/all_to_all | solution.py:630
  20.5 12.6 %collective-permute-start.1 = (f32[8,128]{1,0:T(8,128)S(1)}, f32[8,128]{1,0:T(8,128)S(1)}, u32[]{:S(2)}, u32[]{:S(2)}) collective-permute-start(f32[8,128]{1,0:T(8,128)S(1)} %get-tuple-element.37), channel_id=1, source_target_pairs={{1,0},{2,1},{3,2},{4,3},{5,4},{6,5},{7,6},{8,7},{9,8},{10,9},{11,1... | collective-permute-start | bytes 12296 | tf_op jit(solution)/shard_map/ppermute | solution.py:639
  29.8 5.6 %collective-permute-start = (f32[8,128]{1,0:T(8,128)S(1)}, f32[8,128]{1,0:T(8,128)S(1)}, u32[]{:S(2)}, u32[]{:S(2)}) collective-permute-start(f32[8,128]{1,0:T(8,128)S(1)} %get-tuple-element.37), channel_id=1, source_target_pairs={{0,1},{1,2},{2,3},{3,4},{4,5},{5,6},{6,7},{7,8},{8,9},{9,10},{10,1... | collective-permute-start | bytes 12296 | tf_op jit(solution)/shard_map/ppermute | solution.py:639
  43.0 5.3 %collective-permute-start.3 = (f32[8,128]{1,0:T(8,128)S(1)}, f32[8,128]{1,0:T(8,128)S(1)}, u32[]{:S(2)}, u32[]{:S(2)}) collective-permute-start(f32[8,128]{1,0:T(8,128)S(1)} %get-tuple-element.51), channel_id=1, source_target_pairs={{1,0},{2,1},{3,2},{4,3},{5,4},{6,5},{7,6},{8,7},{9,8},{10,9},{11,1... | collective-permute-start | bytes 12296 | tf_op jit(solution)/shard_map/ppermute | solution.py:641
  45.3 5.6 %collective-permute-start.2 = (f32[8,128]{1,0:T(8,128)S(1)}, f32[8,128]{1,0:T(8,128)S(1)}, u32[]{:S(2)}, u32[]{:S(2)}) collective-permute-start(f32[8,128]{1,0:T(8,128)S(1)} %get-tuple-element.51), channel_id=1, source_target_pairs={{0,1},{1,2},{2,3},{3,4},{4,5},{5,6},{6,7},{7,8},{8,9},{9,10},{10,1... | collective-permute-start | bytes 12296 | tf_op jit(solution)/shard_map/ppermute | solution.py:641

commit v3 on v2

--- a/solution.py
+++ b/solution.py
@@ -214,7 +214,7 @@
         edge[18, rows, :] = rate
         return carry
 
-    lax.fori_loop(0, blocks, geometry, 0, unroll=2)
+    lax.fori_loop(0, blocks, geometry, 0, unroll=8)
 
     def pooling(kk, carry):
         sums = [[jnp.zeros((8, 128), F32) for _ in range(8)] for _ in range(2)]
@@ -243,7 +243,7 @@
         pooled = pooled + acc[pl.ds(s, 128, stride=8), :]
     pooled = pooled * (1.0 / n_slots)
     grads[...] = pooled
-    second = jnp.broadcast_to(kinds[...], (16, 128)) == 1
+    kind = jnp.concatenate([kinds[...], kinds[...]], axis=1)
     p = [pooled[a * 16 : (a + 1) * 16] for a in range(4)]
     dp = [pooled[64 + a * 16 : 64 + (a + 1) * 16] for a in range(4)]
     for k in range(levels):
@@ -252,12 +252,14 @@
         for a in range(4):
             value = value + p[a] * jnp.broadcast_to(grads[a * 16 + k : a * 16 + k + 1, :], (16, 128))
             moved = moved + p[a] * jnp.broadcast_to(grads[64 + a * 16 + k : 64 + a * 16 + k + 1, :], (16, 128))
-        moved = 2.0 * moved
-        pairs[k * 16 : (k + 1) * 16, 0:128] = jnp.where(second, 0.0, value)
-        pairs[k * 16 : (k + 1) * 16, 128:256] = jnp.where(second, 0.0, moved)
-        pairs[256 + k * 16 : 256 + (k + 1) * 16, 0:128] = jnp.where(second, value, 0.0)
-        pairs[256 + k * 16 : 256 + (k + 1) * 16, 128:256] = jnp.where(second, moved, 0.0)
-    z1 = dot3((ut_hi[...], ut_lo[...]), pairs[...])
+        pairs[k * 16 : (k + 1) * 16, 0:128] = value
+        pairs[k * 16 : (k + 1) * 16, 128:256] = 2.0 * moved
+    both = split(pairs[...])
+    z1 = jnp.where(
+        kind == 1,
+        dot3((ut_hi[:, 256:512], ut_lo[:, 256:512]), both),
+        dot3((ut_hi[:, 0:256], ut_lo[:, 0:256]), both),
+    )
     h1 = jnp.tanh(z1[:, 0:128] + cols[:, 0:1])
     slope1 = 1.0 - h1 * h1
     dh1 = slope1 * z1[:, 128:256]
@@ -271,13 +273,17 @@
     e1 = back[:, 0:128] + read
     delta1 = slope1 * e1
     ddelta1 = slope1 * back[:, 128:256] - 2.0 * h1 * dh1 * e1
-    pairs[...] = dot3((u_hi[...], u_lo[...]), jnp.concatenate([delta1, ddelta1], axis=1))
+    both = split(jnp.concatenate([delta1, ddelta1], axis=1))
+    pairs[...] = jnp.where(
+        kind == 1,
+        dot3((u_hi[256:512, :], u_lo[256:512, :]), both),
+        dot3((u_hi[0:256, :], u_lo[0:256, :]), both),
+    )
     g = [jnp.zeros((16, 128), F32) for _ in range(4)]
     dg = [jnp.zeros((16, 128), F32) for _ in range(4)]
     for k in range(levels):
-        low, top = pl.ds(k * 16, 16), pl.ds(256 + k * 16, 16)
-        m = jnp.where(second, pairs[top, 0:128], pairs[low, 0:128])
-        dm = jnp.where(second, pairs[top, 128:256], pairs[low, 128:256])
+        m = pairs[k * 16 : (k + 1) * 16, 0:128]
+        dm = pairs[k * 16 : (k + 1) * 16, 128:256]
         for a in range(4):
             row = jnp.broadcast_to(grads[a * 16 + k : a * 16 + k + 1, :], (16, 128))
             drow = jnp.broadcast_to(grads[64 + a * 16 + k : 64 + a * 16 + k + 1, :], (16, 128))
@@ -354,7 +360,7 @@
     rows16 = [(rows_of((16, 128)) + 16 * rg).astype(F32).astype(BF16) for rg in range(4)]
     on = jnp.ones((16, 128), BF16)
     off = jnp.zeros((16, 128), BF16)
-    chunk = 8
+    chunk = 32
 
     def scatter(step, total):
         lefts, hots = [], []
@@ -394,7 +400,7 @@
             pltpu.VMEM((19, n, 128), F32),
             pltpu.VMEM((16, n, 128), F32),
             pltpu.VMEM((1024, 128), F32),
-            pltpu.VMEM((512, 256), F32),
+            pltpu.VMEM((256, 256), F32),
             pltpu.VMEM((128, 128), F32),
             pltpu.VMEM((6, n, 128), F32),
             pltpu.VMEM((n, 128), F32),
@@ -403,28 +409,32 @@
     )(*here(tiles, below, above, *lists, *weights))
 
 
-def pack_kernel(places, tangent, map_x, map_y, out):
-    rows = [places[c, 0, 0] for c in range(3)] + [tangent[0, c, 0, 0] for c in range(3)]
+def pack_kernel(places_at, basis_at, map_x_at, map_y_at, out, places, tangent, map_x, map_y, semaphores):
+    last = basis_at.shape[0] - 1
+    copies = fetch((places_at, basis_at.at[last], map_x_at, map_y_at), (places, tangent, map_x, map_y), semaphores)
+    for copy in copies:
+        copy.wait()
+    rows = [places[c, 0, 0] for c in range(3)] + [tangent[c, 0, 0] for c in range(3)]
     rows += [halves(map_x).astype(F32), halves(map_y).astype(F32)]
     out[...] = jnp.broadcast_to(jnp.concatenate(rows, axis=0)[None], out.shape)
 
 
 def pack(positions, basis, map_x, map_y, bricks):
-    last = basis.shape[0] - 1
-    whole = lambda a: pl.BlockSpec(a.shape, lambda i: (0,) * a.ndim)
+    arrays = (positions, basis, map_x, map_y)
     return pl.pallas_call(
         pack_kernel,
-        grid=(1,),
         out_shape=pltpu.VMEM((bricks, 8, 128), F32),
-        in_specs=[
-            whole(positions),
-            pl.BlockSpec((1,) + basis.shape[1:], lambda i: (last,) + (0,) * (basis.ndim - 1)),
-            whole(map_x),
-            whole(map_y),
+        in_specs=[pl.BlockSpec(memory_space=pltpu.HBM)] * 4,
+        out_specs=vmem(1)[0],
+        scratch_shapes=[
+            pltpu.VMEM(positions.shape, F32),
+            pltpu.VMEM(basis.shape[1:], F32),
+            pltpu.VMEM(map_x.shape, jnp.int32),
+            pltpu.VMEM(map_y.shape, jnp.int32),
+            pltpu.SemaphoreType.DMA((4,)),
         ],
-        out_specs=vmem(1)[0],
         name="pack",
-    )(positions, basis, map_x, map_y)
+    )(*(pltpu.with_memory_space_constraint(a, pltpu.HBM) for a in arrays))
 
 
 def brick_reader(grid):
@@ -544,18 +554,11 @@
     product[...] = total
     last = rows_of((32, 128)) == 30
     column = jnp.zeros((32, 128), F32)
-    line = jnp.zeros((8, 32), F32)
     for c in range(3):
         row = total[c : c + 1]
-        rows = jnp.where(last, row, stored[c])
-        column = column + rows * row
-        line = line + lax.dot_general(
-            jnp.broadcast_to(row, (8, 128)), rows, NT, precision=lax.Precision.HIGHEST, preferred_element_type=F32
-        )
+        column = column + jnp.where(last, row, stored[c]) * row
     column = jnp.sum(column, axis=1, keepdims=True)
-    line = jnp.concatenate([line[0:1], jnp.zeros((1, 96), F32)], axis=1)
-    lane = rows_of((32, 128), 1)
-    full = jnp.where(lane == 30, column, jnp.where(last, line, gram[...]))
+    full = jnp.where(rows_of((32, 128), 1) == 30, column, gram[...])
     tile = full[0:8]
     for b in range(1, 4):
         tile = tile + pltpu.roll(full[8 * b : 8 * b + 8], 32 * b, 1)
@@ -591,13 +594,15 @@
     packed = jnp.sum(got[...], axis=0) * (1.0 / entries)
     full = jnp.concatenate([packed] + [pltpu.roll(packed, 128 - 32 * b, 1) for b in range(1, 4)], axis=0)
     column = full[:, count : count + 1]
-    line = full[count : count + 1, :]
+    line = jnp.sum(jnp.where(rows_of((32, 128)) == rows_of((32, 128), 1), column, 0.0), axis=0, keepdims=True)
     row = rows_of((32, 1))
     lane = rows_of((1, 128), 1)
     down = jnp.where(row < count, column, jnp.where(row == count, -1.0, 0.0))
-    across = jnp.where(lane < count, line, jnp.where(lane == count, -1.0, 0.0))
-    square = jnp.sum(jnp.where(rows_of((32, 128), 1) <= count, full * across * down, 0.0), axis=1, keepdims=True)
-    length = jnp.sqrt(jnp.maximum(jnp.sum(square, axis=0, keepdims=True), 0.0) + 1e-06)
+    across = jnp.where(lane < count, line, jnp.where(lane == count, -2.0, 0.0))
+    size = jnp.where(row < count, full * across * down, jnp.where((row == count) & (lane == count), full, 0.0))
+    size = jnp.where(rows_of((32, 128), 1) <= count, size, 0.0)
+    size = jnp.sum(jnp.sum(size, axis=1, keepdims=True), axis=0, keepdims=True)
+    length = jnp.sqrt(jnp.maximum(size, 0.0) + 1e-06)
     norm[...] = length
     correlations[...] = line[:, 0:count]
     share = jnp.where(row < count, column, 0.0)

time: 94.9 us -> 93.1 us (0.981)
  Pallas kernels: 16.6 us -> 14.9 us
    pallas_call x1, Pallas kernels: 7.65 us -> 6.08 us  [product(): pl.pallas_call(product_kernel, out_shape=[pltpu.VMEM((3, 8, 128), F32), p...]
where the time goes in v3:
time: 93.1 us; the launch traced here: 92.6 us
  blocking collectives  41.6 us (45%)
  starting transfers between devices  26.8 us (29%)
  Pallas kernels  14.9 us (16%)
  waiting for transfers between devices  8.62 us (9%)
    all_to_all x2, blocking collectives, exchange(): return lax.all_to_all(x, plane, 0, 0)  24.7 us
    all_to_all x1, blocking collectives, on_device(): summary = lax.all_to_all(summary, 'gz', 0, 0)  16.9 us
    all_to_all x1, starting transfers between devices, exchange(): return lax.all_to_all(x, plane, 0, 0)  10.3 us
    ppermute x1, starting transfers between devices, on_device(): lax.ppermute(message, 'gz', down)  9.26 us
    pallas_call x1, Pallas kernels, product(): pl.pallas_call(product_kernel, out_shape=[pltpu.VMEM((3, 8, 128), F32), p...  6.08 us
    pallas_call x2, Pallas kernels, from_hbm(): pl.pallas_call(kernel, out_shape=[pltpu.VMEM(s, d) for s, d in shapes], i...  5.36 us
    all_to_all x1, waiting for transfers between devices, exchange(): return lax.all_to_all(x, plane, 0, 0)  3.76 us
    ppermute x1, starting transfers between devices, on_device(): lax.ppermute(outgoing, 'gz', up)  2.96 us
  transfers between devices with their start and end apart: 5, of which 3 were waited for; matrix products, arithmetic and copies ran while one was open for 0% of the time, Pallas kernels for 6%

profile of v3, /device:TPU:1, one launch (start us, length us, event | category | flops | bytes accessed | tf_op | source)
XLA Modules:
  0.0 92.6 jit_solution(9682523618644542129)
XLA Ops:
  0.6 1.5 %pack.1 = f32[32,8,128]{2,1,0:T(8,128)} custom-call(f32[3,1,1,1,128]{4,3,2,1,0:T(1,128)} %places_at.1, f32[30,3,1,1,1,128]{5,4,3,2,1,0:T(1,128)} %basis_at.3, s32[1,1,1,2,64]{4,3,2,1,0:T(2,128)} %map_x_at.1, s32[1,1,1,2,64]{4,3,2,1,0:T(2,128)} %map_y_at.1), custom_call_target="tpu_custom_call" | custom-call | tf_op jit(solution)/shard_map/pack/pallas_call | solution.py:424
  2.1 10.3 %all-to-all-start = ((f32[32,8,128]{2,1,0:T(8,128)}), f32[32,8,128]{2,1,0:T(8,128)S(1)}, u32[]{:S(2)}, u32[]{:S(2)}) async-start(f32[32,8,128]{2,1,0:T(8,128)} %pack.1), calls=%async_computation | async-start | bytes 262144 | tf_op jit(solution)/shard_map/all_to_all | solution.py:635
  12.5 4.0 %mixing.1 = (bf16[512,256]{1,0:T(8,128)(2,1)S(1)}, bf16[512,256]{1,0:T(8,128)(2,1)S(1)}, bf16[256,512]{1,0:T(8,128)(2,1)S(1)}, bf16[256,512]{1,0:T(8,128)(2,1)S(1)}, s32[1,128]{1,0:T(1,128)S(1)}) custom-call(f32[2,16,100]{2,1,0:T(8,128)} %table_at, f32[240,1600]{1,0:T(8,128)} %bitcast.6, s32[1,1,1,2,64]{4,3,2,1,0:T(2,128)} %map_at.1), custom_call_target="tpu_custom_call" | custom-call | tf_op jit(solution)/shard_map/mixing/pallas_call | solution.py:136
  16.5 3.8 %all-to-all-done.got.maps = f32[32,8,128]{2,1,0:T(8,128)S(1)} async-done(((f32[32,8,128]{2,1,0:T(8,128)}), f32[32,8,128]{2,1,0:T(8,128)S(1)}, u32[]{:S(2)}, u32[]{:S(2)}) %all-to-all-start) | async-done | bytes 131104 | tf_op jit(solution)/shard_map/all_to_all | solution.py:635
  20.3 0.3 assemble.1
  20.6 9.3 %collective-permute-start.1 = (f32[8,128]{1,0:T(8,128)S(1)}, f32[8,128]{1,0:T(8,128)S(1)}, u32[]{:S(2)}, u32[]{:S(2)}) collective-permute-start(f32[8,128]{1,0:T(8,128)S(1)} %get-tuple-element.37), channel_id=1, source_target_pairs={{1,0},{2,1},{3,2},{4,3},{5,4},{6,5},{7,6},{8,7},{9,8},{10,9},{11,1... | collective-permute-start | bytes 12296 | tf_op jit(solution)/shard_map/ppermute | solution.py:644
  29.8 1.9 %collective-permute-start = (f32[8,128]{1,0:T(8,128)S(1)}, f32[8,128]{1,0:T(8,128)S(1)}, u32[]{:S(2)}, u32[]{:S(2)}) collective-permute-start(f32[8,128]{1,0:T(8,128)S(1)} %get-tuple-element.37), channel_id=1, source_target_pairs={{0,1},{1,2},{2,3},{3,4},{4,5},{5,6},{6,7},{7,8},{8,9},{9,10},{10,1... | collective-permute-start | bytes 12296 | tf_op jit(solution)/shard_map/ppermute | solution.py:644
  31.8 1.3 %lists.1 = (bf16[256,256]{1,0:T(8,128)(2,1)S(1)}, bf16[256,256]{1,0:T(8,128)(2,1)S(1)}, bf16[256,256]{1,0:T(8,128)(2,1)S(1)}, bf16[256,256]{1,0:T(8,128)(2,1)S(1...) custom-call(f32[240,240]{1,0:T(8,128)} %w2_at.1, ...), custom_call_target="tpu_custom_call" | custom-call | tf_op jit(solution)/shard_map/lists/pallas_call | solution.py:136
  33.1 0.0 collective-permute-done.1.above
  33.1 2.3 %collective-permute-done.below = f32[8,128]{1,0:T(8,128)S(1)} collective-permute-done((f32[8,128]{1,0:T(8,128)S(1)}, f32[8,128]{1,0:T(8,128)S(1)}, u32[]{:S(2)}, u32[]{:S(2)}) %collective-permute-start) | collective-permute-done | bytes 4128 | tf_op jit(solution)/shard_map/ppermute | solution.py:644
  35.4 6.1 %product.1 = (f32[3,8,128]{2,1,0:T(8,128)S(1)}, f32[8,128]{1,0:T(8,128)S(1)}) custom-call(f32[3,8,128]{2,1,0:T(8,128)S(1)} %get-tuple-element.36.tiles, f32[8,128]{1,0:T(8,128)S(1)} %collective-permute-done.below, f32[8,128]{1,0:T(8,128)S(1)} %collective-permute-done.1.above, s32[128,128]{1,0:T(8,128)S(1)} %get-tuple-element.38.ids_t, ...), custom_call_target="tpu_custom_call" | custom-call | tf_op jit(solution)/shard_map/product/pallas_call | solution.py:393
  41.5 2.3 %collective-permute-start.3 = (f32[8,128]{1,0:T(8,128)S(1)}, f32[8,128]{1,0:T(8,128)S(1)}, u32[]{:S(2)}, u32[]{:S(2)}) collective-permute-start(f32[8,128]{1,0:T(8,128)S(1)} %get-tuple-element.51), channel_id=1, source_target_pairs={{1,0},{2,1},{3,2},{4,3},{5,4},{6,5},{7,6},{8,7},{9,8},{10,9},{11,1... | collective-permute-start | bytes 12296 | tf_op jit(solution)/shard_map/ppermute | solution.py:646
  43.8 3.0 %collective-permute-start.2 = (f32[8,128]{1,0:T(8,128)S(1)}, f32[8,128]{1,0:T(8,128)S(1)}, u32[]{:S(2)}, u32[]{:S(2)}) collective-permute-start(f32[8,128]{1,0:T(8,128)S(1)} %get-tuple-element.51), channel_id=1, source_target_pairs={{0,1},{1,2},{2,3},{3,4},{4,5},{5,6},{6,7},{7,8},{8,9},{9,10},{10,1... | collective-permute-start | bytes 12296 | tf_op jit(solution)/shard_map/ppermute | solution.py:646
  46.8 0.0 collective-permute-done.3.above
  46.8 2.6 %collective-permute-done.2.below = f32[8,128]{1,0:T(8,128)S(1)} collective-permute-done((f32[8,128]{1,0:T(8,128)S(1)}, f32[8,128]{1,0:T(8,128)S(1)}, u32[]{:S(2)}, u32[]{:S(2)}) %collective-permute-start.2) | collective-permute-done | bytes 4128 | tf_op jit(solution)/shard_map/ppermute | solution.py:646
  49.4 0.2 fold_z.1
  49.6 13.4 %all_to_all.20.got = f32[32,8,128]{2,1,0:T(8,128)S(1)} all-to-all(f32[32,8,128]{2,1,0:T(8,128)S(1)} %get-tuple-element.53), channel_id=1, replica_groups=mesh['gx'=4,'gy'=8,'gz'=16] {'gx','gy'}, dimensions={0} | all-to-all | bytes 262144 | tf_op jit(solution)/shard_map/all_to_all | solution.py:635
  63.0 0.6 fold.1
  63.6 11.2 %all_to_all.21.got = f32[32,8,128]{2,1,0:T(8,128)S(1)} all-to-all(f32[32,8,128]{2,1,0:T(8,128)S(1)} %get-tuple-element.56), channel_id=1, replica_groups=mesh['gx'=4,'gy'=8,'gz'=16] {'gx','gy'}, dimensions={0} | all-to-all | bytes 262144 | tf_op jit(solution)/shard_map/all_to_all | solution.py:635
  74.9 16.9 %all_to_all.22.got = f32[16,8,128]{2,1,0:T(8,128)S(1)} all-to-all(f32[16,8,128]{2,1,0:T(8,128)S(1)} %total.1), channel_id=1, replica_groups=mesh['gx'=4,'gy'=8,'gz'=16] {'gz'}, dimensions={0} | all-to-all | bytes 131072 | tf_op jit(solution)/shard_map/all_to_all | solution.py:650
  91.8 0.8 finish.1
  (1 shorter events, 0.0 us)
Async XLA Ops:
  2.1 18.1 %all-to-all-start = ((f32[32,8,128]{2,1,0:T(8,128)}), f32[32,8,128]{2,1,0:T(8,128)S(1)}, u32[]{:S(2)}, u32[]{:S(2)}) async-start(f32[32,8,128]{2,1,0:T(8,128)} %pack.1), calls=%async_computation | async-start | bytes 262144 | tf_op jit(solution)/shard_map/all_to_all | solution.py:635
  20.6 12.6 %collective-permute-start.1 = (f32[8,128]{1,0:T(8,128)S(1)}, f32[8,128]{1,0:T(8,128)S(1)}, u32[]{:S(2)}, u32[]{:S(2)}) collective-permute-start(f32[8,128]{1,0:T(8,128)S(1)} %get-tuple-element.37), channel_id=1, source_target_pairs={{1,0},{2,1},{3,2},{4,3},{5,4},{6,5},{7,6},{8,7},{9,8},{10,9},{11,1... | collective-permute-start | bytes 12296 | tf_op jit(solution)/shard_map/ppermute | solution.py:644
  29.8 5.6 %collective-permute-start = (f32[8,128]{1,0:T(8,128)S(1)}, f32[8,128]{1,0:T(8,128)S(1)}, u32[]{:S(2)}, u32[]{:S(2)}) collective-permute-start(f32[8,128]{1,0:T(8,128)S(1)} %get-tuple-element.37), channel_id=1, source_target_pairs={{0,1},{1,2},{2,3},{3,4},{4,5},{5,6},{6,7},{7,8},{8,9},{9,10},{10,1... | collective-permute-start | bytes 12296 | tf_op jit(solution)/shard_map/ppermute | solution.py:644
  41.5 5.3 %collective-permute-start.3 = (f32[8,128]{1,0:T(8,128)S(1)}, f32[8,128]{1,0:T(8,128)S(1)}, u32[]{:S(2)}, u32[]{:S(2)}) collective-permute-start(f32[8,128]{1,0:T(8,128)S(1)} %get-tuple-element.51), channel_id=1, source_target_pairs={{1,0},{2,1},{3,2},{4,3},{5,4},{6,5},{7,6},{8,7},{9,8},{10,9},{11,1... | collective-permute-start | bytes 12296 | tf_op jit(solution)/shard_map/ppermute | solution.py:646
  43.8 5.6 %collective-permute-start.2 = (f32[8,128]{1,0:T(8,128)S(1)}, f32[8,128]{1,0:T(8,128)S(1)}, u32[]{:S(2)}, u32[]{:S(2)}) collective-permute-start(f32[8,128]{1,0:T(8,128)S(1)} %get-tuple-element.51), channel_id=1, source_target_pairs={{0,1},{1,2},{2,3},{3,4},{4,5},{5,6},{6,7},{7,8},{8,9},{9,10},{10,1... | collective-permute-start | bytes 12296 | tf_op jit(solution)/shard_map/ppermute | solution.py:646

commit v4 on v3

--- a/solution.py
+++ b/solution.py
@@ -50,8 +50,9 @@
 EXACT = dict(precision=lax.Precision.HIGHEST, preferred_element_type=F32)
 
 
-def mixing_kernel(table_at, w1_at, map_at, u_hi, u_lo, ut_hi, ut_lo, map_row, table, w1t, map_z, outer, inner, k_hi, k_lo, semaphores):
-    copies = fetch((table_at, map_at, w1_at), (table, map_z, w1t), semaphores)
+def mixing_kernel(table_at, w1_at, map_at, basis_at, u_hi, u_lo, ut_hi, ut_lo, map_row, stored, table, w1t, map_z, basis, outer, inner, k_hi, k_lo, semaphores):
+    copies = fetch((table_at, map_at, w1_at, basis_at), (table, map_z, w1t, basis), semaphores)
+    stored[...] = jnp.zeros_like(stored)
     types, levels, width = table.shape
     hidden = w1t.shape[0]
     m2 = w1t.shape[1] // width
@@ -81,6 +82,10 @@
     lax.fori_loop(0, width, kron, 0, unroll=4)
     copies[1].wait()
     map_row[...] = halves(map_z)
+    copies[3].wait()
+    for c in range(3):
+        for k in range(basis.shape[0]):
+            stored[c, k : k + 1, :] = basis[k, c, 0, 0]
     copies[2].wait()
     full = dot3(w1t[...], (k_hi[...], k_lo[...]))
     full = jnp.concatenate([full, jnp.zeros((256 - hidden, count), F32)], axis=0)
@@ -92,12 +97,11 @@
     u_lo[...] = lo
 
 
-def lists_kernel(w2_at, b1_at, b2_at, wo_at, ids_at, counts_at, kinds_at, basis_at, w2_hi, w2_lo, w2t_hi, w2t_lo, cols, ids_t, count_row, kind_row, stored, gram, w2, b1, b2, wo, ids, counts, kinds, basis, pad, semaphores):
-    places = (w2, b1, b2, wo, ids, counts, kinds, basis)
-    copies = fetch((w2_at, b1_at, b2_at, wo_at, ids_at, counts_at, kinds_at, basis_at), places, semaphores)
+def lists_kernel(w2_at, b1_at, b2_at, wo_at, ids_at, counts_at, kinds_at, stored, w2_hi, w2_lo, w2t_hi, w2t_lo, cols, ids_t, count_row, kind_row, gram, w2, b1, b2, wo, ids, counts, kinds, pad, semaphores):
+    places = (w2, b1, b2, wo, ids, counts, kinds)
+    copies = fetch((w2_at, b1_at, b2_at, wo_at, ids_at, counts_at, kinds_at), places, semaphores)
     hidden = w2.shape[0]
     pad[...] = jnp.zeros_like(pad)
-    stored[...] = jnp.zeros_like(stored)
     gram[...] = jnp.zeros_like(gram)
     for copy in copies:
         copy.wait()
@@ -118,8 +122,6 @@
     kind_row[...] = kinds[0, 0]
     total = jnp.zeros((32, 32), F32)
     for c in range(3):
-        for k in range(basis.shape[0]):
-            stored[c, k : k + 1, :] = basis[k, c, 0, 0]
         total = total + lax.dot_general(stored[c], stored[c], NT, **EXACT)
     gram[:, 0:32] = total
 
@@ -132,33 +134,33 @@
     return [pltpu.with_memory_space_constraint(a, pltpu.VMEM) for a in arrays]
 
 
-def from_hbm(kernel, name, shapes, scratch, *arrays):
+def from_hbm(kernel, name, shapes, scratch, *arrays, held=()):
     return pl.pallas_call(
         kernel,
         out_shape=[pltpu.VMEM(s, d) for s, d in shapes],
-        in_specs=[pl.BlockSpec(memory_space=pltpu.HBM)] * len(arrays),
+        in_specs=[pl.BlockSpec(memory_space=pltpu.HBM)] * len(arrays) + vmem(len(held)),
         out_specs=vmem(len(shapes)),
         scratch_shapes=[pltpu.VMEM(a.shape, a.dtype) for a in arrays] + scratch + [pltpu.SemaphoreType.DMA((len(arrays),))],
         name=name,
-    )(*(pltpu.with_memory_space_constraint(a, pltpu.HBM) for a in arrays))
-
-
-def mixing(table, w1, map_z):
+    )(*(pltpu.with_memory_space_constraint(a, pltpu.HBM) for a in arrays), *here(*held))
+
+
+def mixing(table, w1, map_z, basis):
     hp = 256
     count = table.shape[0] * table.shape[1] ** 2
-    shapes = [((count, hp), BF16)] * 2 + [((hp, count), BF16)] * 2 + [((1, 128), jnp.int32)]
+    shapes = [((count, hp), BF16)] * 2 + [((hp, count), BF16)] * 2 + [((1, 128), jnp.int32), ((3, 32, 128), F32)]
     scratch = [pltpu.VMEM((128, count), F32)] * 2 + [pltpu.VMEM((w1.shape[0], count), BF16)] * 2
-    *weights, map_row = from_hbm(mixing_kernel, "mixing", shapes, scratch, table, w1.T, map_z)
-    return weights, map_row
-
-
-def lists_of(w2, b1, b2, wo, ids, counts, kinds, basis):
+    *weights, map_row, stored = from_hbm(mixing_kernel, "mixing", shapes, scratch, table, w1.T, map_z, basis)
+    return weights, map_row, stored
+
+
+def lists_of(w2, b1, b2, wo, ids, counts, kinds, stored):
     hp = 256
     row = ((1, 128), jnp.int32)
-    shapes = [((hp, hp), BF16)] * 4 + [((hp, 128), F32), ((ids.shape[-1], 128), jnp.int32), row, row, ((3, 32, 128), F32), ((32, 128), F32)]
+    shapes = [((hp, hp), BF16)] * 4 + [((hp, 128), F32), ((ids.shape[-1], 128), jnp.int32), row, row, ((32, 128), F32)]
     scratch = [pltpu.VMEM((hp, hp), F32)]
-    done = from_hbm(lists_kernel, "lists", shapes, scratch, w2, b1[None], b2[None], wo[None], ids, counts, kinds, basis)
-    return done[:5], done[5:8], done[8], done[9]
+    done = from_hbm(lists_kernel, "lists", shapes, scratch, w2, b1[None], b2[None], wo[None], ids, counts, kinds, held=(stored,))
+    return done[:5], done[5:8], done[8]
 
 
 def shifted_ghosts(below, above, coord, rows):
@@ -173,7 +175,7 @@
     gap = levels - 1
     blocks = n_slots // 8
     xv[0:3] = tiles[...]
-    xv[3] = shifted_ghosts(pltpu.roll(below[...], 64, 1), pltpu.roll(above[...], 64, 1), 2, 8)
+    xv[3] = shifted_ghosts(pltpu.roll(below[0:8, :], 64, 1), pltpu.roll(above[0:8, :], 64, 1), 2, 8)
     count_row = jnp.broadcast_to(counts[...], (8, 128))
 
     def geometry(nb, carry):
@@ -375,24 +377,21 @@
 
     total = lax.fori_loop(0, n_slots // chunk, scatter, jnp.zeros((48, 64), F32), unroll=2)
     out[...] = jnp.zeros_like(out)
-    sent[...] = jnp.zeros_like(sent)
+    rows = {}
     for c in range(3):
         both = total[c * 8 : c * 8 + 8] + total[24 + c * 8 : 32 + c * 8]
         for q in range(4):
-            row = jnp.concatenate([both[2 * q : 2 * q + 1], both[2 * q + 1 : 2 * q + 2]], axis=1)
-            if q == 0:
-                row = row - jnp.sum(centre[c], axis=0, keepdims=True)
-            if q < 3:
-                out[q, c : c + 1, :] = row
-            else:
-                sent[c : c + 1, :] = row
-
-
-def product(tiles, below, above, lists, weights):
+            rows[q, c] = jnp.concatenate([both[2 * q : 2 * q + 1], both[2 * q + 1 : 2 * q + 2]], axis=1)
+        out[c : c + 1, :] = rows[0, c] - jnp.sum(centre[c], axis=0, keepdims=True)
+    tile = [rows[q, c] for q in range(1, 4) for c in range(3)] + [jnp.zeros((7, 128), F32)]
+    sent[...] = jnp.broadcast_to(jnp.concatenate(tile, axis=0)[None], sent.shape)
+
+
+def product(tiles, below, above, lists, weights, bricks):
     n = lists[0].shape[0]
     return pl.pallas_call(
         product_kernel,
-        out_shape=[pltpu.VMEM((3, 8, 128), F32), pltpu.VMEM((8, 128), F32)],
+        out_shape=[pltpu.VMEM((8, 128), F32), pltpu.VMEM((bricks, 16, 128), F32)],
         in_specs=vmem(15),
         out_specs=vmem(2),
         scratch_shapes=[
@@ -409,29 +408,30 @@
     )(*here(tiles, below, above, *lists, *weights))
 
 
-def pack_kernel(places_at, basis_at, map_x_at, map_y_at, out, places, tangent, map_x, map_y, semaphores):
+def pack_kernel(places_at, basis_at, map_x_at, map_y_at, map_z_at, out, places, tangent, map_x, map_y, map_z, semaphores):
     last = basis_at.shape[0] - 1
-    copies = fetch((places_at, basis_at.at[last], map_x_at, map_y_at), (places, tangent, map_x, map_y), semaphores)
+    copies = fetch((places_at, basis_at.at[last], map_x_at, map_y_at, map_z_at), (places, tangent, map_x, map_y, map_z), semaphores)
     for copy in copies:
         copy.wait()
     rows = [places[c, 0, 0] for c in range(3)] + [tangent[c, 0, 0] for c in range(3)]
-    rows += [halves(map_x).astype(F32), halves(map_y).astype(F32)]
+    rows += [halves(m).astype(F32) for m in (map_x, map_y, map_z)] + [jnp.zeros((7, 128), F32)]
     out[...] = jnp.broadcast_to(jnp.concatenate(rows, axis=0)[None], out.shape)
 
 
-def pack(positions, basis, map_x, map_y, bricks):
-    arrays = (positions, basis, map_x, map_y)
+def pack(positions, basis, map_x, map_y, map_z, bricks):
+    arrays = (positions, basis, map_x, map_y, map_z)
     return pl.pallas_call(
         pack_kernel,
-        out_shape=pltpu.VMEM((bricks, 8, 128), F32),
-        in_specs=[pl.BlockSpec(memory_space=pltpu.HBM)] * 4,
+        out_shape=pltpu.VMEM((bricks, 16, 128), F32),
+        in_specs=[pl.BlockSpec(memory_space=pltpu.HBM)] * 5,
         out_specs=vmem(1)[0],
         scratch_shapes=[
             pltpu.VMEM(positions.shape, F32),
             pltpu.VMEM(basis.shape[1:], F32),
             pltpu.VMEM(map_x.shape, jnp.int32),
             pltpu.VMEM(map_y.shape, jnp.int32),
-            pltpu.SemaphoreType.DMA((4,)),
+            pltpu.VMEM(map_z.shape, jnp.int32),
+            pltpu.SemaphoreType.DMA((5,)),
         ],
         name="pack",
     )(*(pltpu.with_memory_space_constraint(a, pltpu.HBM) for a in arrays))
@@ -457,7 +457,7 @@
     return pltpu.roll(x, 64, 1)
 
 
-def assemble_kernel(grid, got, map_z, tiles, message):
+def assemble_kernel(grid, got, map_z, stored, tiles, message):
     at = brick_reader(grid)
     lower = rows_of((8, 128), 1) < 64
     row = rows_of((8, 128))
@@ -465,7 +465,7 @@
     step_y = jnp.where(row == 1, 1.0, 0.0)
     middle, ghosts, index = {}, {}, {}
     for dy in (-1, 0, 1):
-        own, low, high = at(got, 0, dy), at(got, -1, dy), at(got, 1, dy)
+        own, low, high = (at(got, dx, dy)[0:8] for dx in (0, -1, 1))
         from_low = lane_pick(low, turn(as_index(low[6:7])))
         from_high = lane_pick(high, turn(as_index(high[6:7])))
         middle[dy] = own
@@ -482,117 +482,140 @@
     tiles[2] = third
     chosen = jnp.broadcast_to(map_z[...], (8, 128))
     low = chosen & 127
-    message[...] = jnp.where(
+    message[0:8, :] = jnp.where(
         chosen < 128, lane_pick(middle[0], low), jnp.where(chosen < 256, lane_pick(ghosts[0], low), lane_pick(third, low))
     )
-
-
-def assemble(got, map_z, grid):
+    maps = [at(got, dx, dy)[8:9] for dx in (-1, 0, 1) for dy in (-1, 0, 1)]
+    maps += [at(got, dx, 0)[7:8] for dx in (-1, 0, 1)] + [at(got, 0, 0)[6:7], jnp.zeros((3, 128), F32)]
+    message[8:24, :] = jnp.concatenate(maps, axis=0)
+    for c in range(3):
+        message[24 + 32 * c : 56 + 32 * c, :] = stored[c]
+
+
+def assemble(got, map_z, stored, grid):
     return pl.pallas_call(
         functools.partial(assemble_kernel, grid),
-        out_shape=[pltpu.VMEM((3, 8, 128), F32), pltpu.VMEM((8, 128), F32)],
-        in_specs=vmem(2),
+        out_shape=[pltpu.VMEM((3, 8, 128), F32), pltpu.VMEM((120, 128), F32)],
+        in_specs=vmem(3),
         out_specs=vmem(2),
         name="assemble",
-    )(*here(got, map_z))
-
-
-def thirds(x):
-    hi, rest = x.astype(BF16), x
-    rest = x - hi.astype(F32)
-    mid = rest.astype(BF16)
-    low = (rest - mid.astype(F32)).astype(BF16)
-    return jnp.concatenate([hi.astype(F32), mid.astype(F32), low.astype(F32)], axis=0).astype(BF16)
-
-
-def spread_columns(values, index, columns, first):
-    target = rows_of((columns, 128)) + first
-    hot = jnp.where(jnp.broadcast_to(index, (columns, 128)) == target, 1.0, 0.0).astype(BF16)
-    both = lax.dot_general(thirds(values), hot, NT, preferred_element_type=F32)
-    return both[0:8] + (both[8:16] + both[16:24])
-
-
-def fold_z_kernel(products, below, above, map_z, own, out):
+    )(*here(got, map_z, stored))
+
+
+def meet(low, high):
+    return jnp.where(rows_of((8, 128), 1) < 64, low, high)
+
+
+def fold_layers(spread, own, part, maps_at, above, below):
     lower = rows_of((8, 128), 1) < 64
-    value = jnp.where(lower, turn(below[...]), turn(above[...]))
-    added = spread_columns(value, map_z[...], 384, 0)
-    own[...] = products[0] + added[:, 0:128]
-    first = products[1] + added[:, 128:256]
-    second = products[2] + added[:, 256:384]
-    tile = jnp.concatenate([first[0:3], second[0:3], jnp.zeros((2, 128), F32)], axis=0)
-    out[...] = jnp.broadcast_to(tile[None], out.shape)
-
-
-def fold_z(products, below, above, map_z, bricks):
-    return pl.pallas_call(
-        fold_z_kernel,
-        out_shape=[pltpu.VMEM((8, 128), F32), pltpu.VMEM((bricks, 8, 128), F32)],
-        in_specs=vmem(4),
-        out_specs=vmem(2),
-        name="fold_z",
-    )(*here(products, below, above, map_z))
-
-
-def fold_kernel(grid, own, got, maps, stored, gram, product, out):
+
+    def pair(low, low_index, high, high_index, base):
+        return jnp.concatenate([spread(low, low_index, base + 64, 64), spread(high, high_index, base, 64)], axis=1)
+
+    def folded(home, x_ghosts, y_ghosts, map_x, map_y):
+        sides = x_ghosts + pair(y_ghosts[-1], map_y(-1), y_ghosts[1], map_y(1), 128)
+        return home + spread(y_ghosts[0], map_y(0), 0, 128) + spread(sides, map_x, 0, 128)
+
+    y_ghosts = {dx: meet(part(dx, -1, 1), part(dx, 1, 1)) for dx in (-1, 0, 1)}
+    x_ghosts = meet(part(-1, 0, 0), part(1, 0, 0))
+    layers = [folded(own, x_ghosts, y_ghosts, maps_at(0)[6:7], lambda dx: maps_at(dx)[7:8])]
+    for message, kept in ((above, lower), (below, jnp.logical_not(lower))):
+
+        def sent(dx, dy, message=message, kept=kept):
+            index = message[9 + 3 * (dx + 1) + dy : 10 + 3 * (dx + 1) + dy, :]
+            return jnp.where(kept, part(dx, dy, 2), 0.0), index
+
+        y_ghosts = {dx: pair(*sent(dx, -1), *sent(dx, 1), 256) for dx in (-1, 0, 1)}
+        x_ghosts = pair(*sent(-1, 0), *sent(1, 0), 128)
+        home = spread(*sent(0, 0), 0, 128)
+        layers.append(folded(home, x_ghosts, y_ghosts, message[20:21, :], lambda dx, message=message: message[18 + dx : 19 + dx, :]))
+    return layers
+
+
+def fold_kernel(grid, own, got, maps, below, above, stored, gram, out):
     at = brick_reader(grid)
-    lower = rows_of((8, 128), 1) < 64
-
-    def from_y(dx):
-        return jnp.where(lower, turn(at(got, dx, -1)), turn(at(got, dx, 1)))
-
-    def second(value):
-        return jnp.concatenate([value[3:6], jnp.zeros((5, 128), F32)], axis=0)
-
-    def ghost(dx):
-        index = at(maps, dx, 0)[7:8].astype(jnp.int32)
-        return at(got, dx, 0) + spread_columns(second(from_y(dx)), index, 128, 128)
-
-    mine = at(maps, 0, 0)
-    total = own[...] + spread_columns(second(from_y(0)), mine[7:8].astype(jnp.int32), 128, 0)
-    from_x = jnp.where(lower, turn(ghost(-1)), turn(ghost(1)))
-    total = total + spread_columns(from_x, mine[6:7].astype(jnp.int32), 128, 0)
-    product[...] = total
-    last = rows_of((32, 128)) == 30
+    blank = jnp.zeros((5, 128), F32)
+    target = rows_of((128, 128))
+
+    def spread(values, index, first, count):
+        hi, lo = split(values)
+        left = jnp.concatenate([hi.astype(F32), lo.astype(F32)], axis=0).astype(BF16)
+        hot = jnp.where(jnp.broadcast_to(index.astype(jnp.int32) - first, (count, 128)) == target[0:count], 1.0, 0.0).astype(BF16)
+        both = lax.dot_general(left, hot, NT, preferred_element_type=F32)
+        return both[0:8] + both[8:16]
+
+    def part(dx, dy, q):
+        return turn(jnp.concatenate([at(got, dx, dy)[3 * q : 3 * q + 3], blank], axis=0))
+
+    layers = fold_layers(spread, own[...], part, lambda dx: at(maps, dx, 0), above, below)
     column = jnp.zeros((32, 128), F32)
     for c in range(3):
-        row = total[c : c + 1]
-        column = column + jnp.where(last, row, stored[c]) * row
+        at_rows = pl.ds(24 + 32 * c, 32)
+        bases = (stored[c], above[at_rows, :], below[at_rows, :])
+        for layer, vectors in zip(layers, bases):
+            column = column + vectors * layer[c : c + 1]
     column = jnp.sum(column, axis=1, keepdims=True)
-    full = jnp.where(rows_of((32, 128), 1) == 30, column, gram[...])
-    tile = full[0:8]
+    lane = rows_of((32, 128), 1)
+    full = jnp.where(lane == 30, column, gram[...])
+    tail = jnp.where((lane >= 16) & (lane < 32), full, 0.0)
+    first = full[0:4]
     for b in range(1, 4):
-        tile = tile + pltpu.roll(full[8 * b : 8 * b + 8], 32 * b, 1)
-    out[...] = jnp.broadcast_to(tile[None], out.shape)
-
-
-def fold(own, got, maps, stored, gram, grid):
+        first = first + pltpu.roll(full[4 * b : 4 * b + 4], 32 * b, 1)
+    second = pltpu.roll(tail[16:18], 112, 1)
+    for b in range(1, 8):
+        second = second + pltpu.roll(tail[16 + 2 * b : 18 + 2 * b], 16 * (b - 1), 1)
+    tile = [first, second] + [layer[0:3] for layer in layers] + [jnp.zeros((1, 128), F32)]
+    out[...] = jnp.broadcast_to(jnp.concatenate(tile, axis=0)[None], out.shape)
+
+
+def fold(own, got, maps, below, above, stored, gram, grid, copies):
     return pl.pallas_call(
         functools.partial(fold_kernel, grid),
-        out_shape=[pltpu.VMEM((8, 128), F32), pltpu.VMEM(got.shape, F32)],
-        in_specs=vmem(5),
+        out_shape=pltpu.VMEM((copies, 16, 128), F32),
+        in_specs=vmem(7),
+        out_specs=vmem(1)[0],
+        name="fold",
+    )(*here(own, got, maps, below, above, stored, gram))
+
+
+def column_kernel(got, product, out):
+    count = got.shape[0]
+    here_z = lax.axis_index("gz")
+
+    def vector(z, before, after):
+        return got[z, 6:9, :] + got[before, 9:12, :] + got[after, 12:15, :]
+
+    product[...] = jnp.zeros_like(product)
+    product[0:3, :] = vector(here_z, lax.rem(here_z + (count - 1), count), lax.rem(here_z + 1, count))
+    squares = jnp.zeros((3, 128), F32)
+    for z in range(count):
+        value = vector(z, (z - 1) % count, (z + 1) % count)
+        squares = squares + value * value
+    size = jnp.sum(jnp.sum(squares, axis=1, keepdims=True), axis=0, keepdims=True)
+    tile = got[0, 0:8, :]
+    for z in range(1, count):
+        tile = tile + got[z, 0:8, :]
+    spot = (rows_of((8, 128)) == 4) & (rows_of((8, 128), 1) == 126)
+    tile = jnp.where(spot, size, tile)
+    out[...] = jnp.broadcast_to(tile[None], out.shape)
+
+
+def column_of(got, bricks):
+    return pl.pallas_call(
+        column_kernel,
+        out_shape=[pltpu.VMEM((8, 128), F32), pltpu.VMEM((bricks, 8, 128), F32)],
+        in_specs=vmem(1),
         out_specs=vmem(2),
-        name="fold",
-    )(*here(own, got, maps, stored, gram))
-
-
-def total_kernel(got, out):
-    out[...] = jnp.broadcast_to(jnp.sum(got[...], axis=0)[None], out.shape)
-
-
-def total_of(got, copies):
-    return pl.pallas_call(
-        total_kernel,
-        out_shape=pltpu.VMEM((copies,) + got.shape[1:], F32),
-        in_specs=vmem(1),
-        out_specs=vmem(1)[0],
-        name="total",
+        name="column",
     )(*here(got))
 
 
 def finish_kernel(entries, got, product, stored, result, correlations, norm):
     count = correlations.shape[1]
     packed = jnp.sum(got[...], axis=0) * (1.0 / entries)
-    full = jnp.concatenate([packed] + [pltpu.roll(packed, 128 - 32 * b, 1) for b in range(1, 4)], axis=0)
+    parts = [packed[0:4]] + [pltpu.roll(packed[0:4], 128 - 32 * b, 1) for b in range(1, 4)]
+    parts += [pltpu.roll(packed[4:6], (144 - 16 * b) % 128, 1) for b in range(8)]
+    full = jnp.concatenate(parts, axis=0)
     column = full[:, count : count + 1]
     line = jnp.sum(jnp.where(rows_of((32, 128)) == rows_of((32, 128), 1), column, 0.0), axis=0, keepdims=True)
     row = rows_of((32, 1))
@@ -600,7 +623,9 @@
     down = jnp.where(row < count, column, jnp.where(row == count, -1.0, 0.0))
     across = jnp.where(lane < count, line, jnp.where(lane == count, -2.0, 0.0))
     size = jnp.where(row < count, full * across * down, jnp.where((row == count) & (lane == count), full, 0.0))
-    size = jnp.where(rows_of((32, 128), 1) <= count, size, 0.0)
+    wide = rows_of((32, 128), 1)
+    twice = jnp.where((row < 16) & (wide >= 16) & (wide < count), 2.0, 1.0)
+    size = jnp.where((wide <= count) & ((row < 16) | (wide >= 16)), size * twice, 0.0)
     size = jnp.sum(jnp.sum(size, axis=1, keepdims=True), axis=0, keepdims=True)
     length = jnp.sqrt(jnp.maximum(size, 0.0) + 1e-06)
     norm[...] = length
@@ -634,20 +659,18 @@
     def exchange(x):
         return lax.all_to_all(x, plane, 0, 0)
 
-    packed = pack(positions, basis, map_x, map_y, nx * ny)
+    packed = pack(positions, basis, map_x, map_y, map_z, nx * ny)
     raw = exchange(packed)
     table, _ = lax.optimization_barrier((table, packed))
-    mixed, map_row = mixing(table, fit_w1, map_z)
-    layers, lists, stored, gram = lists_of(fit_w2, fit_b1, fit_b2, fit_out, neighbours, used_count, kinds, basis)
+    mixed, map_row, stored = mixing(table, fit_w1, map_z, basis)
+    layers, lists, gram = lists_of(fit_w2, fit_b1, fit_b2, fit_out, neighbours, used_count, kinds, stored)
     raw, map_row = lax.optimization_barrier((raw, map_row))
-    tiles, message = assemble(raw, map_row, (nx, ny))
+    tiles, message = assemble(raw, map_row, stored, (nx, ny))
     below, above = lax.ppermute(message, "gz", up), lax.ppermute(message, "gz", down)
-    products, outgoing = product(tiles, below, above, lists, (*mixed, *layers))
-    below, above = lax.ppermute(outgoing, "gz", up), lax.ppermute(outgoing, "gz", down)
-    own, shared = fold_z(products, below, above, map_row, nx * ny)
-    hessian_vec, summary = fold(own, exchange(shared), raw, stored, gram, (nx, ny))
-    summary = total_of(exchange(summary), nz)
-    summary = lax.all_to_all(summary, "gz", 0, 0)
+    own, shared = product(tiles, below, above, lists, (*mixed, *layers), nx * ny)
+    summary = fold(own, exchange(shared), raw, below, above, stored, gram, (nx, ny), nz)
+    hessian_vec, summary = column_of(lax.all_to_all(summary, "gz", 0, 0), nx * ny)
+    summary = exchange(summary)
     entries = 3 * positions.shape[-1] * nx * ny * nz
     next_vector, correlations, vector_norm = finish(summary, hessian_vec, stored, positions.shape, basis.shape[0], entries)
     return next_vector, correlations.reshape(-1), vector_norm.reshape(())

time: 93.1 us -> 91.6 us (0.984)
  starting transfers between devices: 26.8 us -> 21.5 us
  blocking collectives: 41.6 us -> 45.2 us
    ppermute x2 -> x0, starting transfers between devices: 5.28 us -> none  [the longest x1 2.96 us: on_device(): lax.ppermute(outgoing, 'gz', up)]
    all_to_all x2, blocking collectives: 24.7 us -> 27.8 us  [exchange(): return lax.all_to_all(x, plane, 0, 0)]
    ppermute x2 -> x0, waiting for transfers between devices: 2.59 us -> none  [the longest x1 2.59 us: on_device(): lax.ppermute(outgoing, 'gz', up)]
    all_to_all x1, waiting for transfers between devices: 3.76 us -> 5.01 us  [exchange(): return lax.all_to_all(x, plane, 0, 0)]
    pallas_call x5 -> x4, Pallas kernels: 8.4 us -> 9.19 us  [the longest x1 6.1 us: product(): pl.pallas_call(product_kernel, out_shape=[pltpu.VMEM((8, 128), F32), pltp...]
  transfers between devices with their start and end apart: 5 -> 3, of which waited for: 3 -> 2; matrix products, arithmetic and copies ran while one was open for 0% -> 0% of each run, Pallas kernels for 6% -> 6%
where the time goes in v4:
time: 91.6 us; the launch traced here: 91.1 us
  blocking collectives  45.2 us (49%)
  starting transfers between devices  21.5 us (23%)
  Pallas kernels  15.7 us (17%)
  waiting for transfers between devices  7.94 us (9%)
    all_to_all x2, blocking collectives, exchange(): return lax.all_to_all(x, plane, 0, 0)  27.8 us
    all_to_all x1, blocking collectives, on_device(): lax.all_to_all(summary, 'gz', 0, 0)  17.4 us
    all_to_all x1, starting transfers between devices, exchange(): return lax.all_to_all(x, plane, 0, 0)  10.4 us
    ppermute x1, starting transfers between devices, on_device(): lax.ppermute(message, 'gz', down)  9.24 us
    pallas_call x1, Pallas kernels, product(): pl.pallas_call(product_kernel, out_shape=[pltpu.VMEM((8, 128), F32), pltp...  6.1 us
    pallas_call x2, Pallas kernels, from_hbm(): pl.pallas_call(kernel, out_shape=[pltpu.VMEM(s, d) for s, d in shapes], i...  5.36 us
    all_to_all x1, waiting for transfers between devices, exchange(): return lax.all_to_all(x, plane, 0, 0)  5.01 us
    ppermute x1, waiting for transfers between devices, on_device(): lax.ppermute(message, 'gz', up)  2.93 us
  transfers between devices with their start and end apart: 3, of which 2 were waited for; matrix products, arithmetic and copies ran while one was open for 0% of the time, Pallas kernels for 6%

profile of v4, /device:TPU:1, one launch (start us, length us, event | category | flops | bytes accessed | tf_op | source)
XLA Modules:
  0.0 91.1 jit_solution(7679543119591974905)
XLA Ops:
  0.6 1.6 %pack.1 = f32[32,16,128]{2,1,0:T(8,128)} custom-call(f32[3,1,1,1,128]{4,3,2,1,0:T(1,128)} %places_at.1, f32[30,3,1,1,1,128]{5,4,3,2,1,0:T(1,128)} %basis_at.3, s32[1,1,1,2,64]{4,3,2,1,0:T(2,128)} %map_x_at.1, s32[1,1,1,2,64]{4,3,2,1,0:T(2,128)} %map_y_at.1, s32[1,1,1,2,64]{4,3,2,1,0:T(2,128)} %map_at.1), custom_call_target="tpu_custom_call" | custom-call | tf_op jit(solution)/shard_map/pack/pallas_call | solution.py:423
  2.2 10.4 %all-to-all-start = ((f32[32,16,128]{2,1,0:T(8,128)}), f32[32,16,128]{2,1,0:T(8,128)S(1)}, u32[]{:S(2)}, u32[]{:S(2)}) async-start(f32[32,16,128]{2,1,0:T(8,128)} %pack.1), calls=%async_computation | async-start | bytes 524288 | tf_op jit(solution)/shard_map/all_to_all | solution.py:660
  12.6 4.1 %mixing.1 = (bf16[512,256]{1,0:T(8,128)(2,1)S(1)}, bf16[512,256]{1,0:T(8,128)(2,1)S(1)}, bf16[256,512]{1,0:T(8,128)(2,1)S(1)}, bf16[256,512]{1,0:T(8,128)(2,1)S(...) custom-call(f32[2,16,100]{2,1,0:T(8,128)} %table_at, f32[240,1600]{1,0:T(8,128)} %bitcast.6, ...), custom_call_target="tpu_custom_call" | custom-call | tf_op jit(solution)/shard_map/mixing/pallas_call | solution.py:138
  16.7 5.0 %all-to-all-done.got.maps = f32[32,16,128]{2,1,0:T(8,128)S(1)} async-done(((f32[32,16,128]{2,1,0:T(8,128)}), f32[32,16,128]{2,1,0:T(8,128)S(1)}, u32[]{:S(2)}, u32[]{:S(2)}) %all-to-all-start) | async-done | bytes 262176 | tf_op jit(solution)/shard_map/all_to_all | solution.py:660
  21.7 0.3 assemble.1
  21.9 9.2 %collective-permute-start.1 = (f32[120,128]{1,0:T(8,128)S(1)}, f32[120,128]{1,0:T(8,128)S(1)}, u32[]{:S(2)}, u32[]{:S(2)}) collective-permute-start(f32[120,128]{1,0:T(8,128)S(1)} %get-tuple-element.36), channel_id=1, source_target_pairs={{1,0},{2,1},{3,2},{4,3},{5,4},{6,5},{7,6},{8,7},{9,8},{10,9},{11,1... | collective-permute-start | bytes 184328 | tf_op jit(solution)/shard_map/ppermute | solution.py:669
  31.2 1.9 %collective-permute-start = (f32[120,128]{1,0:T(8,128)S(1)}, f32[120,128]{1,0:T(8,128)S(1)}, u32[]{:S(2)}, u32[]{:S(2)}) collective-permute-start(f32[120,128]{1,0:T(8,128)S(1)} %get-tuple-element.36), channel_id=1, source_target_pairs={{0,1},{1,2},{2,3},{3,4},{4,5},{5,6},{6,7},{7,8},{8,9},{9,10},{10,1... | collective-permute-start | bytes 184328 | tf_op jit(solution)/shard_map/ppermute | solution.py:669
  33.1 1.3 %lists.1 = (bf16[256,256]{1,0:T(8,128)(2,1)S(1)}, bf16[256,256]{1,0:T(8,128)(2,1)S(1)}, bf16[256,256]{1,0:T(8,128)(2,1)S(1)}, bf16[256,256]{1,0:T(8,128)(2,1)S(1...) custom-call(f32[240,240]{1,0:T(8,128)} %w2_at.1, ...), custom_call_target="tpu_custom_call" | custom-call | tf_op jit(solution)/shard_map/lists/pallas_call | solution.py:138
  34.4 0.0 collective-permute-done.1.above
  34.4 2.9 %collective-permute-done.below = f32[120,128]{1,0:T(8,128)S(1)} collective-permute-done((f32[120,128]{1,0:T(8,128)S(1)}, f32[120,128]{1,0:T(8,128)S(1)}, u32[]{:S(2)}, u32[]{:S(2)}) %collective-permute-start) | collective-permute-done | bytes 61472 | tf_op jit(solution)/shard_map/ppermute | solution.py:669
  37.4 6.1 %product.1 = (f32[8,128]{1,0:T(8,128)S(1)}, f32[32,16,128]{2,1,0:T(8,128)S(1)}) custom-call(f32[3,8,128]{2,1,0:T(8,128)S(1)} %get-tuple-element.35.tiles, f32[120,128]{1,0:T(8,128)S(1)} %collective-permute-done.below, f32[120,128]{1,0:T(8,128)S(1)} %collective-permute-done.1.above, s32[128,128]{1,0:T(8,128)S(1)} %get-tuple-element.37.ids_t, ...), custom_call_target="tpu_custom_call" | custom-call | tf_op jit(solution)/shard_map/product/pallas_call | solution.py:392
  43.5 13.9 %all_to_all.20.got = f32[32,16,128]{2,1,0:T(8,128)S(1)} all-to-all(f32[32,16,128]{2,1,0:T(8,128)S(1)} %get-tuple-element.50), channel_id=1, replica_groups=mesh['gx'=4,'gy'=8,'gz'=16] {'gx','gy'}, dimensions={0} | all-to-all | bytes 524288 | tf_op jit(solution)/shard_map/all_to_all | solution.py:660
  57.3 1.4 %fold.1 = f32[16,16,128]{2,1,0:T(8,128)S(1)} custom-call(f32[8,128]{1,0:T(8,128)S(1)} %get-tuple-element.49.own, f32[32,16,128]{2,1,0:T(8,128)S(1)} %all_to_all.20.got, f32[32,16,128]{2,1,0:T(8,128)S(1)} %all-to-all-done.got.maps, f32[120,128]{1,0:T(8,128)S(1)} %collective-permute-done.below, f32[120,128]{1,0:T(8,128)S(1)} %collective-permute-done.1.above, ...), custom_call_target="tpu_custom_call" | custom-call | tf_op jit(solution)/shard_map/fold/pallas_call | solution.py:572
  58.7 17.4 %all_to_all.21.got = f32[16,16,128]{2,1,0:T(8,128)S(1)} all-to-all(f32[16,16,128]{2,1,0:T(8,128)S(1)} %fold.1), channel_id=1, replica_groups=mesh['gx'=4,'gy'=8,'gz'=16] {'gz'}, dimensions={0} | all-to-all | bytes 262144 | tf_op jit(solution)/shard_map/all_to_all | solution.py:672
  76.2 0.1 column.1
  76.3 13.9 %all_to_all.22.got = f32[32,8,128]{2,1,0:T(8,128)S(1)} all-to-all(f32[32,8,128]{2,1,0:T(8,128)S(1)} %get-tuple-element.52), channel_id=1, replica_groups=mesh['gx'=4,'gy'=8,'gz'=16] {'gx','gy'}, dimensions={0} | all-to-all | bytes 262144 | tf_op jit(solution)/shard_map/all_to_all | solution.py:660
  90.2 0.9 finish.1
Async XLA Ops:
  2.2 19.4 %all-to-all-start = ((f32[32,16,128]{2,1,0:T(8,128)}), f32[32,16,128]{2,1,0:T(8,128)S(1)}, u32[]{:S(2)}, u32[]{:S(2)}) async-start(f32[32,16,128]{2,1,0:T(8,128)} %pack.1), calls=%async_computation | async-start | bytes 524288 | tf_op jit(solution)/shard_map/all_to_all | solution.py:660
  21.9 12.5 %collective-permute-start.1 = (f32[120,128]{1,0:T(8,128)S(1)}, f32[120,128]{1,0:T(8,128)S(1)}, u32[]{:S(2)}, u32[]{:S(2)}) collective-permute-start(f32[120,128]{1,0:T(8,128)S(1)} %get-tuple-element.36), channel_id=1, source_target_pairs={{1,0},{2,1},{3,2},{4,3},{5,4},{6,5},{7,6},{8,7},{9,8},{10,9},{11,1... | collective-permute-start | bytes 184328 | tf_op jit(solution)/shard_map/ppermute | solution.py:669
  31.2 6.2 %collective-permute-start = (f32[120,128]{1,0:T(8,128)S(1)}, f32[120,128]{1,0:T(8,128)S(1)}, u32[]{:S(2)}, u32[]{:S(2)}) collective-permute-start(f32[120,128]{1,0:T(8,128)S(1)} %get-tuple-element.36), channel_id=1, source_target_pairs={{0,1},{1,2},{2,3},{3,4},{4,5},{5,6},{6,7},{7,8},{8,9},{9,10},{10,1... | collective-permute-start | bytes 184328 | tf_op jit(solution)/shard_map/ppermute | solution.py:669

commit v5 on v4

--- a/solution.py
+++ b/solution.py
@@ -383,7 +383,9 @@
         for q in range(4):
             rows[q, c] = jnp.concatenate([both[2 * q : 2 * q + 1], both[2 * q + 1 : 2 * q + 2]], axis=1)
         out[c : c + 1, :] = rows[0, c] - jnp.sum(centre[c], axis=0, keepdims=True)
-    tile = [rows[q, c] for q in range(1, 4) for c in range(3)] + [jnp.zeros((7, 128), F32)]
+    half = rows_of((1, 128), 1) < 64
+    tile = [rows[q, c] for q in range(1, 4) for c in range(3)]
+    tile += [jnp.where(half, above[10:11, :], below[10:11, :]), above[9:10, :], below[9:10, :], jnp.zeros((4, 128), F32)]
     sent[...] = jnp.broadcast_to(jnp.concatenate(tile, axis=0)[None], sent.shape)
 
 
@@ -408,30 +410,29 @@
     )(*here(tiles, below, above, *lists, *weights))
 
 
-def pack_kernel(places_at, basis_at, map_x_at, map_y_at, map_z_at, out, places, tangent, map_x, map_y, map_z, semaphores):
+def pack_kernel(places_at, basis_at, map_x_at, map_y_at, out, places, tangent, map_x, map_y, semaphores):
     last = basis_at.shape[0] - 1
-    copies = fetch((places_at, basis_at.at[last], map_x_at, map_y_at, map_z_at), (places, tangent, map_x, map_y, map_z), semaphores)
+    copies = fetch((places_at, basis_at.at[last], map_x_at, map_y_at), (places, tangent, map_x, map_y), semaphores)
     for copy in copies:
         copy.wait()
     rows = [places[c, 0, 0] for c in range(3)] + [tangent[c, 0, 0] for c in range(3)]
-    rows += [halves(m).astype(F32) for m in (map_x, map_y, map_z)] + [jnp.zeros((7, 128), F32)]
+    rows += [halves(m).astype(F32) for m in (map_x, map_y)]
     out[...] = jnp.broadcast_to(jnp.concatenate(rows, axis=0)[None], out.shape)
 
 
-def pack(positions, basis, map_x, map_y, map_z, bricks):
-    arrays = (positions, basis, map_x, map_y, map_z)
+def pack(positions, basis, map_x, map_y, bricks):
+    arrays = (positions, basis, map_x, map_y)
     return pl.pallas_call(
         pack_kernel,
-        out_shape=pltpu.VMEM((bricks, 16, 128), F32),
-        in_specs=[pl.BlockSpec(memory_space=pltpu.HBM)] * 5,
+        out_shape=pltpu.VMEM((bricks, 8, 128), F32),
+        in_specs=[pl.BlockSpec(memory_space=pltpu.HBM)] * 4,
         out_specs=vmem(1)[0],
         scratch_shapes=[
             pltpu.VMEM(positions.shape, F32),
             pltpu.VMEM(basis.shape[1:], F32),
             pltpu.VMEM(map_x.shape, jnp.int32),
             pltpu.VMEM(map_y.shape, jnp.int32),
-            pltpu.VMEM(map_z.shape, jnp.int32),
-            pltpu.SemaphoreType.DMA((5,)),
+            pltpu.SemaphoreType.DMA((4,)),
         ],
         name="pack",
     )(*(pltpu.with_memory_space_constraint(a, pltpu.HBM) for a in arrays))
@@ -465,7 +466,7 @@
     step_y = jnp.where(row == 1, 1.0, 0.0)
     middle, ghosts, index = {}, {}, {}
     for dy in (-1, 0, 1):
-        own, low, high = (at(got, dx, dy)[0:8] for dx in (0, -1, 1))
+        own, low, high = (at(got, dx, dy) for dx in (0, -1, 1))
         from_low = lane_pick(low, turn(as_index(low[6:7])))
         from_high = lane_pick(high, turn(as_index(high[6:7])))
         middle[dy] = own
@@ -485,17 +486,15 @@
     message[0:8, :] = jnp.where(
         chosen < 128, lane_pick(middle[0], low), jnp.where(chosen < 256, lane_pick(ghosts[0], low), lane_pick(third, low))
     )
-    maps = [at(got, dx, dy)[8:9] for dx in (-1, 0, 1) for dy in (-1, 0, 1)]
-    maps += [at(got, dx, 0)[7:8] for dx in (-1, 0, 1)] + [at(got, 0, 0)[6:7], jnp.zeros((3, 128), F32)]
-    message[8:24, :] = jnp.concatenate(maps, axis=0)
+    message[8:16, :] = jnp.concatenate([middle[0][6:8], map_z[...].astype(F32), jnp.zeros((5, 128), F32)], axis=0)
     for c in range(3):
-        message[24 + 32 * c : 56 + 32 * c, :] = stored[c]
+        message[16 + 32 * c : 48 + 32 * c, :] = stored[c]
 
 
 def assemble(got, map_z, stored, grid):
     return pl.pallas_call(
         functools.partial(assemble_kernel, grid),
-        out_shape=[pltpu.VMEM((3, 8, 128), F32), pltpu.VMEM((120, 128), F32)],
+        out_shape=[pltpu.VMEM((3, 8, 128), F32), pltpu.VMEM((112, 128), F32)],
         in_specs=vmem(3),
         out_specs=vmem(2),
         name="assemble",
@@ -506,7 +505,7 @@
     return jnp.where(rows_of((8, 128), 1) < 64, low, high)
 
 
-def fold_layers(spread, own, part, maps_at, above, below):
+def fold_layers(spread, own, part, row_at, maps_at, above, below):
     lower = rows_of((8, 128), 1) < 64
 
     def pair(low, low_index, high, high_index, base):
@@ -519,16 +518,15 @@
     y_ghosts = {dx: meet(part(dx, -1, 1), part(dx, 1, 1)) for dx in (-1, 0, 1)}
     x_ghosts = meet(part(-1, 0, 0), part(1, 0, 0))
     layers = [folded(own, x_ghosts, y_ghosts, maps_at(0)[6:7], lambda dx: maps_at(dx)[7:8])]
-    for message, kept in ((above, lower), (below, jnp.logical_not(lower))):
-
-        def sent(dx, dy, message=message, kept=kept):
-            index = message[9 + 3 * (dx + 1) + dy : 10 + 3 * (dx + 1) + dy, :]
-            return jnp.where(kept, part(dx, dy, 2), 0.0), index
+    for message, kept, at_row in ((above, lower, 10), (below, jnp.logical_not(lower), 11)):
+
+        def sent(dx, dy, kept=kept):
+            return jnp.where(kept, part(dx, dy, 2), 0.0), row_at(dx, dy, 9)
 
         y_ghosts = {dx: pair(*sent(dx, -1), *sent(dx, 1), 256) for dx in (-1, 0, 1)}
         x_ghosts = pair(*sent(-1, 0), *sent(1, 0), 128)
         home = spread(*sent(0, 0), 0, 128)
-        layers.append(folded(home, x_ghosts, y_ghosts, message[20:21, :], lambda dx, message=message: message[18 + dx : 19 + dx, :]))
+        layers.append(folded(home, x_ghosts, y_ghosts, message[8:9, :], lambda dx, at_row=at_row: row_at(dx, 0, at_row)))
     return layers
 
 
@@ -547,10 +545,12 @@
     def part(dx, dy, q):
         return turn(jnp.concatenate([at(got, dx, dy)[3 * q : 3 * q + 3], blank], axis=0))
 
-    layers = fold_layers(spread, own[...], part, lambda dx: at(maps, dx, 0), above, below)
+    layers = fold_layers(
+        spread, own[...], part, lambda dx, dy, r: at(got, dx, dy)[r : r + 1], lambda dx: at(maps, dx, 0), above, below
+    )
     column = jnp.zeros((32, 128), F32)
     for c in range(3):
-        at_rows = pl.ds(24 + 32 * c, 32)
+        at_rows = pl.ds(16 + 32 * c, 32)
         bases = (stored[c], above[at_rows, :], below[at_rows, :])
         for layer, vectors in zip(layers, bases):
             column = column + vectors * layer[c : c + 1]
@@ -659,7 +659,7 @@
     def exchange(x):
         return lax.all_to_all(x, plane, 0, 0)
 
-    packed = pack(positions, basis, map_x, map_y, map_z, nx * ny)
+    packed = pack(positions, basis, map_x, map_y, nx * ny)
     raw = exchange(packed)
     table, _ = lax.optimization_barrier((table, packed))
     mixed, map_row, stored = mixing(table, fit_w1, map_z, basis)

time: 91.6 us -> 90.3 us (0.986)
  waiting for transfers between devices: 7.94 us -> 6.61 us
    all_to_all x1, waiting for transfers between devices: 5.01 us -> 3.72 us  [exchange(): return lax.all_to_all(x, plane, 0, 0)]
where the time goes in v5:
time: 90.3 us; the launch traced here: 89.8 us
  blocking collectives  45.3 us (50%)
  starting transfers between devices  21.5 us (24%)
  Pallas kernels  15.6 us (17%)
  waiting for transfers between devices  6.61 us (7%)
    all_to_all x2, blocking collectives, exchange(): return lax.all_to_all(x, plane, 0, 0)  27.9 us
    all_to_all x1, blocking collectives, on_device(): lax.all_to_all(summary, 'gz', 0, 0)  17.4 us
    all_to_all x1, starting transfers between devices, exchange(): return lax.all_to_all(x, plane, 0, 0)  10.3 us
    ppermute x1, starting transfers between devices, on_device(): lax.ppermute(message, 'gz', down)  9.26 us
    pallas_call x1, Pallas kernels, product(): pl.pallas_call(product_kernel, out_shape=[pltpu.VMEM((8, 128), F32), pltp...  6.1 us
    pallas_call x2, Pallas kernels, from_hbm(): pl.pallas_call(kernel, out_shape=[pltpu.VMEM(s, d) for s, d in shapes], i...  5.36 us
    all_to_all x1, waiting for transfers between devices, exchange(): return lax.all_to_all(x, plane, 0, 0)  3.72 us
    ppermute x1, waiting for transfers between devices, on_device(): lax.ppermute(message, 'gz', up)  2.88 us
  transfers between devices with their start and end apart: 3, of which 2 were waited for; matrix products, arithmetic and copies ran while one was open for 0% of the time, Pallas kernels for 6%

profile of v5, /device:TPU:1, one launch (start us, length us, event | category | flops | bytes accessed | tf_op | source)
XLA Modules:
  0.0 89.8 jit_solution(2441131768831689493)
XLA Ops:
  0.6 1.5 %pack.1 = f32[32,8,128]{2,1,0:T(8,128)} custom-call(f32[3,1,1,1,128]{4,3,2,1,0:T(1,128)} %places_at.1, f32[30,3,1,1,1,128]{5,4,3,2,1,0:T(1,128)} %basis_at.3, s32[1,1,1,2,64]{4,3,2,1,0:T(2,128)} %map_x_at.1, s32[1,1,1,2,64]{4,3,2,1,0:T(2,128)} %map_y_at.1), custom_call_target="tpu_custom_call" | custom-call | tf_op jit(solution)/shard_map/pack/pallas_call | solution.py:425
  2.1 10.3 %all-to-all-start = ((f32[32,8,128]{2,1,0:T(8,128)}), f32[32,8,128]{2,1,0:T(8,128)S(1)}, u32[]{:S(2)}, u32[]{:S(2)}) async-start(f32[32,8,128]{2,1,0:T(8,128)} %pack.1), calls=%async_computation | async-start | bytes 262144 | tf_op jit(solution)/shard_map/all_to_all | solution.py:660
  12.5 4.1 %mixing.1 = (bf16[512,256]{1,0:T(8,128)(2,1)S(1)}, bf16[512,256]{1,0:T(8,128)(2,1)S(1)}, bf16[256,512]{1,0:T(8,128)(2,1)S(1)}, bf16[256,512]{1,0:T(8,128)(2,1)S(...) custom-call(f32[2,16,100]{2,1,0:T(8,128)} %table_at, f32[240,1600]{1,0:T(8,128)} %bitcast.6, ...), custom_call_target="tpu_custom_call" | custom-call | tf_op jit(solution)/shard_map/mixing/pallas_call | solution.py:138
  16.5 3.7 %all-to-all-done.got.maps = f32[32,8,128]{2,1,0:T(8,128)S(1)} async-done(((f32[32,8,128]{2,1,0:T(8,128)}), f32[32,8,128]{2,1,0:T(8,128)S(1)}, u32[]{:S(2)}, u32[]{:S(2)}) %all-to-all-start) | async-done | bytes 131104 | tf_op jit(solution)/shard_map/all_to_all | solution.py:660
  20.3 0.3 assemble.1
  20.6 9.3 %collective-permute-start.1 = (f32[112,128]{1,0:T(8,128)S(1)}, f32[112,128]{1,0:T(8,128)S(1)}, u32[]{:S(2)}, u32[]{:S(2)}) collective-permute-start(f32[112,128]{1,0:T(8,128)S(1)} %get-tuple-element.36), channel_id=1, source_target_pairs={{1,0},{2,1},{3,2},{4,3},{5,4},{6,5},{7,6},{8,7},{9,8},{10,9},{11,1... | collective-permute-start | bytes 172040 | tf_op jit(solution)/shard_map/ppermute | solution.py:669
  29.8 1.9 %collective-permute-start = (f32[112,128]{1,0:T(8,128)S(1)}, f32[112,128]{1,0:T(8,128)S(1)}, u32[]{:S(2)}, u32[]{:S(2)}) collective-permute-start(f32[112,128]{1,0:T(8,128)S(1)} %get-tuple-element.36), channel_id=1, source_target_pairs={{0,1},{1,2},{2,3},{3,4},{4,5},{5,6},{6,7},{7,8},{8,9},{9,10},{10,1... | collective-permute-start | bytes 172040 | tf_op jit(solution)/shard_map/ppermute | solution.py:669
  31.7 1.3 %lists.1 = (bf16[256,256]{1,0:T(8,128)(2,1)S(1)}, bf16[256,256]{1,0:T(8,128)(2,1)S(1)}, bf16[256,256]{1,0:T(8,128)(2,1)S(1)}, bf16[256,256]{1,0:T(8,128)(2,1)S(1...) custom-call(f32[240,240]{1,0:T(8,128)} %w2_at.1, ...), custom_call_target="tpu_custom_call" | custom-call | tf_op jit(solution)/shard_map/lists/pallas_call | solution.py:138
  33.1 0.0 collective-permute-done.1.above
  33.1 2.9 %collective-permute-done.below = f32[112,128]{1,0:T(8,128)S(1)} collective-permute-done((f32[112,128]{1,0:T(8,128)S(1)}, f32[112,128]{1,0:T(8,128)S(1)}, u32[]{:S(2)}, u32[]{:S(2)}) %collective-permute-start) | collective-permute-done | bytes 57376 | tf_op jit(solution)/shard_map/ppermute | solution.py:669
  36.0 6.1 %product.1 = (f32[8,128]{1,0:T(8,128)S(1)}, f32[32,16,128]{2,1,0:T(8,128)S(1)}) custom-call(f32[3,8,128]{2,1,0:T(8,128)S(1)} %get-tuple-element.35.tiles, f32[112,128]{1,0:T(8,128)S(1)} %collective-permute-done.below, f32[112,128]{1,0:T(8,128)S(1)} %collective-permute-done.1.above, s32[128,128]{1,0:T(8,128)S(1)} %get-tuple-element.37.ids_t, ...), custom_call_target="tpu_custom_call" | custom-call | tf_op jit(solution)/shard_map/product/pallas_call | solution.py:394
  42.1 14.0 %all_to_all.20.got = f32[32,16,128]{2,1,0:T(8,128)S(1)} all-to-all(f32[32,16,128]{2,1,0:T(8,128)S(1)} %get-tuple-element.50), channel_id=1, replica_groups=mesh['gx'=4,'gy'=8,'gz'=16] {'gx','gy'}, dimensions={0} | all-to-all | bytes 524288 | tf_op jit(solution)/shard_map/all_to_all | solution.py:660
  56.0 1.4 %fold.1 = f32[16,16,128]{2,1,0:T(8,128)S(1)} custom-call(f32[8,128]{1,0:T(8,128)S(1)} %get-tuple-element.49.own, f32[32,16,128]{2,1,0:T(8,128)S(1)} %all_to_all.20.got, f32[32,8,128]{2,1,0:T(8,128)S(1)} %all-to-all-done.got.maps, f32[112,128]{1,0:T(8,128)S(1)} %collective-permute-done.below, f32[112,128]{1,0:T(8,128)S(1)} %collective-permute-done.1.above, ...), custom_call_target="tpu_custom_call" | custom-call | tf_op jit(solution)/shard_map/fold/pallas_call | solution.py:572
  57.5 17.4 %all_to_all.21.got = f32[16,16,128]{2,1,0:T(8,128)S(1)} all-to-all(f32[16,16,128]{2,1,0:T(8,128)S(1)} %fold.1), channel_id=1, replica_groups=mesh['gx'=4,'gy'=8,'gz'=16] {'gz'}, dimensions={0} | all-to-all | bytes 262144 | tf_op jit(solution)/shard_map/all_to_all | solution.py:672
  74.9 0.1 column.1
  75.0 13.9 %all_to_all.22.got = f32[32,8,128]{2,1,0:T(8,128)S(1)} all-to-all(f32[32,8,128]{2,1,0:T(8,128)S(1)} %get-tuple-element.52), channel_id=1, replica_groups=mesh['gx'=4,'gy'=8,'gz'=16] {'gx','gy'}, dimensions={0} | all-to-all | bytes 262144 | tf_op jit(solution)/shard_map/all_to_all | solution.py:660
  88.9 0.9 finish.1
Async XLA Ops:
  2.1 18.1 %all-to-all-start = ((f32[32,8,128]{2,1,0:T(8,128)}), f32[32,8,128]{2,1,0:T(8,128)S(1)}, u32[]{:S(2)}, u32[]{:S(2)}) async-start(f32[32,8,128]{2,1,0:T(8,128)} %pack.1), calls=%async_computation | async-start | bytes 262144 | tf_op jit(solution)/shard_map/all_to_all | solution.py:660
  20.6 12.5 %collective-permute-start.1 = (f32[112,128]{1,0:T(8,128)S(1)}, f32[112,128]{1,0:T(8,128)S(1)}, u32[]{:S(2)}, u32[]{:S(2)}) collective-permute-start(f32[112,128]{1,0:T(8,128)S(1)} %get-tuple-element.36), channel_id=1, source_target_pairs={{1,0},{2,1},{3,2},{4,3},{5,4},{6,5},{7,6},{8,7},{9,8},{10,9},{11,1... | collective-permute-start | bytes 172040 | tf_op jit(solution)/shard_map/ppermute | solution.py:669
  29.8 6.1 %collective-permute-start = (f32[112,128]{1,0:T(8,128)S(1)}, f32[112,128]{1,0:T(8,128)S(1)}, u32[]{:S(2)}, u32[]{:S(2)}) collective-permute-start(f32[112,128]{1,0:T(8,128)S(1)} %get-tuple-element.36), channel_id=1, source_target_pairs={{0,1},{1,2},{2,3},{3,4},{4,5},{5,6},{6,7},{7,8},{8,9},{9,10},{10,1... | collective-permute-start | bytes 172040 | tf_op jit(solution)/shard_map/ppermute | solution.py:669

commit v6 on v5

--- a/solution.py
+++ b/solution.py
@@ -216,7 +216,7 @@
         edge[18, rows, :] = rate
         return carry
 
-    lax.fori_loop(0, blocks, geometry, 0, unroll=8)
+    lax.fori_loop(0, blocks, geometry, 0, unroll=16)
 
     def pooling(kk, carry):
         sums = [[jnp.zeros((8, 128), F32) for _ in range(8)] for _ in range(2)]
@@ -357,7 +357,7 @@
         return tuple(result)
 
     zero = jnp.zeros((8, 128), F32)
-    centre = lax.fori_loop(0, blocks, backward, (zero, zero, zero), unroll=2)
+    centre = lax.fori_loop(0, blocks, backward, (zero, zero, zero), unroll=8)
     row8 = rows_of((8, 128))
     rows16 = [(rows_of((16, 128)) + 16 * rg).astype(F32).astype(BF16) for rg in range(4)]
     on = jnp.ones((16, 128), BF16)

time: 90.3 us -> 90.1 us (level)
  no operation moved by 1% of the time
where the time goes in v6:
time: 90.1 us; the launch traced here: 89.6 us
  blocking collectives  45.3 us (50%)
  starting transfers between devices  21.5 us (24%)
  Pallas kernels  15.4 us (17%)
  waiting for transfers between devices  6.61 us (7%)
    all_to_all x2, blocking collectives, exchange(): return lax.all_to_all(x, plane, 0, 0)  27.9 us
    all_to_all x1, blocking collectives, on_device(): lax.all_to_all(summary, 'gz', 0, 0)  17.4 us
    all_to_all x1, starting transfers between devices, exchange(): return lax.all_to_all(x, plane, 0, 0)  10.3 us
    ppermute x1, starting transfers between devices, on_device(): lax.ppermute(message, 'gz', down)  9.26 us
    pallas_call x1, Pallas kernels, product(): pl.pallas_call(product_kernel, out_shape=[pltpu.VMEM((8, 128), F32), pltp...  5.88 us
    pallas_call x2, Pallas kernels, from_hbm(): pl.pallas_call(kernel, out_shape=[pltpu.VMEM(s, d) for s, d in shapes], i...  5.36 us
    all_to_all x1, waiting for transfers between devices, exchange(): return lax.all_to_all(x, plane, 0, 0)  3.72 us
    ppermute x1, waiting for transfers between devices, on_device(): lax.ppermute(message, 'gz', up)  2.88 us
  transfers between devices with their start and end apart: 3, of which 2 were waited for; matrix products, arithmetic and copies ran while one was open for 0% of the time, Pallas kernels for 6%

profile of v6, /device:TPU:1, one launch (start us, length us, event | category | flops | bytes accessed | tf_op | source)
XLA Modules:
  0.0 89.6 jit_solution(12257805185288802759)
XLA Ops:
  0.6 1.5 %pack.1 = f32[32,8,128]{2,1,0:T(8,128)} custom-call(f32[3,1,1,1,128]{4,3,2,1,0:T(1,128)} %places_at.1, f32[30,3,1,1,1,128]{5,4,3,2,1,0:T(1,128)} %basis_at.3, s32[1,1,1,2,64]{4,3,2,1,0:T(2,128)} %map_x_at.1, s32[1,1,1,2,64]{4,3,2,1,0:T(2,128)} %map_y_at.1), custom_call_target="tpu_custom_call" | custom-call | tf_op jit(solution)/shard_map/pack/pallas_call | solution.py:425
  2.1 10.3 %all-to-all-start = ((f32[32,8,128]{2,1,0:T(8,128)}), f32[32,8,128]{2,1,0:T(8,128)S(1)}, u32[]{:S(2)}, u32[]{:S(2)}) async-start(f32[32,8,128]{2,1,0:T(8,128)} %pack.1), calls=%async_computation | async-start | bytes 262144 | tf_op jit(solution)/shard_map/all_to_all | solution.py:660
  12.5 4.1 %mixing.1 = (bf16[512,256]{1,0:T(8,128)(2,1)S(1)}, bf16[512,256]{1,0:T(8,128)(2,1)S(1)}, bf16[256,512]{1,0:T(8,128)(2,1)S(1)}, bf16[256,512]{1,0:T(8,128)(2,1)S(...) custom-call(f32[2,16,100]{2,1,0:T(8,128)} %table_at, f32[240,1600]{1,0:T(8,128)} %bitcast.6, ...), custom_call_target="tpu_custom_call" | custom-call | tf_op jit(solution)/shard_map/mixing/pallas_call | solution.py:138
  16.5 3.7 %all-to-all-done.got.maps = f32[32,8,128]{2,1,0:T(8,128)S(1)} async-done(((f32[32,8,128]{2,1,0:T(8,128)}), f32[32,8,128]{2,1,0:T(8,128)S(1)}, u32[]{:S(2)}, u32[]{:S(2)}) %all-to-all-start) | async-done | bytes 131104 | tf_op jit(solution)/shard_map/all_to_all | solution.py:660
  20.3 0.3 assemble.1
  20.6 9.3 %collective-permute-start.1 = (f32[112,128]{1,0:T(8,128)S(1)}, f32[112,128]{1,0:T(8,128)S(1)}, u32[]{:S(2)}, u32[]{:S(2)}) collective-permute-start(f32[112,128]{1,0:T(8,128)S(1)} %get-tuple-element.36), channel_id=1, source_target_pairs={{1,0},{2,1},{3,2},{4,3},{5,4},{6,5},{7,6},{8,7},{9,8},{10,9},{11,1... | collective-permute-start | bytes 172040 | tf_op jit(solution)/shard_map/ppermute | solution.py:669
  29.8 1.9 %collective-permute-start = (f32[112,128]{1,0:T(8,128)S(1)}, f32[112,128]{1,0:T(8,128)S(1)}, u32[]{:S(2)}, u32[]{:S(2)}) collective-permute-start(f32[112,128]{1,0:T(8,128)S(1)} %get-tuple-element.36), channel_id=1, source_target_pairs={{0,1},{1,2},{2,3},{3,4},{4,5},{5,6},{6,7},{7,8},{8,9},{9,10},{10,1... | collective-permute-start | bytes 172040 | tf_op jit(solution)/shard_map/ppermute | solution.py:669
  31.7 1.3 %lists.1 = (bf16[256,256]{1,0:T(8,128)(2,1)S(1)}, bf16[256,256]{1,0:T(8,128)(2,1)S(1)}, bf16[256,256]{1,0:T(8,128)(2,1)S(1)}, bf16[256,256]{1,0:T(8,128)(2,1)S(1...) custom-call(f32[240,240]{1,0:T(8,128)} %w2_at.1, ...), custom_call_target="tpu_custom_call" | custom-call | tf_op jit(solution)/shard_map/lists/pallas_call | solution.py:138
  33.1 0.0 collective-permute-done.1.above
  33.1 2.9 %collective-permute-done.below = f32[112,128]{1,0:T(8,128)S(1)} collective-permute-done((f32[112,128]{1,0:T(8,128)S(1)}, f32[112,128]{1,0:T(8,128)S(1)}, u32[]{:S(2)}, u32[]{:S(2)}) %collective-permute-start) | collective-permute-done | bytes 57376 | tf_op jit(solution)/shard_map/ppermute | solution.py:669
  36.0 5.9 %product.1 = (f32[8,128]{1,0:T(8,128)S(1)}, f32[32,16,128]{2,1,0:T(8,128)S(1)}) custom-call(f32[3,8,128]{2,1,0:T(8,128)S(1)} %get-tuple-element.35.tiles, f32[112,128]{1,0:T(8,128)S(1)} %collective-permute-done.below, f32[112,128]{1,0:T(8,128)S(1)} %collective-permute-done.1.above, s32[128,128]{1,0:T(8,128)S(1)} %get-tuple-element.37.ids_t, ...), custom_call_target="tpu_custom_call" | custom-call | tf_op jit(solution)/shard_map/product/pallas_call | solution.py:394
  41.8 14.0 %all_to_all.20.got = f32[32,16,128]{2,1,0:T(8,128)S(1)} all-to-all(f32[32,16,128]{2,1,0:T(8,128)S(1)} %get-tuple-element.50), channel_id=1, replica_groups=mesh['gx'=4,'gy'=8,'gz'=16] {'gx','gy'}, dimensions={0} | all-to-all | bytes 524288 | tf_op jit(solution)/shard_map/all_to_all | solution.py:660
  55.8 1.4 %fold.1 = f32[16,16,128]{2,1,0:T(8,128)S(1)} custom-call(f32[8,128]{1,0:T(8,128)S(1)} %get-tuple-element.49.own, f32[32,16,128]{2,1,0:T(8,128)S(1)} %all_to_all.20.got, f32[32,8,128]{2,1,0:T(8,128)S(1)} %all-to-all-done.got.maps, f32[112,128]{1,0:T(8,128)S(1)} %collective-permute-done.below, f32[112,128]{1,0:T(8,128)S(1)} %collective-permute-done.1.above, ...), custom_call_target="tpu_custom_call" | custom-call | tf_op jit(solution)/shard_map/fold/pallas_call | solution.py:572
  57.2 17.4 %all_to_all.21.got = f32[16,16,128]{2,1,0:T(8,128)S(1)} all-to-all(f32[16,16,128]{2,1,0:T(8,128)S(1)} %fold.1), channel_id=1, replica_groups=mesh['gx'=4,'gy'=8,'gz'=16] {'gz'}, dimensions={0} | all-to-all | bytes 262144 | tf_op jit(solution)/shard_map/all_to_all | solution.py:672
  74.7 0.1 column.1
  74.8 13.9 %all_to_all.22.got = f32[32,8,128]{2,1,0:T(8,128)S(1)} all-to-all(f32[32,8,128]{2,1,0:T(8,128)S(1)} %get-tuple-element.52), channel_id=1, replica_groups=mesh['gx'=4,'gy'=8,'gz'=16] {'gx','gy'}, dimensions={0} | all-to-all | bytes 262144 | tf_op jit(solution)/shard_map/all_to_all | solution.py:660
  88.7 0.9 finish.1
Async XLA Ops:
  2.1 18.1 %all-to-all-start = ((f32[32,8,128]{2,1,0:T(8,128)}), f32[32,8,128]{2,1,0:T(8,128)S(1)}, u32[]{:S(2)}, u32[]{:S(2)}) async-start(f32[32,8,128]{2,1,0:T(8,128)} %pack.1), calls=%async_computation | async-start | bytes 262144 | tf_op jit(solution)/shard_map/all_to_all | solution.py:660
  20.6 12.5 %collective-permute-start.1 = (f32[112,128]{1,0:T(8,128)S(1)}, f32[112,128]{1,0:T(8,128)S(1)}, u32[]{:S(2)}, u32[]{:S(2)}) collective-permute-start(f32[112,128]{1,0:T(8,128)S(1)} %get-tuple-element.36), channel_id=1, source_target_pairs={{1,0},{2,1},{3,2},{4,3},{5,4},{6,5},{7,6},{8,7},{9,8},{10,9},{11,1... | collective-permute-start | bytes 172040 | tf_op jit(solution)/shard_map/ppermute | solution.py:669
  29.8 6.1 %collective-permute-start = (f32[112,128]{1,0:T(8,128)S(1)}, f32[112,128]{1,0:T(8,128)S(1)}, u32[]{:S(2)}, u32[]{:S(2)}) collective-permute-start(f32[112,128]{1,0:T(8,128)S(1)} %get-tuple-element.36), channel_id=1, source_target_pairs={{0,1},{1,2},{2,3},{3,4},{4,5},{5,6},{6,7},{7,8},{8,9},{9,10},{10,1... | collective-permute-start | bytes 172040 | tf_op jit(solution)/shard_map/ppermute | solution.py:669
